TPU v7x, 32 devices: a whole 2x2x4 slice. The times are simulated.
32 devices in a mesh: section: 2 (over core), dp: 4 (over z), tensor: 4 (over y, x).
Axes of the slice: x: 2, y: 2, z: 4, core: 2. Of those that a mesh axis runs over, the one named last changes fastest.
Arguments:
- inputs: bfloat16 [2, 4, 2048, 768], P(None, 'dp', 'tensor'), may hold values from -6 to 6
- cotangent: bfloat16 [2, 4, 2048, 768], P(None, 'dp', 'tensor'), may hold values from -6 to 6
- segments: int32 [2, 4, 2048], P(None, 'dp'), may hold values from 0 to 3, never falling along the last dimension, each value on 1 to 1024 neighbouring positions
- live_blocks: int32 [2, 4], P(None, 'dp'), may hold values from 8 to 16
- ln1_gain: bfloat16 [2, 768], P('section', ('dp', 'tensor')), may hold values from 0.25 to 1.75
- ln1_bias: bfloat16 [2, 768], P('section', ('dp', 'tensor')), may hold values from -3 to 3
- qkv_weight: bfloat16 [2, 768, 2304], P('section', 'dp', 'tensor'), may hold values from -0.21875 to 0.21875
- qkv_bias: bfloat16 [2, 12, 192], P('section', 'tensor', 'dp'), may hold values from -2 to 2
- out_weight: bfloat16 [2, 768, 768], P('section', 'tensor', 'dp'), may hold values from -0.875 to 0.875
- out_bias: bfloat16 [2, 768], P('section', ('dp', 'tensor')), may hold values from -3 to 3
- ln2_gain: bfloat16 [2, 768], P('section', ('dp', 'tensor')), may hold values from 0.25 to 1.75
- ln2_bias: bfloat16 [2, 768], P('section', ('dp', 'tensor')), may hold values from -3 to 3
- fc1_weight: bfloat16 [2, 768, 3072], P('section', 'dp', 'tensor'), may hold values from -0.21875 to 0.21875
- fc1_bias: bfloat16 [2, 12, 256], P('section', 'tensor', 'dp'), may hold values from -3 to 3
- fc2_weight: bfloat16 [2, 3072, 768], P('section', 'tensor', 'dp'), may hold values from -0.109375 to 0.109375
- fc2_bias: bfloat16 [2, 768], P('section', ('dp', 'tensor')), may hold values from -3 to 3
Outputs:
- section_outputs: bfloat16 [2, 2, 4, 2048, 768], P('section', None, 'dp', 'tensor')
- input_grads: bfloat16 [2, 2, 4, 2048, 768], P('section', None, 'dp', 'tensor')
- ln1_gain_grad: float32 [2, 768], P('section', ('dp', 'tensor'))
- ln1_bias_grad: float32 [2, 768], P('section', ('dp', 'tensor'))
- qkv_weight_grad: float32 [2, 768, 2304], P('section', 'dp', 'tensor')
- qkv_bias_grad: float32 [2, 12, 192], P('section', 'tensor', 'dp')
- out_weight_grad: float32 [2, 768, 768], P('section', 'tensor', 'dp')
- out_bias_grad: float32 [2, 768], P('section', ('dp', 'tensor'))
- ln2_gain_grad: float32 [2, 768], P('section', ('dp', 'tensor'))
- ln2_bias_grad: float32 [2, 768], P('section', ('dp', 'tensor'))
- fc1_weight_grad: float32 [2, 768, 3072], P('section', 'dp', 'tensor')
- fc1_bias_grad: float32 [2, 12, 256], P('section', 'tensor', 'dp')
- fc2_weight_grad: float32 [2, 3072, 768], P('section', 'tensor', 'dp')
- fc2_bias_grad: float32 [2, 768], P('section', ('dp', 'tensor'))
Inputs may be any that keep to these rules, and one draw needn't show every extreme that they name: `segments`: within a row the document numbers never fall; a document holds 1 to 1024 tokens.
All inputs are finite; a program needn't handle non-finite values.
Results may differ from a plain program's by a relative error of at most 0.018.
Values may be sent and summed in bfloat16 or wider, within the bound.
A program may use at most 256 MiB of HBM per device.

v0:
```python
import jax
import jax.numpy as jnp
from jax import lax
from jax.sharding import PartitionSpec as P

HEAD_DIM = 64
ROTARY = 16
BLOCK = 128
QBLOCK = 512


EPS = 1e-05
NEGATIVE = -1e30


def shifted(value, axis, steps):
    count = lax.axis_size(axis)
    initial, last = (max(0, -steps), min(count, count - steps))
    return lax.ppermute(value, axis, [(source, source + steps) for source in range(initial, last)])


def normalize_rows(values):
    average = jnp.mean(values, axis=-1, keepdims=True)
    centered = values - average
    spread = jnp.mean(centered * centered, axis=-1, keepdims=True)
    scaling = lax.rsqrt(spread + EPS)
    return (centered * scaling, scaling)


def norm_back(downward, unit_rows, scaling, gain):
    gain_grad = jnp.sum(downward * unit_rows, axis=0)
    bias_grad = jnp.sum(downward, axis=0)
    unit_grad = downward * gain
    return (scaling * center_back(unit_grad, unit_rows), gain_grad, bias_grad)


def center_back(unit_grad, unit_rows):
    return (
        unit_grad
        - jnp.mean(unit_grad, axis=-1, keepdims=True)
        - unit_rows * jnp.mean(unit_grad * unit_rows, axis=-1, keepdims=True)
    )


def positions_of(segment):
    counter = jnp.arange(segment.shape[0], dtype=jnp.int32)
    starts = jnp.concatenate([jnp.ones((1,), dtype=bool), segment[1:] != segment[:-1]])
    doc_start = lax.cummax(jnp.where(starts, counter, 0), axis=0)
    return counter - doc_start


def rotary_tables(segment):
    positions = positions_of(segment).astype(jnp.float32)
    frequency = 10000.0 ** (-(jnp.arange(ROTARY // 2, dtype=jnp.float32) * (2.0 / ROTARY)))
    angles = positions[:, None] * frequency[None, :]
    angles = jnp.concatenate([angles, angles], axis=-1)
    return (jnp.cos(angles)[:, None, :], jnp.sin(angles)[:, None, :])


def rotate(values, cosines, sines):
    half_width = ROTARY // 2
    rotated_part = values[..., :ROTARY]
    swapped = jnp.concatenate(
        [-rotated_part[..., half_width:], rotated_part[..., :half_width]], axis=-1
    )
    return jnp.concatenate(
        [rotated_part * cosines + swapped * sines, values[..., ROTARY:]], axis=-1
    )


def rotate_back(grads_in, cosines, sines):
    half_width = ROTARY // 2
    rotated_part = grads_in[..., :ROTARY]
    moved = rotated_part * sines
    turned = jnp.concatenate([moved[..., half_width:], -moved[..., :half_width]], axis=-1)
    return jnp.concatenate([rotated_part * cosines + turned, grads_in[..., ROTARY:]], axis=-1)


def allowed_block(segment, live_count, offset, count):
    query_index = offset + jnp.arange(count, dtype=jnp.int32)
    key_index = jnp.arange(segment.shape[0], dtype=jnp.int32)
    query_docs = lax.dynamic_slice_in_dim(segment, offset, count)
    same_doc = query_docs[:, None] == segment[None, :]
    causal = key_index[None, :] <= query_index[:, None]
    present = (key_index < live_count * BLOCK)[None, :] | (
        key_index[None, :] == query_index[:, None]
    )
    return same_doc & causal & present


def times_transposed(left_rows, right_rows):
    return lax.dot_general(
        left_rows, right_rows, (((1,), (1,)), ((), ())), preferred_element_type=jnp.float32
    )


def rows_product(left_rows, right_rows):
    return lax.dot_general(
        left_rows, right_rows, (((0,), (0,)), ((), ())), preferred_element_type=jnp.float32
    )


def attend(query_rows, key_rows, value_rows, segment, live_count):
    rows_total = query_rows.shape[0]
    blocks = rows_total // QBLOCK
    pieces = query_rows.reshape(blocks, QBLOCK, query_rows.shape[1], query_rows.shape[2])
    starts = jnp.arange(blocks, dtype=jnp.int32) * QBLOCK

    def one_block(element):
        block_rows, offset = element
        scores = (
            jnp.einsum("qhd,khd->hqk", block_rows, key_rows, preferred_element_type=jnp.float32)
            * 0.125
        )
        scores = jnp.where(
            allowed_block(segment, live_count, offset, QBLOCK)[None], scores, NEGATIVE
        )
        row_max = jnp.max(scores, axis=-1, keepdims=True)
        weights = jnp.exp(scores - row_max)
        denominator = jnp.sum(weights, axis=-1, keepdims=True)
        probability = (weights / denominator).astype(jnp.bfloat16)
        attended_block = jnp.einsum(
            "hqk,khd->qhd", probability, value_rows, preferred_element_type=jnp.float32
        )
        return (attended_block, (row_max + jnp.log(denominator))[..., 0])

    attended, log_sums = lax.map(one_block, (pieces, starts))
    return (attended.reshape(rows_total, -1), log_sums)


def attend_back(query_rows, key_rows, value_rows, log_sums, output_grad, segment, live_count):
    rows_total, head_count, features = query_rows.shape
    blocks = rows_total // QBLOCK
    pieces = query_rows.reshape(blocks, QBLOCK, head_count, features)
    grad_blocks = output_grad.reshape(blocks, QBLOCK, head_count, features)
    starts = jnp.arange(blocks, dtype=jnp.int32) * QBLOCK

    def one_block(carried, element):
        key_grad, value_grad = carried
        block_rows, grad_rows_block, block_sums, offset = element
        scores = (
            jnp.einsum("qhd,khd->hqk", block_rows, key_rows, preferred_element_type=jnp.float32)
            * 0.125
        )
        scores = jnp.where(
            allowed_block(segment, live_count, offset, QBLOCK)[None], scores, NEGATIVE
        )
        probability = jnp.exp(scores - block_sums[..., None])
        prob_grad = jnp.einsum(
            "qhd,khd->hqk", grad_rows_block, value_rows, preferred_element_type=jnp.float32
        )
        row_dot = jnp.sum(probability * prob_grad, axis=-1, keepdims=True)
        score_grad = (probability * (prob_grad - row_dot)).astype(jnp.bfloat16)
        query_grad = (
            jnp.einsum("hqk,khd->qhd", score_grad, key_rows, preferred_element_type=jnp.float32)
            * 0.125
        )
        key_grad = (
            key_grad
            + jnp.einsum("hqk,qhd->khd", score_grad, block_rows, preferred_element_type=jnp.float32)
            * 0.125
        )
        value_grad = value_grad + jnp.einsum(
            "hqk,qhd->khd",
            probability.astype(jnp.bfloat16),
            grad_rows_block,
            preferred_element_type=jnp.float32,
        )
        return ((key_grad, value_grad), query_grad)

    blank_grads = jnp.zeros(key_rows.shape, jnp.float32)
    (key_grad, value_grad), query_grad = lax.scan(
        one_block, (blank_grads, blank_grads), (pieces, grad_blocks, log_sums, starts)
    )
    return (query_grad.reshape(rows_total, head_count, features), key_grad, value_grad)


def forward_layer(values, weights, vectors, segment, live_count):
    mix_weight, mix_bias, out_matrix, up_matrix, up_bias, down_matrix = weights
    gain_first, bias_first, out_shift, gain_second, bias_second, down_shift = vectors
    source = values.astype(jnp.float32)
    unit_rows, scaling = normalize_rows(source)
    normed_first = (unit_rows * gain_first + bias_first).astype(jnp.bfloat16)
    normed_second = (unit_rows * gain_second + bias_second).astype(jnp.bfloat16)
    whole_first, whole_second = (
        lax.all_gather(normed_first, "tensor", axis=0, tiled=True),
        lax.all_gather(normed_second, "tensor", axis=0, tiled=True),
    )
    rows_total = whole_first.shape[0]
    projected = jnp.dot(
        whole_first, mix_weight, preferred_element_type=jnp.float32
    ) + mix_bias.reshape(-1).astype(jnp.float32)
    projected = projected.reshape(rows_total, -1, 3 * HEAD_DIM)
    cosines, sines = rotary_tables(segment)
    query_rows = rotate(projected[..., :HEAD_DIM], cosines, sines).astype(jnp.bfloat16)
    key_rows = rotate(projected[..., HEAD_DIM : 2 * HEAD_DIM], cosines, sines).astype(jnp.bfloat16)
    value_rows = projected[..., 2 * HEAD_DIM :].astype(jnp.bfloat16)
    attended, log_sums = attend(query_rows, key_rows, value_rows, segment, live_count)
    attended = attended.astype(jnp.bfloat16)
    hidden = jnp.dot(whole_second, up_matrix, preferred_element_type=jnp.float32) + up_bias.reshape(
        -1
    ).astype(jnp.float32)
    active = jax.nn.gelu(hidden, approximate=False).astype(jnp.bfloat16)
    partial_value = jnp.dot(attended, out_matrix, preferred_element_type=jnp.float32) + jnp.dot(
        active, down_matrix, preferred_element_type=jnp.float32
    )
    summed = lax.psum_scatter(
        partial_value.astype(jnp.bfloat16), "tensor", scatter_dimension=0, tiled=True
    ).astype(jnp.float32)
    result = (source + summed + out_shift + down_shift).astype(jnp.bfloat16)
    stored = (
        unit_rows,
        scaling,
        whole_first,
        whole_second,
        query_rows,
        key_rows,
        value_rows,
        log_sums,
        attended,
        hidden,
        active,
        segment,
        live_count,
    )
    return (result, stored)


def backward_layer(downward, weights, vectors, stored):
    mix_weight, mix_bias, out_matrix, up_matrix, up_bias, down_matrix = weights
    gain_first, bias_first, out_shift, gain_second, bias_second, down_shift = vectors
    (
        unit_rows,
        scaling,
        whole_first,
        whole_second,
        query_rows,
        key_rows,
        value_rows,
        log_sums,
        attended,
        hidden,
        active,
        segment,
        live_count,
    ) = stored
    residual_grad = downward.astype(jnp.float32)
    whole_grad = lax.all_gather(downward, "tensor", axis=0, tiled=True)
    rows_total = whole_grad.shape[0]
    out_grad = rows_product(attended, whole_grad)
    down_grad = rows_product(active, whole_grad)
    active_grad = times_transposed(whole_grad, down_matrix)
    gelu_pull = jax.vjp(lambda inner: jax.nn.gelu(inner, approximate=False), hidden)[1]
    hidden_grad = gelu_pull(active_grad)[0].astype(jnp.bfloat16)
    attended_grad = (
        times_transposed(whole_grad, out_matrix).astype(jnp.bfloat16).reshape(query_rows.shape)
    )
    cosines, sines = rotary_tables(segment)
    query_grad, key_grad, value_grad = attend_back(
        query_rows, key_rows, value_rows, log_sums, attended_grad, segment, live_count
    )
    mixed_grad = jnp.concatenate(
        [
            rotate_back(query_grad, cosines, sines),
            rotate_back(key_grad, cosines, sines),
            value_grad,
        ],
        axis=-1,
    )
    mixed_grad = mixed_grad.reshape(rows_total, -1).astype(jnp.bfloat16)
    mix_grad = rows_product(whole_first, mixed_grad)
    mix_bias_grad = jnp.sum(mixed_grad.astype(jnp.float32), axis=0).reshape(mix_bias.shape)
    up_grad = rows_product(whole_second, hidden_grad)
    up_bias_grad = jnp.sum(hidden_grad.astype(jnp.float32), axis=0).reshape(up_bias.shape)
    first_part = times_transposed(mixed_grad, mix_weight)
    second_part = times_transposed(hidden_grad, up_matrix)
    partial_value = jnp.concatenate([first_part, second_part], axis=1)
    summed = lax.psum_scatter(
        partial_value.astype(jnp.bfloat16), "tensor", scatter_dimension=0, tiled=True
    ).astype(jnp.float32)
    features = downward.shape[1]
    back_first, gain_first_grad, bias_first_grad = norm_back(
        summed[:, :features], unit_rows, scaling, gain_first
    )
    back_second, gain_second_grad, bias_second_grad = norm_back(
        summed[:, features:], unit_rows, scaling, gain_second
    )
    source_grad = residual_grad + back_first + back_second
    column_sums = jnp.sum(residual_grad, axis=0)
    matrices = (mix_grad, mix_bias_grad, out_grad, up_grad, up_bias_grad, down_grad)
    vector_grads = (
        gain_first_grad,
        bias_first_grad,
        column_sums,
        gain_second_grad,
        bias_second_grad,
        column_sums,
    )
    return (source_grad.astype(jnp.bfloat16), matrices, vector_grads)


def shards(
    inputs,
    cotangent,
    segments,
    live_blocks,
    ln1_gain,
    ln1_bias,
    qkv_weight,
    qkv_bias,
    out_weight,
    out_bias,
    ln2_gain,
    ln2_bias,
    fc1_weight,
    fc1_bias,
    fc2_weight,
    fc2_bias,
):
    micro_count = inputs.shape[0]
    first_section = lax.axis_index("section") == 0
    gathered = (
        lax.all_gather(ln1_gain[0], ("dp", "tensor"), axis=0, tiled=True),
        lax.all_gather(ln1_bias[0], ("dp", "tensor"), axis=0, tiled=True),
        lax.all_gather(out_bias[0], ("dp", "tensor"), axis=0, tiled=True),
        lax.all_gather(ln2_gain[0], ("dp", "tensor"), axis=0, tiled=True),
        lax.all_gather(ln2_bias[0], ("dp", "tensor"), axis=0, tiled=True),
        lax.all_gather(fc2_bias[0], ("dp", "tensor"), axis=0, tiled=True),
    )
    vectors = tuple((vector.astype(jnp.float32) for vector in gathered))

    def weights_now():
        return (
            lax.all_gather(qkv_weight[0], "dp", axis=0, tiled=True),
            lax.all_gather(qkv_bias[0], "dp", axis=1, tiled=True),
            lax.all_gather(out_weight[0], "dp", axis=1, tiled=True),
            lax.all_gather(fc1_weight[0], "dp", axis=0, tiled=True),
            lax.all_gather(fc1_bias[0], "dp", axis=1, tiled=True),
            lax.all_gather(fc2_weight[0], "dp", axis=1, tiled=True),
        )

    incoming = jnp.zeros(inputs.shape[2:], jnp.bfloat16)
    results = []
    states = []
    for turn_index in range(micro_count + 1):
        first_pick = min(turn_index, micro_count - 1)
        second_pick = max(turn_index - 1, 0)
        values = jnp.where(first_section, inputs[first_pick, 0], incoming)
        segment = jnp.where(first_section, segments[first_pick, 0], segments[second_pick, 0])
        live_count = jnp.where(
            first_section, live_blocks[first_pick, 0], live_blocks[second_pick, 0]
        )
        result, stored = forward_layer(values, weights_now(), vectors, segment, live_count)
        results.append(result)
        states.append(stored)
        if turn_index < micro_count:
            incoming = shifted(result, "section", 1)
    coming = jnp.zeros(inputs.shape[2:], jnp.bfloat16)
    back_rows = []
    matrix_totals = None
    vector_totals = None
    for turn_index in range(micro_count + 1):
        lower_state = states[max(turn_index - 1, 0)]
        upper_state = states[min(turn_index + 1, micro_count)]
        stored = jax.tree.map(
            lambda former, latter: jnp.where(first_section, former, latter),
            lower_state,
            upper_state,
        )
        if turn_index < micro_count:
            upstream = cotangent[turn_index, 0]
        else:
            upstream = jnp.zeros_like(coming)
        downward = jnp.where(first_section, coming, upstream)
        source_grad, matrices, vector_grads = backward_layer(
            downward, weights_now(), vectors, stored
        )
        back_rows.append(source_grad)
        matrices = (
            lax.psum_scatter(
                matrices[0].astype(jnp.bfloat16), "dp", scatter_dimension=0, tiled=True
            ).astype(jnp.float32),
            lax.psum_scatter(
                matrices[1].astype(jnp.bfloat16), "dp", scatter_dimension=1, tiled=True
            ).astype(jnp.float32),
            lax.psum_scatter(
                matrices[2].astype(jnp.bfloat16), "dp", scatter_dimension=1, tiled=True
            ).astype(jnp.float32),
            lax.psum_scatter(
                matrices[3].astype(jnp.bfloat16), "dp", scatter_dimension=0, tiled=True
            ).astype(jnp.float32),
            lax.psum_scatter(
                matrices[4].astype(jnp.bfloat16), "dp", scatter_dimension=1, tiled=True
            ).astype(jnp.float32),
            lax.psum_scatter(
                matrices[5].astype(jnp.bfloat16), "dp", scatter_dimension=1, tiled=True
            ).astype(jnp.float32),
        )
        if matrix_totals is None:
            matrix_totals = matrices
            vector_totals = vector_grads
        else:
            matrix_totals = tuple(
                (running + adding for running, adding in zip(matrix_totals, matrices))
            )
            vector_totals = tuple(
                (running + adding for running, adding in zip(vector_totals, vector_grads))
            )
        if turn_index < micro_count:
            coming = shifted(source_grad, "section", -1)
    vector_totals = (
        lax.psum_scatter(vector_totals[0], ("dp", "tensor"), scatter_dimension=0, tiled=True),
        lax.psum_scatter(vector_totals[1], ("dp", "tensor"), scatter_dimension=0, tiled=True),
        lax.psum_scatter(vector_totals[2], ("dp", "tensor"), scatter_dimension=0, tiled=True),
        lax.psum_scatter(vector_totals[3], ("dp", "tensor"), scatter_dimension=0, tiled=True),
        lax.psum_scatter(vector_totals[4], ("dp", "tensor"), scatter_dimension=0, tiled=True),
        lax.psum_scatter(vector_totals[5], ("dp", "tensor"), scatter_dimension=0, tiled=True),
    )
    forward_rows = jnp.stack(
        [
            jnp.where(first_section, results[batch_index], results[batch_index + 1])
            for batch_index in range(micro_count)
        ]
    )
    backward_rows = jnp.stack(
        [
            jnp.where(first_section, back_rows[batch_index + 1], back_rows[batch_index])
            for batch_index in range(micro_count)
        ]
    )
    section_outputs = forward_rows[None, :, None]
    input_grads = backward_rows[None, :, None]
    return (
        section_outputs,
        input_grads,
        vector_totals[0][None],
        vector_totals[1][None],
        matrix_totals[0][None],
        matrix_totals[1][None],
        matrix_totals[2][None],
        vector_totals[2][None],
        vector_totals[3][None],
        vector_totals[4][None],
        matrix_totals[3][None],
        matrix_totals[4][None],
        matrix_totals[5][None],
        vector_totals[5][None],
    )


def solution(mesh):
    in_specs = (
        P(None, "dp", "tensor", None),
        P(None, "dp", "tensor", None),
        P(None, "dp", None),
        P(None, "dp"),
        P("section", ("dp", "tensor")),
        P("section", ("dp", "tensor")),
        P("section", "dp", "tensor"),
        P("section", "tensor", "dp"),
        P("section", "tensor", "dp"),
        P("section", ("dp", "tensor")),
        P("section", ("dp", "tensor")),
        P("section", ("dp", "tensor")),
        P("section", "dp", "tensor"),
        P("section", "tensor", "dp"),
        P("section", "tensor", "dp"),
        P("section", ("dp", "tensor")),
    )
    out_specs = (
        P("section", None, "dp", "tensor", None),
        P("section", None, "dp", "tensor", None),
        P("section", ("dp", "tensor")),
        P("section", ("dp", "tensor")),
        P("section", "dp", "tensor"),
        P("section", "tensor", "dp"),
        P("section", "tensor", "dp"),
        P("section", ("dp", "tensor")),
        P("section", ("dp", "tensor")),
        P("section", ("dp", "tensor")),
        P("section", "dp", "tensor"),
        P("section", "tensor", "dp"),
        P("section", "tensor", "dp"),
        P("section", ("dp", "tensor")),
    )
    return jax.shard_map(shards, mesh=mesh, in_specs=in_specs, out_specs=out_specs, check_vma=False)
```

profile of v0, /device:TPU:0, one launch (start us, length us, event | category | flops | bytes accessed | tf_op | source)
XLA Modules:
  0.0 2312.8 jit_solution(13576138527376660457)
XLA Ops:
  17.3 78.6 %all-reduce.12 = (bf16[768]{0:T(1024)(128)(2,1)S(1)}, bf16[768]{0:T(1024)(128)(2,1)S(1)}, bf16[768]{0:T(1024)(128)(2,1)S(1)}, bf16[768]{0:T(1024)(128)(2,1)S(1)}...) all-reduce(bf16[768]{0:T(1024)(128)(2,1)S(1)} %dynamic-update-slice, ...), channel_id=8, replica_groups=mesh['section'=2,'dp'=4,'tensor'=4] {'dp','tensor'}, use_global_device_ids=true, to_apply=%add.3 | all-reduce | flops 4608 | bytes 18432
  187.0 106.4 %while.93 = (s32[]{:T(128)}, bf16[4,512,3,64]{1,3,2,0:T(8,128)(2,1)S(1)}, f32[4,3,512]{2,1,0:T(4,128)S(1)}, s32[4]{0:T(128)S(1)}, s32[2048]{0:T(1024)S(1)}, /*in...) while((s32[]{:T(128)}, ...), condition=%wide.region_7.8_spmd, body=%wide.region_4.7_spmd.sunk | while | flops 849347584 | bytes 44187836 | solution.py:127
  321.2 40.6 %reduce-scatter.43.cloned.1.call-done = bf16[512,768]{1,0:T(8,128)(2,1)} async-done(((bf16[2048,768]{1,0:T(8,128)(2,1)}), bf16[512,768]{1,0:T(8,128)(2,1)}) %reduce-scatter.43.cloned.1.call-update) | async-done | bytes 786448 | tf_op jit(solution)/shard_map/reduce_scatter | solution.py:207
  371.4 42.3 %all-gather.29.cloned.1.call-done = bf16[2048,768]{1,0:T(8,128)(2,1)} async-done(((bf16[512,768]{1,0:T(8,128)(2,1)}), bf16[2048,768]{1,0:T(8,128)(2,1)}) %all-gather.29.cloned.1.call-update) | async-done | bytes 3145744 | tf_op jit(solution)/shard_map/all_gather | solution.py:186
  420.5 106.3 %while.94 = (s32[]{:T(128)}, bf16[4,512,3,64]{1,3,2,0:T(8,128)(2,1)S(1)}, f32[4,3,512]{2,1,0:T(4,128)S(1)}, s32[4]{0:T(128)S(1)}, s32[2048]{0:T(1024)S(1)}, /*in...) while((s32[]{:T(128)}, ...), condition=%wide.region_16.17_spmd, body=%wide.region_13.16_spmd.sunk | while | flops 849347584 | bytes 44187836 | solution.py:127
  556.4 40.0 %reduce-scatter.45.cloned.1.call-done = bf16[512,768]{1,0:T(8,128)(2,1)} async-done(((bf16[2048,768]{1,0:T(8,128)(2,1)}), bf16[512,768]{1,0:T(8,128)(2,1)}) %reduce-scatter.45.cloned.1.call-update) | async-done | bytes 786448 | tf_op jit(solution)/shard_map/reduce_scatter | solution.py:207
  604.3 37.7 %all-gather.45.cloned.1.call-done = bf16[1,1,2048,768]{3,2,1,0:T(8,128)(2,1)} async-done(((bf16[1,1,512,768]{3,2,1,0:T(8,128)(2,1)}), bf16[1,1,2048,768]{3,2,1,0:T(8,128)(2,1)}) %all-gather.45.cloned.1.call-update) | async-done | bytes 3145744 | tf_op jit(solution)/shard_map/all_gather | solution.py:248
  708.6 105.8 %while.95 = (s32[]{:T(128)}, bf16[4,512,3,64]{1,3,2,0:T(8,128)(2,1)S(1)}, f32[4,3,512]{2,1,0:T(4,128)S(1)}, s32[4]{0:T(128)S(1)}, s32[2048]{0:T(1024)S(1)}, /*in...) while((s32[]{:T(128)}, ...), condition=%wide.region_25.26_spmd, body=%wide.region_22.25_spmd.sunk | while | flops 849347584 | bytes 44187836 | solution.py:127
  816.6 211.6 %while.96 = (s32[]{:T(128)}, f32[2048,3,64]{0,2,1:T(8,128)}, f32[2048,3,64]{0,2,1:T(8,128)}, f32[4,512,3,64]{1,0,3,2:T(4,128)}, bf16[4,512,3,64]{1,3,2,0:T(8,128...) while((s32[]{:T(128)}, f32[2048,3,64]{0,2,1:T(8,128)}, ...), condition=%wide.region_29.30_spmd.clone, body=%wide.region_27.29_spmd.clone.sunk | while | flops 2068808704 | bytes 177146192 | solution.py:172
  1042.0 69.5 %reduce-scatter.49.cloned.1.call-done = bf16[512,1536]{1,0:T(8,128)(2,1)} async-done(((bf16[2048,1536]{1,0:T(8,128)(2,1)}), bf16[512,1536]{1,0:T(8,128)(2,1)}) %reduce-scatter.49.cloned.1.call-update) | async-done | bytes 1572880 | tf_op jit(solution)/shard_map/reduce_scatter | solution.py:278
  1126.1 31.0 %all-gather.35.cloned.1.call-done = bf16[2048,768]{1,0:T(8,128)(2,1)} async-done(((bf16[512,768]{1,0:T(8,128)(2,1)}), bf16[2048,768]{1,0:T(8,128)(2,1)}) %all-gather.35.cloned.1.call-update) | async-done | bytes 3145744 | tf_op jit(solution)/shard_map/all_gather | solution.py:187
  1175.1 27.7 %all-gather.37.cloned.1.call-done = bf16[2048,768]{1,0:T(8,128)(2,1)} async-done(((bf16[512,768]{1,0:T(8,128)(2,1)}), bf16[2048,768]{1,0:T(8,128)(2,1)}) %all-gather.37.cloned.1.call-update) | async-done | bytes 3145744 | tf_op jit(solution)/shard_map/all_gather | solution.py:248
  1208.9 214.4 %while.97 = (s32[]{:T(128)}, f32[2048,3,64]{0,2,1:T(8,128)}, f32[2048,3,64]{0,2,1:T(8,128)}, f32[4,512,3,64]{1,0,3,2:T(4,128)}, bf16[4,512,3,64]{1,3,2,0:T(8,128...) while((s32[]{:T(128)}, f32[2048,3,64]{0,2,1:T(8,128)}, ...), condition=%wide.region_39.40_spmd.clone, body=%wide.region_37.39_spmd.clone.sunk | while | flops 2068808704 | bytes 177146192 | solution.py:172
  1458.7 70.1 %reduce-scatter.51.cloned.1.call-done = bf16[512,1536]{1,0:T(8,128)(2,1)} async-done(((bf16[2048,1536]{1,0:T(8,128)(2,1)}), bf16[512,1536]{1,0:T(8,128)(2,1)}) %reduce-scatter.51.cloned.1.call-update) | async-done | bytes 1572880 | tf_op jit(solution)/shard_map/reduce_scatter | solution.py:278
  1592.3 215.2 %while.98 = (s32[]{:T(128)}, f32[2048,3,64]{0,2,1:T(8,128)}, f32[2048,3,64]{0,2,1:T(8,128)}, f32[4,512,3,64]{1,0,3,2:T(4,128)}, bf16[4,512,3,64]{1,3,2,0:T(8,128...) while((s32[]{:T(128)}, f32[2048,3,64]{0,2,1:T(8,128)}, ...), condition=%wide.region_49.50_spmd.clone, body=%wide.region_47.49_spmd.clone.sunk | while | flops 2068808704 | bytes 177146192 | solution.py:172
  1936.8 27.2 %reduce-scatter.59.cloned.1.call-done = bf16[192,576]{1,0:T(8,128)(2,1)} async-done(((bf16[768,576]{1,0:T(8,128)(2,1)}), bf16[192,576]{1,0:T(8,128)(2,1)}) %reduce-scatter.59.cloned.1.call-update) | async-done | bytes 221200 | tf_op jit(solution)/shard_map/reduce_scatter | solution.py:380
  1966.1 28.1 %reduce-scatter.67.cloned.1.call-done = bf16[768,192]{0,1:T(8,128)(2,1)} async-done(((bf16[768,768]{0,1:T(8,128)(2,1)}), bf16[768,192]{0,1:T(8,128)(2,1)}) %reduce-scatter.67.cloned.1.call-update) | async-done | bytes 294928 | tf_op jit(solution)/shard_map/reduce_scatter | solution.py:395
  1994.2 30.1 %reduce-scatter.69.cloned.1.call-done = bf16[768,192]{0,1:T(8,128)(2,1)} async-done(((bf16[768,768]{0,1:T(8,128)(2,1)}), bf16[768,192]{0,1:T(8,128)(2,1)}) %reduce-scatter.69.cloned.1.call-update) | async-done | bytes 294928 | tf_op jit(solution)/shard_map/reduce_scatter | solution.py:395
  2024.3 30.3 %reduce-scatter.71.cloned.1.call-done = bf16[768,192]{0,1:T(8,128)(2,1)} async-done(((bf16[768,768]{0,1:T(8,128)(2,1)}), bf16[768,192]{0,1:T(8,128)(2,1)}) %reduce-scatter.71.cloned.1.call-update) | async-done | bytes 294928 | tf_op jit(solution)/shard_map/reduce_scatter | solution.py:395
  2056.7 28.2 %reduce-scatter.61.cloned.1.call-done = bf16[192,768]{1,0:T(8,128)(2,1)} async-done(((bf16[768,768]{1,0:T(8,128)(2,1)}), bf16[192,768]{1,0:T(8,128)(2,1)}) %reduce-scatter.61.cloned.1.call-update) | async-done | bytes 294928 | tf_op jit(solution)/shard_map/reduce_scatter | solution.py:389
  2084.9 30.1 %reduce-scatter.63.cloned.1.call-done = bf16[192,768]{1,0:T(8,128)(2,1)} async-done(((bf16[768,768]{1,0:T(8,128)(2,1)}), bf16[192,768]{1,0:T(8,128)(2,1)}) %reduce-scatter.63.cloned.1.call-update) | async-done | bytes 294928 | tf_op jit(solution)/shard_map/reduce_scatter | solution.py:389
  2115.0 30.9 %reduce-scatter.65.cloned.1.call-done = bf16[192,768]{1,0:T(8,128)(2,1)} async-done(((bf16[768,768]{1,0:T(8,128)(2,1)}), bf16[192,768]{1,0:T(8,128)(2,1)}) %reduce-scatter.65.cloned.1.call-update) | async-done | bytes 294928 | tf_op jit(solution)/shard_map/reduce_scatter | solution.py:389
  2147.9 69.6 %reduce-scatter.53.cloned.1.call-done = bf16[512,1536]{1,0:T(8,128)(2,1)} async-done(((bf16[2048,1536]{1,0:T(8,128)(2,1)}), bf16[512,1536]{1,0:T(8,128)(2,1)}) %reduce-scatter.53.cloned.1.call-update) | async-done | bytes 1572880 | tf_op jit(solution)/shard_map/reduce_scatter | solution.py:278
  2222.9 75.8 %all-reduce.11 = (f32[768]{0:T(1024)S(1)}, f32[768]{0:T(1024)S(1)}, f32[768]{0:T(1024)S(1)}, f32[768]{0:T(1024)S(1)}, f32[768]{0:T(1024)S(1)}) all-reduce(f32[768]{0:T(1024)S(1)} %add_add_fusion.4, f32[768]{0:T(1024)S(1)} %add_add_fusion.3, ...), channel_id=21, replica_groups=mesh['section'=2,'dp'=4,'tensor'=4] {'dp','tensor'}, use_global_device_ids=true, to_apply=%region_60.61.clone | all-reduce | flops 3840 | bytes 30720
  (1134 shorter events, 1450.1 us)
Async XLA Ops:
  7.2 172.9 %all-gather.25.cloned.1.call-start = ((), (), s32[]{:S(2)}) async-start(), calls=%async_computation.24 | async-start | bytes 3932160 | tf_op jit(solution)/shard_map/all_gather | solution.py:186
  99.4 194.0 %all-gather.41.cloned.1.call-start = ((), (), s32[]{:S(2)}) async-start(), calls=%async_computation.47 | async-start | bytes 1474560 | tf_op jit(solution)/shard_map/all_gather | solution.py:337
  100.1 193.3 %all-gather.27.cloned.1.call-start = ((), (), s32[]{:S(2)}) async-start(), calls=%async_computation.25 | async-start | bytes 3932160 | tf_op jit(solution)/shard_map/all_gather | solution.py:187
  100.9 212.2 %all-gather.43.cloned.1.call-start = ((), (), s32[]{:S(2)}) async-start(), calls=%async_computation.48 | async-start | bytes 1474560 | tf_op jit(solution)/shard_map/all_gather | solution.py:339
  101.5 260.3 %reduce-scatter.43.cloned.1.call-start = ((), (), s32[]{:S(2)}) async-start(), calls=%async_computation.26 | async-start | bytes 3932160 | tf_op jit(solution)/shard_map/reduce_scatter | solution.py:207
  369.7 158.3 %all-gather.31.cloned.1.call-start = ((), (), s32[]{:S(2)}) async-start(), calls=%async_computation.28 | async-start | bytes 3932160 | tf_op jit(solution)/shard_map/all_gather | solution.py:187
  371.3 225.0 %reduce-scatter.45.cloned.1.call-start = ((), (), s32[]{:S(2)}) async-start(), calls=%async_computation.29 | async-start | bytes 3932160 | tf_op jit(solution)/shard_map/reduce_scatter | solution.py:207
  652.4 459.1 %reduce-scatter.49.cloned.1.call-start = ((), (), s32[]{:S(2)}) async-start(), calls=%async_computation.33 | async-start | bytes 7864320 | tf_op jit(solution)/shard_map/reduce_scatter | solution.py:278
  1041.9 160.9 %all-gather.37.cloned.1.call-start = ((), (), s32[]{:S(2)}) async-start(), calls=%async_computation.34 | async-start | bytes 3932160 | tf_op jit(solution)/shard_map/all_gather | solution.py:248
  1123.8 405.1 %reduce-scatter.51.cloned.1.call-start = ((), (), s32[]{:S(2)}) async-start(), calls=%async_computation.35 | async-start | bytes 7864320 | tf_op jit(solution)/shard_map/reduce_scatter | solution.py:278
  1542.1 370.8 %reduce-scatter.85.cloned.1.call-start = ((), (), s32[]{:S(2)}) async-start(), calls=%async_computation.56 | async-start | bytes 81920
  1543.0 370.7 %reduce-scatter.79.cloned.1.call-start = ((), (), s32[]{:S(2)}) async-start(), calls=%async_computation.53 | async-start | bytes 491520
  1546.9 367.8 %reduce-scatter.73.cloned.1.call-start = ((), (), s32[]{:S(2)}) async-start(), calls=%async_computation.50 | async-start | bytes 61440
  1549.9 365.6 %reduce-scatter.47.cloned.1.call-start = ((), (), s32[]{:S(2)}) async-start(), calls=%async_computation.32 | async-start | bytes 3932160 | tf_op jit(solution)/shard_map/reduce_scatter | solution.py:207
  1557.9 360.6 %reduce-scatter.75.cloned.1.call-start = ((), (), s32[]{:S(2)}) async-start(), calls=%async_computation.51 | async-start | bytes 61440
  1559.1 360.1 %reduce-scatter.87.cloned.1.call-start = ((), (), s32[]{:S(2)}) async-start(), calls=%async_computation.57 | async-start | bytes 81920
  1561.6 358.5 %reduce-scatter.81.cloned.1.call-start = ((), (), s32[]{:S(2)}) async-start(), calls=%async_computation.54 | async-start | bytes 491520
  1565.3 355.8 %reduce-scatter.77.cloned.1.call-start = ((), (), s32[]{:S(2)}) async-start(), calls=%async_computation.52 | async-start | bytes 61440
  1870.0 154.4 %reduce-scatter.69.cloned.1.call-start = ((), (), s32[]{:S(2)}) async-start(), calls=%async_computation.45 | async-start | bytes 1474560 | tf_op jit(solution)/shard_map/reduce_scatter | solution.py:395
  1875.6 179.0 %reduce-scatter.71.cloned.1.call-start = ((), (), s32[]{:S(2)}) async-start(), calls=%async_computation.46 | async-start | bytes 1474560 | tf_op jit(solution)/shard_map/reduce_scatter | solution.py:395
  1882.6 202.3 %reduce-scatter.61.cloned.1.call-start = ((), (), s32[]{:S(2)}) async-start(), calls=%async_computation.41 | async-start | bytes 1474560 | tf_op jit(solution)/shard_map/reduce_scatter | solution.py:389
  1888.4 226.6 %reduce-scatter.63.cloned.1.call-start = ((), (), s32[]{:S(2)}) async-start(), calls=%async_computation.42 | async-start | bytes 1474560 | tf_op jit(solution)/shard_map/reduce_scatter | solution.py:389
  1894.3 251.6 %reduce-scatter.65.cloned.1.call-start = ((), (), s32[]{:S(2)}) async-start(), calls=%async_computation.43 | async-start | bytes 1474560 | tf_op jit(solution)/shard_map/reduce_scatter | solution.py:389
  1901.1 316.4 %reduce-scatter.53.cloned.1.call-start = ((), (), s32[]{:S(2)}) async-start(), calls=%async_computation.37 | async-start | bytes 7864320 | tf_op jit(solution)/shard_map/reduce_scatter | solution.py:278
  (250 other events, 13574.8 us)
Sparse Core Ops, SparseCore 0:
  99.5 39.6 all-gather.24
  140.8 36.8 all-gather.40
  180.1 42.7 all-gather.26
  224.4 30.2 all-gather.42
  321.2 40.5 reduce-scatter.42
  369.8 43.8 all-gather.28
  416.1 43.8 all-gather.30
  552.2 44.0 reduce-scatter.44
  598.2 43.8 all-gather.44
  652.6 44.2 all-gather.32
  1041.5 70.0 reduce-scatter.48
  1113.2 43.8 all-gather.34
  1158.9 43.8 all-gather.36
  1458.8 70.0 reduce-scatter.50
  1542.2 43.8 all-gather.38
  1651.8 42.0 reduce-scatter.46
  1939.1 24.8 reduce-scatter.58
  1966.3 27.8 reduce-scatter.66
  1996.4 27.8 reduce-scatter.68
  2026.7 27.9 reduce-scatter.70
  2056.9 27.9 reduce-scatter.60
  2087.1 27.9 reduce-scatter.62
  2117.9 27.9 reduce-scatter.64
  2148.8 68.6 reduce-scatter.52
  (11 shorter events, 217.7 us)
where the time goes:
time: 2320 us; the launch traced here: 2310 us
  matrix products  754 us (32%)
  waiting for transfers between devices  694 us (30%)
  other arithmetic  353 us (15%)
  blocking collectives  223 us (10%)
  local copies, waits for them, and re-layouts  206 us (9%)
  loops' own time  50.1 us (2%)
  between operations  24.5 us (1%)
    reduce_scatter x3, waiting for transfers between devices, backward_layer(): lax.psum_scatter(partial_value.astype(jnp.bfloat16), 'tensor', scatter_di...  209 us
    unnamed x2, blocking collectives  154 us
    dot_general x12, matrix products, one_block(): jnp.einsum('hqk,qhd->khd', probability.astype(jnp.bfloat16), grad_rows_bl...  123 us
    dot_general x24, matrix products, one_block(): jnp.einsum('qhd,khd->hqk', block_rows, key_rows, preferred_element_type=j...  109 us
    dynamic_update_slice x24, local copies, waits for them, and re-layouts, attend(): attended, log_sums = lax.map(one_block, (pieces, starts))  108 us
    and x24, other arithmetic, allowed_block(): return same_doc & causal & present  95.9 us
    dot_general x12, matrix products, times_transposed(): lax.dot_general(left_rows, right_rows, (((1,), (1,)), ((), ())), preferre...  90.4 us
    reduce_scatter x3, waiting for transfers between devices, shards(): lax.psum_scatter(matrices[3].astype(jnp.bfloat16), 'dp', scatter_dimensio...  89.2 us
  transfers between devices with their start and end apart: 39, of which 22 were waited for; matrix products, arithmetic and copies ran while one was open for 28% of the time, Pallas kernels for 0%

commit v1 on v0

v1 whole, which is shorter than its diff:
```python
import functools

import jax
import jax.numpy as jnp
from jax import lax
from jax.experimental import pallas as pl
from jax.experimental.pallas import tpu as pltpu
from jax.sharding import PartitionSpec as P

F32 = jnp.float32
BF = jnp.bfloat16
MESH = pl.DeviceIdType.MESH
HD = 64
ROT = 16
LIVE = 128
QB = 256
HW = 256
SUB = 64
EPS = 1e-05
NEG = -1e30
VMEM = pl.BlockSpec(memory_space=pltpu.VMEM)
ANY = pl.BlockSpec(memory_space=pl.ANY)
SMEM = pl.BlockSpec(memory_space=pltpu.SMEM)
DMA = pltpu.SemaphoreType.DMA


def sds(shape, dtype):
    return jax.ShapeDtypeStruct(shape, dtype)


def dg(a, b, ca, cb):
    return lax.dot_general(a, b, (((ca,), (cb,)), ((), ())), preferred_element_type=F32)


def dot(a, b):
    return jnp.dot(a, b, preferred_element_type=F32)


def ds(start, size):
    return pl.ds(pl.multiple_of(start, size), size)


def norm_stats(x):
    mu = jnp.mean(x, axis=-1, keepdims=True)
    xc = x - mu
    var = jnp.mean(xc * xc, axis=-1, keepdims=True)
    return xc, lax.rsqrt(var + EPS)


def head_lanes(width, heads):
    lane = lax.broadcasted_iota(jnp.int32, (1, width), 1)
    return [(lane >= h * HD) & (lane < (h + 1) * HD) for h in range(heads)]


def allow_mask(kc, sq, diag):
    m = kc == sq
    if diag:
        r = lax.broadcasted_iota(jnp.int32, (QB, QB), 0)
        c = lax.broadcasted_iota(jnp.int32, (QB, QB), 1)
        m = (m & (r <= c)) | (r == c)
    return m


def attn_fwd_kernel(heads, b_ref, q_ref, k_ref, v_ref, sr_ref, kc_ref, o_ref, lse_ref, vt, s_scr):
    n = q_ref.shape[0] // QB
    width = q_ref.shape[1]
    hm = head_lanes(width, heads)

    def turn(i, _):
        vt[:, ds(i * QB, QB)] = v_ref[ds(i * QB, QB), :].T
        return 0

    lax.fori_loop(0, n, turn, 0)

    def qloop(i, _):
        qi = ds(i * QB, QB)
        q = q_ref[qi, :]
        qm = [jnp.where(hm[h], q, jnp.zeros_like(q)) for h in range(heads)]
        sq = sr_ref[0:1, qi]
        lo = b_ref[0, i]
        hi = b_ref[1, i]

        def scores(j, slot, ms, diag):
            kj = ds(j * QB, QB)
            k = k_ref[kj, :]
            mask = allow_mask(kc_ref[kj, 0:1], sq, diag)
            out = []
            for h in range(heads):
                s = jnp.where(mask, dg(k, qm[h], 1, 1), NEG)
                s_scr[h, ds(slot * QB, QB), :] = s
                out.append(jnp.maximum(ms[h], jnp.max(s, axis=0, keepdims=True)))
            return tuple(out)

        ms = tuple(jnp.full((1, QB), NEG, F32) for _ in range(heads))
        ms = scores(i, 0, ms, True)
        ms = lax.fori_loop(lo, hi, lambda j, ms: scores(j, j - lo + 1, ms, False), ms)

        def weigh(j, slot, st):
            kj = ds(j * QB, QB)
            out = []
            for h in range(heads):
                total, acc = st[h]
                p = jnp.exp(s_scr[h, ds(slot * QB, QB), :] - ms[h])
                total = total + jnp.sum(p, axis=0, keepdims=True)
                acc = acc + dot(vt[h * HD : (h + 1) * HD, kj], p.astype(BF))
                out.append((total, acc))
            return tuple(out)

        st = tuple((jnp.zeros((1, QB), F32), jnp.zeros((HD, QB), F32)) for _ in range(heads))
        st = weigh(i, 0, st)
        st = lax.fori_loop(lo, hi, lambda j, st: weigh(j, j - lo + 1, st), st)
        ot = [st[h][1] * (1.0 / st[h][0]) for h in range(heads)]
        ot = jnp.concatenate(ot + [jnp.zeros((width - heads * HD, QB), F32)], axis=0)
        o_ref[qi, :] = ot.T.astype(BF)
        lse = [ms[h] + jnp.log(st[h][0]) for h in range(heads)]
        lse_ref[:, qi] = jnp.concatenate(lse + [jnp.zeros((8 - heads, QB), F32)], axis=0)
        return 0

    lax.fori_loop(0, n, qloop, 0)


def attn_fwd(heads, bounds, q, k, v, sr, kc):
    rows, width = q.shape
    return pl.pallas_call(
        functools.partial(attn_fwd_kernel, heads),
        out_shape=(sds((rows, width), BF), sds((8, rows), F32)),
        in_specs=[SMEM] + [VMEM] * 5,
        out_specs=(VMEM, VMEM),
        scratch_shapes=[pltpu.VMEM((width, rows), BF), pltpu.VMEM((heads, rows + QB, QB), F32)],
        compiler_params=pltpu.CompilerParams(vmem_limit_bytes=40 << 20),
        name="attn_fwd",
    )(bounds, q, k, v, sr, kc)


def turn_lanes(x, tab, sign):
    width = x.shape[1]
    c, s1, s2 = [jnp.concatenate([tab[:, a * 128 : (a + 1) * 128]] * (width // 128), axis=1) for a in range(3)]
    moved = pltpu.roll(x, width - ROT // 2, 1) * s1 + pltpu.roll(x, ROT // 2, 1) * s2
    return x * c + moved if sign > 0 else x * c - moved


def attn_bwd_kernel(
    heads, b_ref, q_ref, k_ref, v_ref, o_ref, do_ref, lse_ref, sr_ref, kc_ref, tab_ref, out_ref, kt, dk, dv
):
    rows, width = q_ref.shape
    n = rows // QB
    hm = head_lanes(width, heads)

    def turn(i, _):
        kt[:, ds(i * QB, QB)] = k_ref[ds(i * QB, QB), :].T
        return 0

    lax.fori_loop(0, n, turn, 0)
    dk[...] = jnp.zeros_like(dk)
    dv[...] = jnp.zeros_like(dv)
    rowid = lax.broadcasted_iota(jnp.int32, (8, width), 0)
    lane = lax.broadcasted_iota(jnp.int32, (8, width), 1)
    sel = ((lane >= rowid * HD) & (lane < (rowid + 1) * HD)).astype(F32).astype(BF)

    def qloop(i, _):
        qi = ds(i * QB, QB)
        q = q_ref[qi, :]
        do = do_ref[qi, :]
        z = jnp.zeros_like(q)
        qm = [jnp.where(hm[h], q, z) for h in range(heads)]
        dom = [jnp.where(hm[h], do, z) for h in range(heads)]
        qcat = jnp.concatenate(qm, axis=0)
        docat = jnp.concatenate(dom, axis=0)
        prod = do.astype(F32) * o_ref[qi, :].astype(F32)
        high = prod.astype(BF)
        low = (prod - high.astype(F32)).astype(BF)
        delta = dg(sel, high, 1, 1) + dg(sel, low, 1, 1)
        lse = lse_ref[:, qi]
        sq = sr_ref[0:1, qi]
        lo = b_ref[0, i]
        hi = b_ref[1, i]

        def step(j, dqs, diag):
            kj = ds(j * QB, QB)
            k = k_ref[kj, :]
            v = v_ref[kj, :]
            mask = allow_mask(kc_ref[kj, 0:1], sq, diag)
            ps, dss, out = [], [], []
            for h in range(heads):
                s = dg(k, qm[h], 1, 1)
                dp = dg(v, dom[h], 1, 1)
                p = jnp.where(mask, jnp.exp(jnp.where(mask, s - lse[h : h + 1, :], 0.0)), 0.0)
                score_grad = (p * (dp - delta[h : h + 1, :])).astype(BF)
                ps.append(p.astype(BF))
                dss.append(score_grad)
                out.append(dqs[h] + dot(kt[h * HD : (h + 1) * HD, kj], score_grad))
            dv[kj, :] += dot(jnp.concatenate(ps, axis=1), docat)
            dk[kj, :] += dot(jnp.concatenate(dss, axis=1), qcat)
            return tuple(out)

        dqs = tuple(jnp.zeros((HD, QB), F32) for _ in range(heads))
        dqs = step(i, dqs, True)
        dqs = lax.fori_loop(lo, hi, lambda j, d: step(j, d, False), dqs)
        dq = jnp.concatenate(list(dqs) + [jnp.zeros((width - heads * HD, QB), F32)], axis=0).T * 0.125
        out_ref[qi, 0:width] = turn_lanes(dq, tab_ref[qi, :], -1).astype(BF)
        return 0

    lax.fori_loop(0, n, qloop, 0)

    def finish(i, _):
        ii = ds(i * QB, QB)
        out_ref[ii, width : 2 * width] = turn_lanes(dk[ii, :], tab_ref[ii, :], -1).astype(BF)
        out_ref[ii, 2 * width : 3 * width] = dv[ii, :].astype(BF)
        return 0

    lax.fori_loop(0, n, finish, 0)


def attn_bwd(heads, bounds, q, k, v, o, do, lse, sr, kc, tab):
    rows, width = q.shape
    return pl.pallas_call(
        functools.partial(attn_bwd_kernel, heads),
        out_shape=sds((rows, 3 * width), BF),
        in_specs=[SMEM] + [VMEM] * 9,
        out_specs=VMEM,
        scratch_shapes=[
            pltpu.VMEM((width, rows), BF),
            pltpu.VMEM((rows, width), F32),
            pltpu.VMEM((rows, width), F32),
        ],
        compiler_params=pltpu.CompilerParams(vmem_limit_bytes=50 << 20),
        name="attn_bwd",
    )(bounds, q, k, v, o, do, lse, sr, kc, tab)


def places():
    t = lax.axis_index("tensor")
    x, y = t % 2, t // 2
    return t, 2 * y + (1 - x), 2 * (1 - y) + x, 3 - t


def greet(peers):
    bar = pltpu.get_barrier_semaphore()
    for peer in peers:
        pl.semaphore_signal(bar, inc=1, device_id=peer, device_id_type=MESH)
    pl.semaphore_wait(bar, len(peers))


def push(src, dst, ssem, rsem, peer):
    return pltpu.make_async_remote_copy(
        src_ref=src, dst_ref=dst, send_sem=ssem, recv_sem=rsem, device_id=peer, device_id_type=MESH
    )


def pick(i, values):
    out = values[-1]
    for n in range(len(values) - 2, -1, -1):
        out = jnp.where(i == n, values[n], out)
    return out


class Gather:
    def __init__(self, full, ssem, rsem):
        self.t, self.px, self.py, self.pd = places()
        self.full, self.ssem, self.rsem = full, ssem, rsem
        self.half = full.shape[0] // 8

    def rows(self, c, h):
        return ds((2 * c + h) * self.half, self.half)

    def copy(self, i, c, h, peer):
        ref = self.full.at[self.rows(c, h)]
        return push(ref, ref, self.ssem.at[i], self.rsem.at[i], {"tensor": peer})

    def plan(self):
        t, px, py = self.t, self.px, self.py
        return [
            self.copy(0, t, 0, px),
            self.copy(1, t, 1, py),
            self.copy(2, t, 1, px),
            self.copy(3, t, 0, py),
            self.copy(4, px, 0, py),
            self.copy(5, py, 1, px),
        ]

    def order(self, i):
        t, px, py, pd = self.t, self.px, self.py, self.pd
        return pick(i, [t, t, px, py, px, py, pd, pd]), pick(i, [0, 1, 0, 1, 1, 0, 0, 1])

    def arrive(self, i):
        plan = self.plan()

        @pl.when(i == 2)
        def _():
            plan[0].wait_recv()
            plan[4].start()
            plan[1].wait_recv()
            plan[5].start()

        for step in (4, 5, 6, 7):

            @pl.when(i == step)
            def _(step=step):
                plan[step - 2].wait_recv()

    def finish(self):
        for c in self.plan():
            c.wait_send()

    def run(self, work):
        def body(i, _):
            self.arrive(i)
            c, h = self.order(i)
            work((2 * c + h) * self.half)
            return 0

        lax.fori_loop(0, 8, body, 0)
        self.finish()


class Scatter:
    def __init__(self, part, r1x, r1y, r2x, r2y, ssem, rsem):
        self.t, self.px, self.py, self.pd = places()
        self.part, self.r1x, self.r1y, self.r2x, self.r2y = part, r1x, r1y, r2x, r2y
        self.ssem, self.rsem = ssem, rsem
        self.half = part.shape[0] // 8

    def rows(self, c, h):
        return ds((2 * c + h) * self.half, self.half)

    def copy(self, i, c, h, dst, peer):
        return push(self.part.at[self.rows(c, h)], dst, self.ssem.at[i], self.rsem.at[i], {"tensor": peer})

    def plan(self):
        px, py, pd = self.px, self.py, self.pd
        return [
            self.copy(0, pd, 0, self.r1x.at[1], px),
            self.copy(1, pd, 1, self.r1y.at[1], py),
            self.copy(2, px, 0, self.r1x.at[0], px),
            self.copy(3, py, 1, self.r1y.at[0], py),
            self.copy(4, py, 0, self.r2y, py),
            self.copy(5, px, 1, self.r2x, px),
        ]

    def run(self, work, between=None):
        t, px, py, pd = self.t, self.px, self.py, self.pd
        plan = self.plan()

        def body(i, _):
            c = pick(i, [pd, pd, px, py, py, px, t, t])
            h = pick(i, [0, 1, 0, 1, 0, 1, 0, 1])
            work((2 * c + h) * self.half)
            for step in range(4):

                @pl.when(i == step)
                def _(step=step):
                    plan[step].start()

            return 0

        lax.fori_loop(0, 8, body, 0)
        for first, c, h, buf, second in ((0, py, 0, self.r1x, 4), (1, px, 1, self.r1y, 5)):
            plan[first].wait_recv()

            def add(i, _, c=c, h=h, buf=buf):
                rr = ds((2 * c + h) * self.half + i * SUB, SUB)
                got = buf[1, ds(i * SUB, SUB), :].astype(F32)
                self.part[rr, :] = (self.part[rr, :].astype(F32) + got).astype(BF)
                return 0

            lax.fori_loop(0, self.half // SUB, add, 0)
            plan[second].start()
        if between is not None:
            between()

    def arrive(self, h):
        plan = self.plan()
        if h == 0:
            plan[2].wait_recv()
            plan[4].wait_recv()
        else:
            plan[3].wait_recv()
            plan[5].wait_recv()

    def total(self, h, i):
        near, far = (self.r1x, self.r2y) if h == 0 else (self.r1y, self.r2x)
        rr = ds((2 * self.t + h) * self.half + i * SUB, SUB)
        sub = ds(i * SUB, SUB)
        return self.part[rr, :].astype(F32) + near[0, sub, :].astype(F32) + far[sub, :].astype(F32)

    def finish(self):
        for c in self.plan():
            c.wait_send()


def scatter_scratch(rows, width):
    half = rows // 8
    return [
        pltpu.VMEM((rows, width), BF),
        pltpu.VMEM((2, half, width), BF),
        pltpu.VMEM((2, half, width), BF),
        pltpu.VMEM((half, width), BF),
        pltpu.VMEM((half, width), BF),
        DMA((6,)),
        DMA((6,)),
    ]


def gather_kernel(
    dp, tensor, w_ref, sv_ref, pos_ref, fr_ref, wf_ref, vec_ref, tab_ref, own, wss, wrs, fss, frs, vss, vrs
):
    s, z, t = lax.axis_index("section"), lax.axis_index("dp"), lax.axis_index("tensor")
    rows = w_ref.shape[0]
    mate = {"section": 1 - s}
    ring = [{"dp": (z + d) % dp} for d in range(1, dp)]
    group = [{"tensor": (t + d) % tensor} for d in range(1, tensor)]
    greet([mate] + ring + group)

    def block(layer, zz):
        return wf_ref.at[layer, ds(zz * rows, rows)]

    mine = [
        pltpu.make_async_copy(w_ref, block(s, z), own.at[0]),
        pltpu.make_async_copy(sv_ref, vec_ref.at[s, t, z], own.at[1]),
    ]
    for c in mine:
        c.start()
    nv = dp - 1 + tensor - 1 + 1
    first = [push(sv_ref, vec_ref.at[s, t, z], vss.at[d], vrs.at[d], peer) for d, peer in enumerate(ring)]
    for c in first:
        c.start()
    sends = [push(w_ref, block(s, z), wss.at[d], wrs.at[d], peer) for d, peer in enumerate(ring)]
    for c in sends:
        c.start()
    onward = [push(w_ref, block(s, z), fss.at[0], frs.at[0], mate)]
    onward[0].start()
    ang = fr_ref[:, 0:1] * pos_ref[...].astype(F32)
    cs, sn = jnp.cos(ang), jnp.sin(ang)
    wide = ang.shape[1]
    one, zero = jnp.ones((HD - ROT, wide), F32), jnp.zeros((HD - ROT, wide), F32)
    z8 = jnp.zeros_like(cs)
    pieces = ([cs, cs, one] * 2, [-sn, z8, zero] * 2, [z8, sn, zero] * 2)
    for a, piece in enumerate(pieces):
        tab_ref[:, a * 128 : (a + 1) * 128] = jnp.concatenate(piece, axis=0).T
    for c in mine:
        c.wait()
    for c in first:
        c.wait_recv()
    second = []
    for d, peer in enumerate(group):
        i = dp - 1 + d
        second.append(push(vec_ref.at[s, t], vec_ref.at[s, t], vss.at[i], vrs.at[i], peer))
        second[-1].start()
    for c in second:
        c.wait_recv()
    third = push(vec_ref.at[s], vec_ref.at[s], vss.at[nv - 1], vrs.at[nv - 1], mate)
    third.start()
    for d in range(dp - 1):
        sends[d].wait_recv()
        zz = (z - d - 1 + dp) % dp
        onward.append(push(block(s, zz), block(s, zz), fss.at[d + 1], frs.at[d + 1], mate))
        onward[-1].start()
    third.wait_recv()
    for c in onward:
        c.wait_recv()
    for c in first + sends + second + [third] + onward:
        c.wait_send()


def gather_all(dp, tensor, w, sv, pos, fr):
    rows, cols = w.shape
    seq = pos.shape[1]
    nv = dp - 1 + tensor
    return pl.pallas_call(
        functools.partial(gather_kernel, dp, tensor),
        out_shape=(
            sds((2, rows * dp, cols), BF),
            sds((2, tensor, dp) + sv.shape, F32),
            sds((seq, 3 * 128), F32),
        ),
        in_specs=[VMEM] * 4,
        out_specs=(ANY, VMEM, VMEM),
        scratch_shapes=[
            DMA((2,)),
            DMA((dp - 1,)),
            DMA((dp - 1,)),
            DMA((dp,)),
            DMA((dp,)),
            DMA((nv,)),
            DMA((nv,)),
        ],
        compiler_params=pltpu.CompilerParams(collective_id=1, has_side_effects=True, vmem_limit_bytes=40 << 20),
        name="gather_weights",
    )(w, sv, pos, fr)


QKV, FC1, FC2, OUT = 0, 1, 2, 3


def columns(model, ff):
    return {"qkv": 0, "fc1": 3 * HW, "fc2": 3 * HW + ff, "out": 3 * HW + 2 * ff, "end": 3 * HW + 2 * ff + HW}


def project(r0, half, hf, wqkv, wfc1, vec, tab, n1, n2, q, k, v, g, gp):
    rows = ds(r0, half)

    def norm(i, _):
        rr = ds(r0 + i * SUB, SUB)
        xc, r = norm_stats(hf[rr, :].astype(F32))
        xh = xc * r
        n1[rr, :] = (xh * vec[0:1, :] + vec[1:2, :]).astype(BF)
        n2[rr, :] = (xh * vec[3:4, :] + vec[4:5, :]).astype(BF)
        return 0

    lax.fori_loop(0, half // SUB, norm, 0)
    a = n1[rows, :]
    for part, dst in enumerate((q, k, v)):
        cols = slice(part * HW, (part + 1) * HW)
        y = dot(a, wqkv[:, cols]) + vec[6:7, cols]
        if part < 2:
            y = turn_lanes(y, tab[rows, :], 1)
        if part == 0:
            y = y * 0.125
        dst[rows, :] = y.astype(BF)
    a = n2[rows, :]
    for b in range(wfc1.shape[1] // 256):
        cols = slice(b * 256, (b + 1) * 256)
        y = dot(a, wfc1[:, cols]) + vec[7:8, cols]
        cdf = 0.5 + 0.5 * lax.erf(y * 0.7071067811865476)
        g[rows, cols] = (y * cdf).astype(BF)
        gp[rows, cols] = (cdf + y * jnp.exp(-0.5 * y * y) * 0.3989422804014327).astype(BF)


def branch_out(r0, half, o, g, wout, wfc2, part):
    rows = ds(r0, half)
    for b in range(part.shape[1] // 256):
        cols = slice(b * 256, (b + 1) * 256)
        y = dg(o[rows, :], wout[cols, :], 1, 1) + dg(g[rows, :], wfc2[cols, :], 1, 1)
        part[rows, cols] = y.astype(BF)


def back_head(r0, half, dyf, hf, g, gp, n2, o, wfc1, wfc2, wout, vec, do, e2, da, acc, vg):
    rows = ds(r0, half)
    model, ff = wfc1.shape
    dy = dyf[rows, :]
    for b in range(ff // 256):
        cols = slice(b * 256, (b + 1) * 256)
        y = dot(dy, wfc2[:, cols]) * gp[rows, cols].astype(F32)
        low = y.astype(BF)
        da[:, cols] = low
        vg[7:8, cols] += jnp.sum(low.astype(F32), axis=0, keepdims=True)
    do[rows, :] = dot(dy, wout[...]).astype(BF)
    xc, r = norm_stats(hf[rows, :].astype(F32))
    xh = xc * r
    for b in range(model // 256):
        cols = slice(b * 256, (b + 1) * 256)
        dn = dg(da[...], wfc1[cols, :], 1, 1)
        vg[3:4, cols] += jnp.sum(dn * xh[:, cols], axis=0, keepdims=True)
        vg[4:5, cols] += jnp.sum(dn, axis=0, keepdims=True)
        e2[rows, cols] = (dn * vec[3:4, cols]).astype(BF)
    n2t = n2[rows, :].T
    dyt = dy.T
    for b in range(ff // 256):
        cols = slice(b * 256, (b + 1) * 256)
        acc[:, cols] += dot(n2t, da[:, cols])
        acc[:, ff + b * 256 : ff + (b + 1) * 256] += dot(dyt, g[rows, cols])
    acc[:, 2 * ff :] += dot(dyt, o[rows, :])


def back_tail(r0, half, dmix, hf, e2, wqkv, vec, part, vg):
    rows = ds(r0, half)
    dm = dmix[rows, :]
    vg[6:7, :] += jnp.sum(dm.astype(F32), axis=0, keepdims=True)
    xc, r = norm_stats(hf[rows, :].astype(F32))
    xh = xc * r
    for b in range(part.shape[1] // 256):
        cols = slice(b * 256, (b + 1) * 256)
        dn = dg(dm, wqkv[cols, :], 1, 1)
        vg[0:1, cols] += jnp.sum(dn * xh[:, cols], axis=0, keepdims=True)
        vg[1:2, cols] += jnp.sum(dn, axis=0, keepdims=True)
        part[rows, cols] = (dn * vec[0:1, cols] + e2[rows, cols].astype(F32)).astype(BF)


def qkv_grad(n1, dmix, acc, half):
    acc[...] = jnp.zeros_like(acc)

    def body(i, _):
        rows = ds(i * half, half)
        n1t = n1[rows, :].T
        for b in range(3):
            cols = slice(b * HW, (b + 1) * HW)
            acc[:, cols] += dot(n1t, dmix[rows, cols])
        return 0

    lax.fori_loop(0, n1.shape[0] // half, body, 0)


def store_low(acc, out):
    def body(i, _):
        rr = ds(i * SUB, SUB)
        out[rr, :] = acc[rr, :].astype(BF)
        return 0

    lax.fori_loop(0, acc.shape[0] // SUB, body, 0)


def residual_out(sc, own, off, vec, dst, dst2=None, dst2_off=None, after=None):
    for h in range(2):
        sc.arrive(h)

        def body(i, _, h=h):
            rr = ds(h * sc.half + i * SUB, SUB)
            base = own[ds(off + h * sc.half + i * SUB, SUB), :].astype(F32)
            y = (base + sc.total(h, i) + vec[2:3, :] + vec[5:6, :]).astype(BF)
            dst[rr, :] = y
            if dst2 is not None:
                dst2[ds(dst2_off + h * sc.half + i * SUB, SUB), :] = y
            return 0

        lax.fori_loop(0, sc.half // SUB, body, 0)
        if after is not None:
            after(h)


def grad_out(sc, dy, dy_off, hf, vec, dst, dst2=None, dst2_off=None, after=None):
    base = sc.t * 2 * sc.half
    for h in range(2):
        sc.arrive(h)

        def body(i, _, h=h):
            off = h * sc.half + i * SUB
            xc, r = norm_stats(hf[ds(base + off, SUB), :].astype(F32))
            xh = xc * r
            e = sc.total(h, i)
            m1 = jnp.mean(e, axis=-1, keepdims=True)
            m2 = jnp.mean(e * xh, axis=-1, keepdims=True)
            du = dy[ds(dy_off + off, SUB), :].astype(F32) + r * (e - m1 - xh * m2)
            low = du.astype(BF)
            dst[ds(off, SUB), :] = low
            if dst2 is not None:
                dst2[ds(dst2_off + off, SUB), :] = low
            return 0

        lax.fori_loop(0, sc.half // SUB, body, 0)
        if after is not None:
            after(h)


def start_half(ga, h):
    plan = ga.plan()
    for i in ((0, 3) if h == 0 else (1, 2)):
        plan[i].start()


def column_sum(ref, off, count, vg, row):
    def body(i, acc):
        return acc + jnp.sum(ref[ds(off + i * SUB, SUB), :].astype(F32), axis=0, keepdims=True)

    vg[row : row + 1, :] = lax.fori_loop(0, count // SUB, body, jnp.zeros((1, ref.shape[1]), F32))


def load(pairs, sem):
    copies = [pltpu.make_async_copy(a, b, sem.at[i]) for i, (a, b) in enumerate(pairs)]
    for c in copies:
        c.start()
    return copies


def params(cid, mib=58):
    return pltpu.CompilerParams(collective_id=cid, has_side_effects=True, vmem_limit_bytes=mib << 20)


def neighbours():
    t, px, py, pd = places()
    return [{"tensor": px}, {"tensor": py}]


def in_kernel(col, x_ref, wf, vec, tab, hf, n1, n2, q, k, v, g, gp, wqkv, wfc1, gss, grs, lsem):
    greet(neighbours())
    ga = Gather(hf, gss, grs)
    loads = load(
        [
            (x_ref, hf.at[ds(ga.t * 2 * ga.half, 2 * ga.half)]),
            (wf.at[0, :, col["qkv"] : col["fc1"]], wqkv),
            (wf.at[0, :, col["fc1"] : col["fc2"]], wfc1),
        ],
        lsem,
    )
    loads[0].wait()
    start_half(ga, 0)
    start_half(ga, 1)
    loads[1].wait()
    loads[2].wait()
    ga.run(lambda r0: project(r0, ga.half, hf, wqkv, wfc1, vec, tab, n1, n2, q, k, v, g, gp))


def project_shapes(seq, model, ff):
    return (
        sds((seq, model), BF),
        sds((seq, model), BF),
        sds((seq, model), BF),
        sds((seq, HW), BF),
        sds((seq, HW), BF),
        sds((seq, HW), BF),
        sds((seq, ff), BF),
        sds((seq, ff), BF),
    )


def layer_in(col, ff, x, wf, vec, tab):
    seq, model = tab.shape[0], x.shape[1]
    return pl.pallas_call(
        functools.partial(in_kernel, col),
        out_shape=project_shapes(seq, model, ff),
        in_specs=[VMEM, ANY, VMEM, VMEM],
        out_specs=(VMEM,) * 8,
        scratch_shapes=[pltpu.VMEM((model, 3 * HW), BF), pltpu.VMEM((model, ff), BF), DMA((6,)), DMA((6,)), DMA((3,))],
        compiler_params=params(2),
        name="layer_in",
    )(x, wf, vec, tab)


def mid_kernel(
    col, o, g_in, x_ref, wf, vec0, vec1, tab, h_ref, hf, n1, n2, q, k, v, g, gp,
    wout, wfc2, wqkv, wfc1, part, r1x, r1y, r2x, r2y, sss, srs, gss, grs, lsem,
):
    greet(neighbours())
    loads = load(
        [
            (wf.at[0, :, col["out"] : col["end"]], wout),
            (wf.at[0, :, col["fc2"] : col["out"]], wfc2),
            (wf.at[1, :, col["qkv"] : col["fc1"]], wqkv),
            (wf.at[1, :, col["fc1"] : col["fc2"]], wfc1),
        ],
        lsem,
    )
    loads[0].wait()
    loads[1].wait()
    sc = Scatter(part, r1x, r1y, r2x, r2y, sss, srs)
    ga = Gather(hf, gss, grs)
    sc.run(lambda r0: branch_out(r0, sc.half, o, g_in, wout, wfc2, part))
    residual_out(sc, x_ref, 0, vec0, h_ref, hf, sc.t * 2 * sc.half, lambda h: start_half(ga, h))
    loads[2].wait()
    loads[3].wait()
    ga.run(lambda r0: project(r0, ga.half, hf, wqkv, wfc1, vec1, tab, n1, n2, q, k, v, g, gp))
    sc.finish()


def layer_mid(col, ff, o, g, x, wf, vec0, vec1, tab):
    seq, model = tab.shape[0], x.shape[1]
    return pl.pallas_call(
        functools.partial(mid_kernel, col),
        out_shape=(sds(x.shape, BF),) + project_shapes(seq, model, ff),
        in_specs=[VMEM, VMEM, VMEM, ANY, VMEM, VMEM, VMEM],
        out_specs=(VMEM,) * 9,
        scratch_shapes=[
            pltpu.VMEM((model, HW), BF),
            pltpu.VMEM((model, ff), BF),
            pltpu.VMEM((model, 3 * HW), BF),
            pltpu.VMEM((model, ff), BF),
        ]
        + scatter_scratch(seq, model)
        + [DMA((6,)), DMA((6,)), DMA((4,))],
        compiler_params=params(3),
        name="layer_mid",
    )(o, g, x, wf, vec0, vec1, tab)


def turn_kernel(
    col, o, g, h_ref, hf, cot, wf, vec, n2, gp, y_ref, dyf, do, e2, gr, vg,
    wout, wfc2, wfc1, da, acc, part, r1x, r1y, r2x, r2y, sss, srs, gss, grs, lsem,
):
    greet(neighbours())
    ga = Gather(dyf, gss, grs)
    sc = Scatter(part, r1x, r1y, r2x, r2y, sss, srs)
    loads = load(
        [
            (cot, dyf.at[ds(ga.t * 2 * ga.half, 2 * ga.half)]),
            (wf.at[1, :, col["out"] : col["end"]], wout),
            (wf.at[1, :, col["fc2"] : col["out"]], wfc2),
            (wf.at[1, :, col["fc1"] : col["fc2"]], wfc1),
        ],
        lsem,
    )
    loads[0].wait()
    start_half(ga, 0)
    start_half(ga, 1)
    vg[...] = jnp.zeros_like(vg)
    acc[...] = jnp.zeros_like(acc)
    for c in loads[1:]:
        c.wait()
    sc.run(lambda r0: branch_out(r0, sc.half, o, g, wout, wfc2, part))
    ga.run(lambda r0: back_head(r0, ga.half, dyf, hf, g, gp, n2, o, wfc1, wfc2, wout, vec, do, e2, da, acc, vg))
    column_sum(cot, 0, cot.shape[0], vg, 2)
    store_low(acc, gr)
    residual_out(sc, h_ref, 0, vec, y_ref)
    sc.finish()


def layer_turn(col, ff, o, g, h, hf, cot, wf, vec, n2, gp):
    seq, model = hf.shape
    return pl.pallas_call(
        functools.partial(turn_kernel, col),
        out_shape=(
            sds(h.shape, BF),
            sds((seq, model), BF),
            sds((seq, HW), BF),
            sds((seq, model), BF),
            sds((model, 2 * ff + HW), BF),
            sds((8, model), F32),
        ),
        in_specs=[VMEM] * 5 + [ANY] + [VMEM] * 3,
        out_specs=(VMEM,) * 6,
        scratch_shapes=[
            pltpu.VMEM((model, HW), BF),
            pltpu.VMEM((model, ff), BF),
            pltpu.VMEM((model, ff), BF),
            pltpu.VMEM((seq // 8, ff), BF),
            pltpu.VMEM((model, 2 * ff + HW), F32),
        ]
        + scatter_scratch(seq, model)
        + [DMA((6,)), DMA((6,)), DMA((4,))],
        compiler_params=params(4, 63),
        name="layer_turn",
    )(o, g, h, hf, cot, wf, vec, n2, gp)


def back_kernel(
    col, dmix, e2_in, cot, hf, n1, wf, vec1, vec0, xf, g, gp, n2, o, dh_ref, dhf, gq, vgf, do, e2, gr, vgd,
    wqkv, wout, wfc2, wfc1, da, acc, part, r1x, r1y, r2x, r2y, sss, srs, gss, grs, lsem,
):
    greet(neighbours())
    ga = Gather(dhf, gss, grs)
    sc = Scatter(part, r1x, r1y, r2x, r2y, sss, srs)
    loads = load(
        [
            (wf.at[1, :, col["qkv"] : col["fc1"]], wqkv),
            (wf.at[0, :, col["out"] : col["end"]], wout),
            (wf.at[0, :, col["fc2"] : col["out"]], wfc2),
            (wf.at[0, :, col["fc1"] : col["fc2"]], wfc1),
        ],
        lsem,
    )
    vgf[...] = jnp.zeros_like(vgf)
    vgd[...] = jnp.zeros_like(vgd)
    loads[0].wait()

    def between():
        small = acc.at[:, 0 : 3 * HW]
        qkv_grad(n1, dmix, small, sc.half)
        store_low(small, gq)
        acc[...] = jnp.zeros_like(acc)

    sc.run(lambda r0: back_tail(r0, sc.half, dmix, hf, e2_in, wqkv, vec1, part, vgf), between)
    grad_out(sc, cot, 0, hf, vec1, dh_ref, dhf, sc.t * 2 * sc.half, lambda h: start_half(ga, h))
    for c in loads[1:]:
        c.wait()
    ga.run(lambda r0: back_head(r0, ga.half, dhf, xf, g, gp, n2, o, wfc1, wfc2, wout, vec0, do, e2, da, acc, vgd))
    column_sum(dh_ref, 0, dh_ref.shape[0], vgd, 2)
    store_low(acc, gr)
    sc.finish()


def layer_back(col, ff, dmix, e2, cot, hf, n1, wf, vec1, vec0, xf, g, gp, n2, o):
    seq, model = hf.shape
    return pl.pallas_call(
        functools.partial(back_kernel, col),
        out_shape=(
            sds(cot.shape, BF),
            sds((seq, model), BF),
            sds((model, 3 * HW), BF),
            sds((8, model), F32),
            sds((seq, HW), BF),
            sds((seq, model), BF),
            sds((model, 2 * ff + HW), BF),
            sds((8, model), F32),
        ),
        in_specs=[VMEM] * 5 + [ANY] + [VMEM] * 7,
        out_specs=(VMEM,) * 8,
        scratch_shapes=[
            pltpu.VMEM((model, 3 * HW), BF),
            pltpu.VMEM((model, HW), BF),
            pltpu.VMEM((model, ff), BF),
            pltpu.VMEM((model, ff), BF),
            pltpu.VMEM((seq // 8, ff), BF),
            pltpu.VMEM((model, 2 * ff + HW), F32),
        ]
        + scatter_scratch(seq, model)
        + [DMA((6,)), DMA((6,)), DMA((4,))],
        compiler_params=params(5, 63),
        name="layer_back",
    )(dmix, e2, cot, hf, n1, wf, vec1, vec0, xf, g, gp, n2, o)


def last_kernel(
    col, dmix, e2_in, dh, xf, n1, wf, vec0, dx_ref, gq, vgf,
    wqkv, acc, part, r1x, r1y, r2x, r2y, sss, srs, lsem,
):
    greet(neighbours())
    sc = Scatter(part, r1x, r1y, r2x, r2y, sss, srs)
    loads = load([(wf.at[0, :, col["qkv"] : col["fc1"]], wqkv)], lsem)
    vgf[...] = jnp.zeros_like(vgf)
    loads[0].wait()

    def between():
        qkv_grad(n1, dmix, acc, sc.half)
        store_low(acc, gq)

    sc.run(lambda r0: back_tail(r0, sc.half, dmix, xf, e2_in, wqkv, vec0, part, vgf), between)
    grad_out(sc, dh, 0, xf, vec0, dx_ref)
    sc.finish()


def layer_last(col, dmix, e2, dh, xf, n1, wf, vec0):
    seq, model = xf.shape
    return pl.pallas_call(
        functools.partial(last_kernel, col),
        out_shape=(sds(dh.shape, BF), sds((model, 3 * HW), BF), sds((8, model), F32)),
        in_specs=[VMEM] * 5 + [ANY] + [VMEM],
        out_specs=(VMEM,) * 3,
        scratch_shapes=[pltpu.VMEM((model, 3 * HW), BF), pltpu.VMEM((model, 3 * HW), F32)]
        + scatter_scratch(seq, model)
        + [DMA((1,))],
        compiler_params=params(6),
        name="layer_last",
    )(dmix, e2, dh, xf, n1, wf, vec0)


def reduce_kernel(
    dp, tensor, gq0, gr0, gq1, gr1, vf0, vd0, vf1, vd1, out, vout,
    rq, rr, sb, rb, va, vr, vb, gss, grs, pss, prs, vss, vrs,
):
    s, z, t = lax.axis_index("section"), lax.axis_index("dp"), lax.axis_index("tensor")
    mate = {"section": 1 - s}
    ring = [{"dp": (z + d) % dp} for d in range(1, dp)]
    group = [{"tensor": (t + d) % tensor} for d in range(1, tensor)]
    greet([mate] + ring + group)
    rows = out.shape[0]
    nq = gq0.shape[1]

    def swap(q, r):
        return [push(q, rq, gss.at[0], grs.at[0], mate), push(r, rr, gss.at[1], grs.at[1], mate)]

    @pl.when(s == 0)
    def _():
        for c in swap(gq1, gr1):
            c.start()

    @pl.when(s == 1)
    def _():
        for c in swap(gq0, gr0):
            c.start()

    va[0, 0:8, :] = vf0[...] + vd0[...]
    va[0, 8:16, :] = vf1[...] + vd1[...]
    for c in swap(gq0, gr0):
        c.wait_recv()
    vsend = [push(va.at[0], vr.at[0], vss.at[0], vrs.at[0], mate)]
    vsend[0].start()
    sends = [push(sb.at[d], rb.at[d], pss.at[d], prs.at[d], peer) for d, peer in enumerate(ring)]

    def own_sum(zz, write):
        def body(i, _):
            src = ds(zz * rows + i * 16, 16)
            mine = lax.select(s == 0, gq0[src, :].astype(F32), gq1[src, :].astype(F32))
            write(i, 0, nq, mine + rq[src, :].astype(F32))
            mine = lax.select(s == 0, gr0[src, :].astype(F32), gr1[src, :].astype(F32))
            write(i, nq, out.shape[1], mine + rr[src, :].astype(F32))
            return 0

        lax.fori_loop(0, rows // 16, body, 0)

    for d in range(dp - 1):

        def write(i, a, b, value, d=d):
            sb[d, ds(i * 16, 16), a:b] = value.astype(BF)

        own_sum((z + d + 1) % dp, write)
        sends[d].start()
        if d == 0:
            vsend[0].wait_recv()
            va[1] = va[0] + vr[0]
    first = [push(va.at[1], vr.at[1 + d], vss.at[1 + d], vrs.at[1 + d], peer) for d, peer in enumerate(ring)]
    for c in first:
        c.start()

    def write_own(i, a, b, value):
        out[ds(i * 16, 16), a:b] = value

    own_sum(z, write_own)
    total = va[1]
    for d, c in enumerate(first):
        c.wait_recv()
        total = total + vr[1 + d]
    va[2] = total
    for d in range(dp - 1):
        sends[d].wait_recv()

        def add(i, _, d=d):
            rr_ = ds(i * 16, 16)
            out[rr_, :] += rb[d, rr_, :].astype(F32)
            return 0

        lax.fori_loop(0, rows // 16, add, 0)
        if d == 0:
            second = []
            for e, peer in enumerate(group):
                i = dp + e
                second.append(push(va.at[2], vr.at[i], vss.at[i], vrs.at[i], peer))
                second[-1].start()
    extra = jnp.zeros_like(total)
    for e, c in enumerate(second):
        c.wait_recv()
        extra = extra + vr[dp + e]
    row = lax.broadcasted_iota(jnp.int32, total.shape, 0)
    vout[...] = total + jnp.where(row % 8 < 6, extra, 0.0)
    for c in swap(gq0, gr0) + vsend + first + second + sends:
        c.wait_send()


def reduce_all(dp, tensor, gq0, gr0, gq1, gr1, vf0, vd0, vf1, vd1):
    model, nq = gq0.shape
    cols = nq + gr0.shape[1]
    rows = model // dp
    nv = dp + tensor - 1
    return pl.pallas_call(
        functools.partial(reduce_kernel, dp, tensor),
        out_shape=(sds((rows, cols), F32), sds((16, model), F32)),
        in_specs=[VMEM] * 8,
        out_specs=(VMEM, VMEM),
        scratch_shapes=[
            pltpu.VMEM(gq0.shape, BF),
            pltpu.VMEM(gr0.shape, BF),
            pltpu.VMEM((dp - 1, rows, cols), BF),
            pltpu.VMEM((dp - 1, rows, cols), BF),
            pltpu.VMEM((3, 16, model), F32),
            pltpu.VMEM((nv, 16, model), F32),
            pltpu.VMEM((8, 128), F32),
            DMA((2,)),
            DMA((2,)),
            DMA((dp - 1,)),
            DMA((dp - 1,)),
            DMA((nv,)),
            DMA((nv,)),
        ],
        compiler_params=params(7),
        name="reduce_grads",
    )(gq0, gr0, gq1, gr1, vf0, vd0, vf1, vd1)


def attention_plan(seg, live):
    seq = seg.shape[0]
    counter = jnp.arange(seq, dtype=jnp.int32)
    before = [jnp.sum((seg == v).astype(jnp.int32)) for v in range(3)]
    start = sum(jnp.where(seg > v, before[v], 0) for v in range(3))
    kc = jnp.where(counter < live * LIVE, seg, -1)
    lo = start[::QB] // QB
    hi = jnp.minimum(jnp.arange(seq // QB, dtype=jnp.int32), (live * LIVE + QB - 1) // QB)
    bounds = jnp.stack([jnp.minimum(lo, hi), hi]).astype(jnp.int32)
    return bounds, (counter - start)[None, :], seg[None, :], kc[:, None]


def by_part(w):
    rows = w.shape[0]
    heads = w.shape[1] // (3 * HD)
    w = w.reshape(rows, heads, 3, HD).transpose(0, 2, 1, 3).reshape(rows, 3, heads * HD)
    return jnp.pad(w, ((0, 0), (0, 0), (0, HW - heads * HD))).reshape(rows, 3 * HW)


def by_head(w, heads):
    rows = w.shape[0]
    w = w.reshape(rows, 3, HW)[:, :, : heads * HD].reshape(rows, 3, heads, HD)
    return w.transpose(0, 2, 1, 3).reshape(rows, heads * 3 * HD)


def shards(
    dp, tensor, inputs, cotangent, segments, live_blocks, ln1_gain, ln1_bias, qkv_weight, qkv_bias,
    out_weight, out_bias, ln2_gain, ln2_bias, fc1_weight, fc1_bias, fc2_weight, fc2_bias,
):
    s, z, t = lax.axis_index("section"), lax.axis_index("dp"), lax.axis_index("tensor")
    model = inputs.shape[-1]
    ff = fc1_weight.shape[2]
    heads = qkv_bias.shape[1]
    col = columns(model, ff)

    def mine(a):
        return lax.dynamic_index_in_dim(a, s, 0, keepdims=False)[0]

    x, cot, seg, live = mine(inputs), mine(cotangent), mine(segments), mine(live_blocks)
    bounds, pos, sr, kc = attention_plan(seg, live)
    wout = jnp.pad(out_weight[0].T, ((0, 0), (0, HW - heads * HD)))
    w = jnp.concatenate([by_part(qkv_weight[0]), fc1_weight[0], fc2_weight[0].T, wout], axis=1)
    small = jnp.stack([ln1_gain[0], ln1_bias[0], out_bias[0], ln2_gain[0], ln2_bias[0], fc2_bias[0]])
    own = small.shape[1]

    def lanes(a):
        return jnp.pad(a.astype(F32), ((0, 0), (0, 128 - a.shape[1])))

    sv = jnp.concatenate([lanes(small), lanes(qkv_bias[0]), lanes(fc1_bias[0])], axis=0)
    sv = jnp.pad(sv, ((0, -sv.shape[0] % 8), (0, 0)))
    fr = 10000.0 ** (-(jnp.arange(ROT // 2, dtype=F32) * (2.0 / ROT)))
    fr = jnp.broadcast_to(fr[:, None], (ROT // 2, 128))
    wf, vecs, tab = gather_all(dp, tensor, w, sv, pos, fr)
    wide = vecs[..., :6, :own].transpose(0, 3, 2, 1, 4).reshape(2, 6, model)
    here = lax.dynamic_index_in_dim(vecs, t, 1, keepdims=False)
    qw, fw = qkv_bias.shape[2], fc1_bias.shape[2]
    qb = here[:, :, 6 : 6 + heads, :qw].transpose(0, 2, 1, 3).reshape(2, heads * 3 * HD)
    fb = here[:, :, 6 + heads : 6 + 2 * heads, :fw].transpose(0, 2, 1, 3).reshape(2, 1, ff)
    vec = jnp.concatenate([wide, by_part(qb)[:, None], fb], axis=1)
    v0, v1 = vec[0], vec[1]

    xf, n1a, n2a, qa, ka, va, ga, gpa = layer_in(col, ff, x, wf, v0, tab)
    oa, lsea = attn_fwd(heads, bounds, qa, ka, va, sr, kc)
    h, hf, n1b, n2b, qb_, kb, vb, gb, gpb = layer_mid(col, ff, oa, ga, x, wf, v0, v1, tab)
    ob, lseb = attn_fwd(heads, bounds, qb_, kb, vb, sr, kc)
    y, dyf, dob, e2b, grb, vdb = layer_turn(col, ff, ob, gb, h, hf, cot, wf, v1, n2b, gpb)
    dmb = attn_bwd(heads, bounds, qb_, kb, vb, ob, dob, lseb, sr, kc, tab)
    dh, dhf, gqb, vfb, doa, e2a, gra, vda = layer_back(
        col, ff, dmb, e2b, cot, hf, n1b, wf, v1, v0, xf, ga, gpa, n2a, oa
    )
    dma = attn_bwd(heads, bounds, qa, ka, va, oa, doa, lsea, sr, kc, tab)
    dx, gqa, vfa = layer_last(col, dma, e2a, dh, xf, n1a, wf, v0)
    gw, gv = reduce_all(dp, tensor, gqa, gra, gqb, grb, vfa, vda, vfb, vdb)

    first = s == 0

    def swapped(a0, a1):
        got = lax.ppermute(jnp.where(first, a1, a0), "section", [(0, 1), (1, 0)])
        keep = jnp.where(first, a0, a1)
        return jnp.stack([jnp.where(first, keep, got), jnp.where(first, got, keep)])[None, :, None]

    section_outputs = swapped(h, y)
    input_grads = swapped(dx, dh)
    gv = lax.dynamic_index_in_dim(gv.reshape(2, 8, model), s, 0, keepdims=False)
    short = lax.dynamic_slice_in_dim(gv[:6], (z * tensor + t) * own, own, 1)
    gqb_ = by_head(gv[6:7], heads).reshape(heads, 3 * HD)
    gqb_ = lax.dynamic_slice_in_dim(gqb_, z * qw, qw, 1)[None]
    gfb = lax.dynamic_slice_in_dim(gv[7].reshape(heads, ff // heads), z * fw, fw, 1)[None]
    gqkv = by_head(gw[:, : col["fc1"]], heads)[None]
    gfc1 = gw[:, col["fc1"] : col["fc2"]][None]
    gfc2 = gw[:, col["fc2"] : col["out"]].T[None]
    gout = gw[:, col["out"] : col["out"] + heads * HD].T[None]
    return (
        section_outputs,
        input_grads,
        short[0:1],
        short[1:2],
        gqkv,
        gqb_,
        gout,
        short[2:3],
        short[3:4],
        short[4:5],
        gfc1,
        gfb,
        gfc2,
        short[2:3],
    )


def solution(mesh):
    both = ("dp", "tensor")
    in_specs = (
        P(None, "dp", "tensor", None),
        P(None, "dp", "tensor", None),
        P(None, "dp", None),
        P(None, "dp"),
        P("section", both),
        P("section", both),
        P("section", "dp", "tensor"),
        P("section", "tensor", "dp"),
        P("section", "tensor", "dp"),
        P("section", both),
        P("section", both),
        P("section", both),
        P("section", "dp", "tensor"),
        P("section", "tensor", "dp"),
        P("section", "tensor", "dp"),
        P("section", both),
    )
    out_specs = (
        P("section", None, "dp", "tensor", None),
        P("section", None, "dp", "tensor", None),
        P("section", both),
        P("section", both),
        P("section", "dp", "tensor"),
        P("section", "tensor", "dp"),
        P("section", "tensor", "dp"),
        P("section", both),
        P("section", both),
        P("section", both),
        P("section", "dp", "tensor"),
        P("section", "tensor", "dp"),
        P("section", "tensor", "dp"),
        P("section", both),
    )
    body = functools.partial(shards, mesh.shape["dp"], mesh.shape["tensor"])
    return jax.shard_map(body, mesh=mesh, in_specs=in_specs, out_specs=out_specs, check_vma=False)
```

time: 2320 us -> 643 us (0.28)
  matrix products: 754 us -> 0 us
  waiting for transfers between devices: 694 us -> 0.01 us
  Pallas kernels: 0 us -> 586 us
  other arithmetic: 353 us -> 13.2 us
  blocking collectives: 223 us -> 0 us
  local copies, waits for them, and re-layouts: 206 us -> 44.2 us
  loops' own time: 50.1 us -> 0 us
    dot_general x120 -> x0, matrix products: 754 us -> none  [the longest x12 123 us: one_block(): jnp.einsum('hqk,qhd->khd', probability.astype(jnp.bfloat16), grad_rows_bl...]
    pallas_call x0 -> x11, Pallas kernels: none -> 586 us  [the longest x1 151 us: reduce_all(): pl.pallas_call(functools.partial(reduce_kernel, dp, tensor), out_shape=(s...]
    reduce_scatter x15 -> x0, waiting for transfers between devices: 506 us -> none  [the longest x3 209 us: backward_layer(): lax.psum_scatter(partial_value.astype(jnp.bfloat16), 'tensor', scatter_di...]
    all_gather x11 -> x0, waiting for transfers between devices: 177 us -> none  [the longest x3 86.2 us: backward_layer(): whole_grad = lax.all_gather(downward, 'tensor', axis=0, tiled=True)]
    unnamed x2 -> x0, blocking collectives: 154 us -> none
    dynamic_update_slice x24 -> x0, local copies, waits for them, and re-layouts: 108 us -> none  [attend(): attended, log_sums = lax.map(one_block, (pieces, starts))]
    reduce_sum x27 -> x1, other arithmetic: 102 us -> 0.69 us  [attention_plan(): before = [jnp.sum((seg == v).astype(jnp.int32)) for v in range(3)]]
    and x24 -> x0, other arithmetic: 95.9 us -> none  [allowed_block(): return same_doc & causal & present]
  transfers between devices with their start and end apart: 39 -> 2, of which waited for: 22 -> 0; matrix products, arithmetic and copies ran while one was open for 28% -> 3% of each run, Pallas kernels for 0% -> 23%
where the time goes in v1:
time: 643 us; the launch traced here: 645 us
  Pallas kernels  586 us (91%)
  local copies, waits for them, and re-layouts  44.2 us (7%)
  other arithmetic  13.2 us (2%)
    pallas_call x1, Pallas kernels, reduce_all(): pl.pallas_call(functools.partial(reduce_kernel, dp, tensor), out_shape=(s...  151 us
    pallas_call x1, Pallas kernels, gather_all(): pl.pallas_call(functools.partial(gather_kernel, dp, tensor), out_shape=(s...  76.1 us
    pallas_call x1, Pallas kernels, layer_mid(): pl.pallas_call(functools.partial(mid_kernel, col), out_shape=(sds(x.shape...  69.9 us
    pallas_call x1, Pallas kernels, layer_back(): pl.pallas_call(functools.partial(back_kernel, col), out_shape=(sds(cot.sh...  67.2 us
    pallas_call x2, Pallas kernels, attn_bwd(): pl.pallas_call(functools.partial(attn_bwd_kernel, heads), out_shape=sds((...  64.8 us
    pallas_call x1, Pallas kernels, layer_turn(): pl.pallas_call(functools.partial(turn_kernel, col), out_shape=(sds(h.shap...  62.3 us
    pallas_call x1, Pallas kernels, layer_in(): pl.pallas_call(functools.partial(in_kernel, col), out_shape=project_shape...  41 us
    pallas_call x1, Pallas kernels, layer_last(): pl.pallas_call(functools.partial(last_kernel, col), out_shape=(sds(dh.sha...  27.5 us
  transfers between devices with their start and end apart: 2, of which 0 were waited for; matrix products, arithmetic and copies ran while one was open for 3% of the time, Pallas kernels for 23%

profile of v1, /device:TPU:0, one launch (start us, length us, event | category | flops | bytes accessed | tf_op | source)
XLA Modules:
  0.0 645.0 jit_solution(4456908929195983820)
XLA Ops:
  3.2 2.0 fusion.10.pos_ref
  5.4 76.1 %gather_weights.1 = (bf16[2,768,2560]{2,1,0:T(8,128)(2,1)S(1)}, f32[2,4,4,16,128]{4,3,2,1,0:T(8,128)S(1)}, f32[2048,384]{1,0:T(8,128)S(1)}) custom-call(bf16[192,2560]{1,0:T(8,128)(2,1)S(1)} %fusion.2.w_ref, f32[16,128]{1,0:T(8,128)S(1)} %pad_convert_fusion.sv_ref, s32[1,2048]{1,0:T(1,128)S(1)} %fusion.10.pos_ref, f32[8,128]{1,0:T(8,128)S(1)} %broadcast_in_dim.59.fr_ref), custom_call_target="tpu_custom_call" | custom-call | tf_op jit(solution)/shard_map/gather_weights/pallas_call | solution.py:469
  81.5 3.1 copy-done
  84.6 1.7 copy-done.1
  87.6 2.0 fusion.4
  92.0 3.0 dynamic-slice_bitcast_fusion
  95.0 41.0 %layer_in.1 = (bf16[2048,768]{1,0:T(8,128)(2,1)}, bf16[2048,768]{1,0:T(8,128)(2,1)}, bf16[2048,768]{1,0:T(8,128)(2,1)}, bf16[2048,256]{1,0:T(8,128)(2,1)}, bf16[...) custom-call(bf16[512,768]{1,0:T(8,128)(2,1)} %get-tuple-element.146.x_r, ...), custom_call_target="tpu_custom_call" | custom-call | tf_op jit(solution)/shard_map/layer_in/pallas_call | solution.py:707
  139.7 13.2 %attn_fwd.2 = (bf16[2048,256]{1,0:T(8,128)(2,1)S(1)}, f32[8,2048]{1,0:T(8,128)S(1)}) custom-call(s32[2,8]{1,0:T(2,128)S(1)} %pad_add_fusion.b_ref, bf16[2048,256]{1,0:T(8,128)(2,1)S(1)} %copy-done.4, bf16[2048,256]{1,0:T(8,128)(2,1)S(1)} %copy-done.6, bf16[2048,256]{1,0:T(8,128)(2,1)S(1)} %copy-done.8, s32[1,2048]{1,0:T(1,128)S(1)} %get-tuple-element.139.sr_ref, ...), custom_call_target="tpu_custom_call" | custom-call | tf_op jit(solution)/shard_map/attn_fwd/pallas_call | solution.py:124
  153.9 69.9 %layer_mid.1 = (bf16[512,768]{1,0:T(8,128)(2,1)}, bf16[2048,768]{1,0:T(8,128)(2,1)}, bf16[2048,768]{1,0:T(8,128)(2,1)}, bf16[2048,768]{1,0:T(8,128)(2,1)}, bf16[...) custom-call(bf16[2048,256]{1,0:T(8,128)(2,1)} %copy-done.3, ...), custom_call_target="tpu_custom_call" | custom-call | tf_op jit(solution)/shard_map/layer_mid/pallas_call | solution.py:746
  227.5 13.2 %attn_fwd.3 = (bf16[2048,256]{1,0:T(8,128)(2,1)S(1)}, f32[8,2048]{1,0:T(8,128)S(1)}) custom-call(s32[2,8]{1,0:T(2,128)S(1)} %pad_add_fusion.b_ref, bf16[2048,256]{1,0:T(8,128)(2,1)S(1)} %copy-done.10, bf16[2048,256]{1,0:T(8,128)(2,1)S(1)} %copy-done.12, bf16[2048,256]{1,0:T(8,128)(2,1)S(1)} %copy-done.14, s32[1,2048]{1,0:T(1,128)S(1)} %get-tuple-element.139.sr_ref, ...), custom_call_target="tpu_custom_call" | custom-call | tf_op jit(solution)/shard_map/attn_fwd/pallas_call | solution.py:124
  241.8 62.3 %layer_turn.1 = (bf16[512,768]{1,0:T(8,128)(2,1)}, bf16[2048,768]{1,0:T(8,128)(2,1)}, bf16[2048,256]{1,0:T(8,128)(2,1)}, bf16[2048,768]{1,0:T(8,128)(2,1)}, bf16[768,1792]{1,0:T(8,128)(2,1)}, /*index=5*/f32[8,768]{1,0:T(8,128)}) custom-call(bf16[2048,256]{1,0:T(8,128)(2,1)} %copy-done.16, bf16[2048,768]{1,0:T(8,128)(2,1)} %get-tuple-element.68.g, ...), custom_call_target="tpu_custom_call" | custom-call | tf_op jit(solution)/shard_map/layer_turn/pallas_call | solution.py:797
  307.7 32.5 %attn_bwd.2.dmix = bf16[2048,768]{1,0:T(8,128)(2,1)} custom-call(s32[2,8]{1,0:T(2,128)S(1)} %pad_add_fusion.b_ref, bf16[2048,256]{1,0:T(8,128)(2,1)S(1)} %copy-done.11, bf16[2048,256]{1,0:T(8,128)(2,1)S(1)} %copy-done.13, bf16[2048,256]{1,0:T(8,128)(2,1)S(1)} %copy-done.15, bf16[2048,256]{1,0:T(8,128)(2,1)} %copy-done.16, ...), custom_call_target="tpu_custom_call" | custom-call | tf_op jit(solution)/shard_map/attn_bwd/pallas_call | solution.py:216
  340.2 67.2 %layer_back.1 = (bf16[512,768]{1,0:T(8,128)(2,1)}, bf16[2048,768]{1,0:T(8,128)(2,1)}, bf16[768,768]{1,0:T(8,128)(2,1)}, f32[8,768]{1,0:T(8,128)}, bf16[2048,256]...) custom-call(bf16[2048,768]{1,0:T(8,128)(2,1)} %attn_bwd.2.dmix, ...), custom_call_target="tpu_custom_call" | custom-call | tf_op jit(solution)/shard_map/layer_back/pallas_call | solution.py:861
  411.1 32.3 %attn_bwd.3.dmix = bf16[2048,768]{1,0:T(8,128)(2,1)} custom-call(s32[2,8]{1,0:T(2,128)S(1)} %pad_add_fusion.b_ref, bf16[2048,256]{1,0:T(8,128)(2,1)S(1)} %copy-done.5, bf16[2048,256]{1,0:T(8,128)(2,1)S(1)} %copy-done.7, bf16[2048,256]{1,0:T(8,128)(2,1)S(1)} %copy-done.9, bf16[2048,256]{1,0:T(8,128)(2,1)} %copy-done.3, ...), custom_call_target="tpu_custom_call" | custom-call | tf_op jit(solution)/shard_map/attn_bwd/pallas_call | solution.py:216
  443.4 27.5 %layer_last.1 = (bf16[512,768]{1,0:T(8,128)(2,1)}, bf16[768,768]{1,0:T(8,128)(2,1)}, f32[8,768]{1,0:T(8,128)}) custom-call(bf16[2048,768]{1,0:T(8,128)(2,1)} %attn_bwd.3.dmix, bf16[2048,768]{1,0:T(8,128)(2,1)} %get-tuple-element.82.e2_in, bf16[512,768]{1,0:T(8,128)(2,1)} %get-tuple-element.83.dh, bf16[2048,768]{1,0:T(8,128)(2,1)} %get-tuple-element.77.xf, ...), custom_call_target="tpu_custom_call" | custom-call | tf_op jit(solution)/shard_map/layer_last/pallas_call | solution.py:911
  473.5 150.5 %reduce_grads.1 = (f32[192,2560]{1,0:T(8,128)}, f32[16,768]{1,0:T(8,128)}) custom-call(bf16[768,768]{1,0:T(8,128)(2,1)} %get-tuple-element.86.gq0, bf16[768,1792]{1,0:T(8,128)(2,1)} %get-tuple-element.87.gr0, bf16[768,768]{1,0:T(8,128)(2,1)} %get-tuple-element.88.gq1, bf16[768,1792]{1,0:T(8,128)(2,1)} %get-tuple-element.89.gr1, ...), custom_call_target="tpu_custom_call" | custom-call | tf_op jit(solution)/shard_map/reduce_grads/pallas_call | solution.py:1021
  624.0 2.5 slice_bitcast_fusion
  627.7 2.3 copy.50
  630.0 1.9 copy.51
  631.9 2.1 copy.55
  639.4 1.3 select_bitcast_fusion.1
  640.6 1.3 maximum_bitcast_fusion.1
  641.9 1.3 select_bitcast_fusion.3
  643.2 1.3 maximum_bitcast_fusion
  (125 shorter events, 31.7 us)
Async XLA Ops:
  0.7 1.6 copy-start.23
  0.7 1.7 copy-start.27
  0.7 1.7 copy-start.28
  0.7 1.7 copy-start.29
  0.7 1.7 copy-start.30
  0.7 1.7 copy-start.31
  0.7 1.7 copy-start.32
  0.7 1.8 copy-start.26
  0.7 1.8 copy-start.25
  0.7 1.8 copy-start.24
  0.8 4.4 copy-start.21
  0.8 4.4 copy-start.22
  2.3 84.1 %copy-start.34 = (s32[2,1]{0,1:T(1,128)S(1)}, s32[2,1]{0,1:T(1,128)}, u32[]{:S(2)}) copy-start(s32[2,1]{0,1:T(1,128)} %param.19) | copy-start | bytes 28
  81.5 3.1 copy-start
  84.6 1.7 copy-start.1
  92.0 131.8 %copy-start.2 = (s32[2048,1]{1,0:T(8,128)}, s32[2048,1]{1,0:T(8,128)S(1)}, u32[]{:S(2)}) copy-start(s32[2048,1]{1,0:T(8,128)S(1)} %fusion.1.kc_ref) | copy-start | bytes 24580
  136.0 1.2 copy-start.4
  443.4 27.5 %copy-start.18 = (bf16[512,768]{1,0:T(8,128)(2,1)S(1)}, bf16[512,768]{1,0:T(8,128)(2,1)}, u32[]{:S(2)}) copy-start(bf16[512,768]{1,0:T(8,128)(2,1)} %get-tuple-element.83.dh) | copy-start | bytes 2359300
  470.8 1.4 copy-start.17
  470.9 1.6 copy-start.19
  471.9 167.5 %collective-permute-start.1 = (bf16[512,768]{1,0:T(8,128)(2,1)}, bf16[512,768]{1,0:T(8,128)(2,1)}, u32[]{:S(2)}, u32[]{:S(2)}) collective-permute-start(bf16[512,768]{1,0:T(8,128)(2,1)} %broadcast_select_fusion), channel_id=1, source_target_pairs={{0,16},{16,0},{1,17},{17,1},{2,18},{18,2},{3,19},{19,3},{4,20},{20... | collective-permute-start | bytes 2359304 | tf_op jit(solution)/shard_map/ppermute | solution.py:1123
  473.5 168.4 %collective-permute-start = (bf16[512,768]{1,0:T(8,128)(2,1)}, bf16[512,768]{1,0:T(8,128)(2,1)}, u32[]{:S(2)}, u32[]{:S(2)}) collective-permute-start(bf16[512,768]{1,0:T(8,128)(2,1)} %broadcast_select_fusion.2), channel_id=1, source_target_pairs={{0,16},{16,0},{1,17},{17,1},{2,18},{18,2},{3,19},{19,3},{4,20},{20... | collective-permute-start | bytes 2359304 | tf_op jit(solution)/shard_map/ppermute | solution.py:1123
  627.7 11.6 %copy-start.20 = (bf16[512,768]{1,0:T(8,128)(2,1)S(1)}, bf16[512,768]{1,0:T(8,128)(2,1)}, u32[]{:S(2)}) copy-start(bf16[512,768]{1,0:T(8,128)(2,1)} %get-tuple-element.85) | copy-start | bytes 2359300
  639.3 5.1 copy-start.33
  (13 other events, 15.4 us)

commit v2 on v1

v2 whole, which is shorter than its diff:
```python
import functools

import jax
import jax.numpy as jnp
from jax import lax
from jax.experimental import pallas as pl
from jax.experimental.pallas import tpu as pltpu
from jax.sharding import PartitionSpec as P

F32 = jnp.float32
BF = jnp.bfloat16
MESH = pl.DeviceIdType.MESH
HD = 64
ROT = 16
LIVE = 128
QB = 256
HW = 256
SUB = 64
EPS = 1e-05
NEG = -1e30
VMEM = pl.BlockSpec(memory_space=pltpu.VMEM)
ANY = pl.BlockSpec(memory_space=pl.ANY)
SMEM = pl.BlockSpec(memory_space=pltpu.SMEM)
DMA = pltpu.SemaphoreType.DMA


def sds(shape, dtype):
    return jax.ShapeDtypeStruct(shape, dtype)


def dg(a, b, ca, cb):
    return lax.dot_general(a, b, (((ca,), (cb,)), ((), ())), preferred_element_type=F32)


def dot(a, b):
    return jnp.dot(a, b, preferred_element_type=F32)


def ds(start, size):
    return pl.ds(pl.multiple_of(start, size), size)


def norm_stats(x):
    mu = jnp.mean(x, axis=-1, keepdims=True)
    xc = x - mu
    var = jnp.mean(xc * xc, axis=-1, keepdims=True)
    return xc, lax.rsqrt(var + EPS)


def head_lanes(width, heads):
    lane = lax.broadcasted_iota(jnp.int32, (1, width), 1)
    return [(lane >= h * HD) & (lane < (h + 1) * HD) for h in range(heads)]


def allow_mask(kc, sq, diag):
    m = kc == sq
    if diag:
        r = lax.broadcasted_iota(jnp.int32, (QB, QB), 0)
        c = lax.broadcasted_iota(jnp.int32, (QB, QB), 1)
        m = (m & (r <= c)) | (r == c)
    return m


def attn_fwd_kernel(heads, b_ref, q_ref, k_ref, v_ref, sr_ref, kc_ref, o_ref, lse_ref, vt, s_scr):
    n = q_ref.shape[0] // QB
    width = q_ref.shape[1]
    hm = head_lanes(width, heads)

    def turn(i, _):
        vt[:, ds(i * QB, QB)] = v_ref[ds(i * QB, QB), :].T
        return 0

    lax.fori_loop(0, n, turn, 0)

    def qloop(i, _):
        qi = ds(i * QB, QB)
        q = q_ref[qi, :]
        qm = [jnp.where(hm[h], q, jnp.zeros_like(q)) for h in range(heads)]
        sq = sr_ref[0:1, qi]
        lo = b_ref[0, i]
        hi = b_ref[1, i]

        def scores(j, slot, ms, diag):
            kj = ds(j * QB, QB)
            k = k_ref[kj, :]
            mask = allow_mask(kc_ref[kj, 0:1], sq, diag)
            out = []
            for h in range(heads):
                s = jnp.where(mask, dg(k, qm[h], 1, 1), NEG)
                s_scr[h, ds(slot * QB, QB), :] = s
                out.append(jnp.maximum(ms[h], jnp.max(s, axis=0, keepdims=True)))
            return tuple(out)

        ms = tuple(jnp.full((1, QB), NEG, F32) for _ in range(heads))
        ms = scores(i, 0, ms, True)
        ms = lax.fori_loop(lo, hi, lambda j, ms: scores(j, j - lo + 1, ms, False), ms)

        def weigh(j, slot, st):
            kj = ds(j * QB, QB)
            out = []
            for h in range(heads):
                total, acc = st[h]
                p = jnp.exp(s_scr[h, ds(slot * QB, QB), :] - ms[h])
                total = total + jnp.sum(p, axis=0, keepdims=True)
                acc = acc + dot(vt[h * HD : (h + 1) * HD, kj], p.astype(BF))
                out.append((total, acc))
            return tuple(out)

        st = tuple((jnp.zeros((1, QB), F32), jnp.zeros((HD, QB), F32)) for _ in range(heads))
        st = weigh(i, 0, st)
        st = lax.fori_loop(lo, hi, lambda j, st: weigh(j, j - lo + 1, st), st)
        ot = [st[h][1] * (1.0 / st[h][0]) for h in range(heads)]
        ot = jnp.concatenate(ot + [jnp.zeros((width - heads * HD, QB), F32)], axis=0)
        o_ref[qi, :] = ot.T.astype(BF)
        lse = [ms[h] + jnp.log(st[h][0]) for h in range(heads)]
        lse_ref[:, qi] = jnp.concatenate(lse + [jnp.zeros((8 - heads, QB), F32)], axis=0)
        return 0

    lax.fori_loop(0, n, qloop, 0)


def attn_fwd(heads, bounds, q, k, v, sr, kc):
    rows, width = q.shape
    return pl.pallas_call(
        functools.partial(attn_fwd_kernel, heads),
        out_shape=(sds((rows, width), BF), sds((8, rows), F32)),
        in_specs=[SMEM] + [VMEM] * 5,
        out_specs=(VMEM, VMEM),
        scratch_shapes=[pltpu.VMEM((width, rows), BF), pltpu.VMEM((heads, rows + QB, QB), F32)],
        compiler_params=pltpu.CompilerParams(vmem_limit_bytes=40 << 20),
        cost_estimate=cost(15),
        name="attn_fwd",
    )(bounds, q, k, v, sr, kc)


def turn_lanes(x, tab, sign):
    width = x.shape[1]
    c, sn = [jnp.concatenate([tab[:, a * 128 : (a + 1) * 128]] * (width // 128), axis=1) for a in range(2)]
    lane = lax.broadcasted_iota(jnp.int32, (1, width), 1) % HD
    moved = jnp.where(lane < ROT // 2, pltpu.roll(x, width - ROT // 2, 1), pltpu.roll(x, ROT // 2, 1)) * sn
    return x * c + moved if sign > 0 else x * c - moved


def attn_bwd_kernel(
    heads, b_ref, q_ref, k_ref, v_ref, o_ref, do_ref, lse_ref, sr_ref, kc_ref, tab_ref, out_ref, kt, dk, dv
):
    rows, width = q_ref.shape
    n = rows // QB
    hm = head_lanes(width, heads)

    def turn(i, _):
        kt[:, ds(i * QB, QB)] = k_ref[ds(i * QB, QB), :].T
        return 0

    lax.fori_loop(0, n, turn, 0)
    dk[...] = jnp.zeros_like(dk)
    dv[...] = jnp.zeros_like(dv)
    rowid = lax.broadcasted_iota(jnp.int32, (8, width), 0)
    lane = lax.broadcasted_iota(jnp.int32, (8, width), 1)
    sel = ((lane >= rowid * HD) & (lane < (rowid + 1) * HD)).astype(F32).astype(BF)

    def qloop(i, _):
        qi = ds(i * QB, QB)
        q = q_ref[qi, :]
        do = do_ref[qi, :]
        z = jnp.zeros_like(q)
        qm = [jnp.where(hm[h], q, z) for h in range(heads)]
        dom = [jnp.where(hm[h], do, z) for h in range(heads)]
        qcat = jnp.concatenate(qm, axis=0)
        docat = jnp.concatenate(dom, axis=0)
        prod = do.astype(F32) * o_ref[qi, :].astype(F32)
        high = prod.astype(BF)
        low = (prod - high.astype(F32)).astype(BF)
        delta = dg(sel, high, 1, 1) + dg(sel, low, 1, 1)
        lse = lse_ref[:, qi]
        sq = sr_ref[0:1, qi]
        lo = b_ref[0, i]
        hi = b_ref[1, i]

        def step(j, dqs, diag):
            kj = ds(j * QB, QB)
            k = k_ref[kj, :]
            v = v_ref[kj, :]
            mask = allow_mask(kc_ref[kj, 0:1], sq, diag)
            ps, dss, out = [], [], []
            for h in range(heads):
                s = dg(k, qm[h], 1, 1)
                dp = dg(v, dom[h], 1, 1)
                p = jnp.where(mask, jnp.exp(jnp.where(mask, s - lse[h : h + 1, :], 0.0)), 0.0)
                score_grad = (p * (dp - delta[h : h + 1, :])).astype(BF)
                ps.append(p.astype(BF))
                dss.append(score_grad)
                out.append(dqs[h] + dot(kt[h * HD : (h + 1) * HD, kj], score_grad))
            dv[kj, :] += dot(jnp.concatenate(ps, axis=1), docat)
            dk[kj, :] += dot(jnp.concatenate(dss, axis=1), qcat)
            return tuple(out)

        dqs = tuple(jnp.zeros((HD, QB), F32) for _ in range(heads))
        dqs = step(i, dqs, True)
        dqs = lax.fori_loop(lo, hi, lambda j, d: step(j, d, False), dqs)
        dq = jnp.concatenate(list(dqs) + [jnp.zeros((width - heads * HD, QB), F32)], axis=0).T * 0.125
        out_ref[qi, 0:width] = turn_lanes(dq, tab_ref[qi, :], -1).astype(BF)
        return 0

    lax.fori_loop(0, n, qloop, 0)

    def finish(i, _):
        ii = ds(i * QB, QB)
        out_ref[ii, width : 2 * width] = turn_lanes(dk[ii, :], tab_ref[ii, :], -1).astype(BF)
        out_ref[ii, 2 * width : 3 * width] = dv[ii, :].astype(BF)
        return 0

    lax.fori_loop(0, n, finish, 0)


def attn_bwd(heads, bounds, q, k, v, o, do, lse, sr, kc, tab):
    rows, width = q.shape
    return pl.pallas_call(
        functools.partial(attn_bwd_kernel, heads),
        out_shape=sds((rows, 3 * width), BF),
        in_specs=[SMEM] + [VMEM] * 9,
        out_specs=VMEM,
        scratch_shapes=[
            pltpu.VMEM((width, rows), BF),
            pltpu.VMEM((rows, width), F32),
            pltpu.VMEM((rows, width), F32),
        ],
        compiler_params=pltpu.CompilerParams(vmem_limit_bytes=50 << 20),
        cost_estimate=cost(35),
        name="attn_bwd",
    )(bounds, q, k, v, o, do, lse, sr, kc, tab)


def places():
    t = lax.axis_index("tensor")
    x, y = t % 2, t // 2
    return t, 2 * y + (1 - x), 2 * (1 - y) + x, 3 - t


def greet(peers):
    bar = pltpu.get_barrier_semaphore()
    for peer in peers:
        pl.semaphore_signal(bar, inc=1, device_id=peer, device_id_type=MESH)
    pl.semaphore_wait(bar, len(peers))


def push(src, dst, ssem, rsem, peer):
    return pltpu.make_async_remote_copy(
        src_ref=src, dst_ref=dst, send_sem=ssem, recv_sem=rsem, device_id=peer, device_id_type=MESH
    )


def pick(i, values):
    out = values[-1]
    for n in range(len(values) - 2, -1, -1):
        out = jnp.where(i == n, values[n], out)
    return out


class Gather:
    def __init__(self, full, ssem, rsem):
        self.t, self.px, self.py, self.pd = places()
        self.full, self.ssem, self.rsem = full, ssem, rsem
        self.half = full.shape[0] // 8

    def rows(self, c, h):
        return ds((2 * c + h) * self.half, self.half)

    def copy(self, i, c, h, peer):
        ref = self.full.at[self.rows(c, h)]
        return push(ref, ref, self.ssem.at[i], self.rsem.at[i], {"tensor": peer})

    def plan(self, i):
        t, px, py = self.t, self.px, self.py
        c, h, peer = [(t, 0, px), (t, 1, py), (t, 1, px), (t, 0, py), (px, 0, py), (py, 1, px)][i]
        return self.copy(i, c, h, peer)

    def order(self, i):
        t, px, py, pd = self.t, self.px, self.py, self.pd
        return pick(i, [t, t, px, py, px, py, pd, pd]), pick(i, [0, 1, 0, 1, 1, 0, 0, 1])

    def arrive(self, i):
        @pl.when(i == 2)
        def _():
            self.plan(0).wait_recv()
            self.plan(4).start()
            self.plan(1).wait_recv()
            self.plan(5).start()

        for step in (4, 5, 6, 7):

            @pl.when(i == step)
            def _(step=step):
                self.plan(step - 2).wait_recv()

    def finish(self):
        for i in range(6):
            self.plan(i).wait_send()

    def run(self, work):
        def body(i, _):
            self.arrive(i)
            c, h = self.order(i)
            work((2 * c + h) * self.half, i)
            return 0

        lax.fori_loop(0, 8, body, 0)
        self.finish()


class Scatter:
    def __init__(self, part, r1x, r1y, r2x, r2y, ssem, rsem):
        self.t, self.px, self.py, self.pd = places()
        self.part, self.r1x, self.r1y, self.r2x, self.r2y = part, r1x, r1y, r2x, r2y
        self.ssem, self.rsem = ssem, rsem
        self.half = part.shape[0] // 8

    def rows(self, c, h):
        return ds((2 * c + h) * self.half, self.half)

    def copy(self, i, c, h, dst, peer):
        return push(self.part.at[self.rows(c, h)], dst, self.ssem.at[i], self.rsem.at[i], {"tensor": peer})

    def plan(self, i):
        px, py, pd = self.px, self.py, self.pd
        c, h, dst, peer = [
            (pd, 0, self.r1x.at[1], px),
            (pd, 1, self.r1y.at[1], py),
            (px, 0, self.r1x.at[0], px),
            (py, 1, self.r1y.at[0], py),
            (py, 0, self.r2y, py),
            (px, 1, self.r2x, px),
        ][i]
        return self.copy(i, c, h, dst, peer)

    def run(self, work, early=None):
        t, px, py, pd = self.t, self.px, self.py, self.pd

        def body(i, _):
            c = pick(i, [pd, pd, px, py, py, px, t, t])
            h = pick(i, [0, 1, 0, 1, 0, 1, 0, 1])
            work((2 * c + h) * self.half)
            for step in range(4):

                @pl.when(i == step)
                def _(step=step):
                    self.plan(step).start()

            return 0

        lax.fori_loop(0, 8, body, 0)
        if early is not None:
            early()
        for first, c, h, buf, second in ((0, py, 0, self.r1x, 4), (1, px, 1, self.r1y, 5)):
            self.plan(first).wait_recv()

            def add(i, _, c=c, h=h, buf=buf):
                rr = ds((2 * c + h) * self.half + i * SUB, SUB)
                got = buf[1, ds(i * SUB, SUB), :].astype(F32)
                self.part[rr, :] = (self.part[rr, :].astype(F32) + got).astype(BF)
                return 0

            lax.fori_loop(0, self.half // SUB, add, 0)
            self.plan(second).start()

    def arrive(self, h):
        for i in (2, 4) if h == 0 else (3, 5):
            self.plan(i).wait_recv()

    def total(self, h, i):
        near, far = (self.r1x, self.r2y) if h == 0 else (self.r1y, self.r2x)
        rr = ds((2 * self.t + h) * self.half + i * SUB, SUB)
        sub = ds(i * SUB, SUB)
        return self.part[rr, :].astype(F32) + near[0, sub, :].astype(F32) + far[sub, :].astype(F32)

    def finish(self):
        for i in range(6):
            self.plan(i).wait_send()


def scatter_scratch(rows, width):
    half = rows // 8
    return [
        pltpu.VMEM((rows, width), BF),
        pltpu.VMEM((2, half, width), BF),
        pltpu.VMEM((2, half, width), BF),
        pltpu.VMEM((half, width), BF),
        pltpu.VMEM((half, width), BF),
        DMA((6,)),
        DMA((6,)),
    ]


class Mesh:
    def __init__(self, dp, tensor):
        self.dp, self.tensor = dp, tensor
        self.s, self.z, self.t = lax.axis_index("section"), lax.axis_index("dp"), lax.axis_index("tensor")
        self.mate = {"section": 1 - self.s}
        self.ring = [{"dp": (self.z + d) % dp} for d in range(1, dp)]
        self.group = [{"tensor": (self.t + d) % tensor} for d in range(1, tensor)]


class WeightGather:
    def __init__(self, me, layer, shard, full, groups, sems):
        self.me, self.layer, self.shard, self.full, self.groups = me, layer, shard, full, groups
        self.own, self.wss, self.wrs, self.fss, self.frs = sems
        self.rows = shard.shape[0]

    def block(self, zz, g):
        a, b = self.groups[g]
        return self.full.at[ds(zz * self.rows, self.rows), a:b]

    def mine(self, g):
        a, b = self.groups[g]
        return self.shard.at[:, a:b]

    def local(self, g):
        return pltpu.make_async_copy(self.mine(g), self.block(self.me.z, g), self.own.at[g])

    def out(self, g, d):
        return push(self.mine(g), self.block(self.me.z, g), self.wss.at[g, d], self.wrs.at[g, d], self.me.ring[d])

    def hand(self, g, d):
        zz = (self.me.z + self.me.dp - d) % self.me.dp
        src = self.mine(g) if d == 0 else self.block(zz, g)
        return push(src, self.block(zz, g), self.fss.at[g, d], self.frs.at[g, d], self.me.mate)

    def send(self):
        @pl.when(self.me.s == self.layer)
        def _():
            for g in range(len(self.groups)):
                for d in range(self.me.dp - 1):
                    self.out(g, d).start()
                self.hand(g, 0).start()
                self.local(g).start()

    def wait(self, g):
        @pl.when(self.me.s == self.layer)
        def _():
            for d in range(self.me.dp - 1):
                self.out(g, d).wait_recv()
                self.hand(g, d + 1).start()
            self.local(g).wait()

        @pl.when(self.me.s != self.layer)
        def _():
            for d in range(self.me.dp):
                self.hand(g, d).wait_recv()

    def finish(self):
        @pl.when(self.me.s == self.layer)
        def _():
            for g in range(len(self.groups)):
                for d in range(self.me.dp - 1):
                    self.out(g, d).wait_send()
                for d in range(self.me.dp):
                    self.hand(g, d).wait_send()

    @staticmethod
    def scratch(dp, n):
        return [DMA((n,)), DMA((n, dp - 1)), DMA((n, dp - 1)), DMA((n, dp)), DMA((n, dp))]


class GradReduce:
    def __init__(self, me, layer, grad, got, sb, own, hand_sems, rb=None, ring_sems=None):
        self.me, self.layer, self.grad, self.got, self.sb, self.own = me, layer, grad, got, sb, own
        self.hss, self.hrs = hand_sems
        self.rb, self.ring_sems = rb, ring_sems
        self.rows = own.shape[0]

    def hand(self, src=None):
        return push(self.grad if src is None else src, self.got, self.hss, self.hrs, self.me.mate)

    def send(self, src=None):
        @pl.when(self.me.s != self.layer)
        def _():
            self.hand(src).start()

    def out(self, d):
        pss, prs = self.ring_sems
        return push(self.sb.at[d], self.rb.at[d], pss.at[d], prs.at[d], self.me.ring[d])

    def blocks(self, zz, write):
        def body(i, _):
            rr = ds(zz * self.rows + i * 16, 16)
            write(ds(i * 16, 16), self.grad[rr, :].astype(F32) + self.got[rr, :].astype(F32))
            return 0

        lax.fori_loop(0, self.rows // 16, body, 0)

    def reduce(self):
        @pl.when(self.me.s == self.layer)
        def _():
            self.hand().wait_recv()
            for d in range(self.me.dp - 1):

                def write(rr, value, d=d):
                    self.sb[d, rr, :] = value.astype(BF)

                self.blocks((self.me.z + d + 1) % self.me.dp, write)
                if self.rb is not None:
                    self.out(d).start()

            def write(rr, value):
                self.own[rr, :] = value

            self.blocks(self.me.z, write)

    def collect(self):
        @pl.when(self.me.s == self.layer)
        def _():
            for d in range(self.me.dp - 1):
                self.out(d).wait_recv()

                def add(i, _, d=d):
                    rr = ds(i * 16, 16)
                    self.own[rr, :] += self.rb[d, rr, :].astype(F32)
                    return 0

                lax.fori_loop(0, self.rows // 16, add, 0)
            for d in range(self.me.dp - 1):
                self.out(d).wait_send()

    def finish(self, src=None):
        @pl.when(self.me.s != self.layer)
        def _():
            self.hand(src).wait_send()


class VectorGather:
    def __init__(self, me, sv, buf, ss, rs, own):
        self.me, self.sv, self.buf, self.ss, self.rs, self.own = me, sv, buf, ss, rs, own

    def local(self):
        me = self.me
        return pltpu.make_async_copy(self.sv, self.buf.at[me.s, me.t, me.z], self.own)

    def stage(self, n):
        me = self.me
        if n == 0:
            dst = self.buf.at[me.s, me.t, me.z]
            return [push(self.sv, dst, self.ss.at[d], self.rs.at[d], peer) for d, peer in enumerate(me.ring)]
        base = me.dp - 1
        if n == 1:
            ref = self.buf.at[me.s, me.t]
            return [
                push(ref, ref, self.ss.at[base + d], self.rs.at[base + d], peer) for d, peer in enumerate(me.group)
            ]
        i = base + me.tensor - 1
        ref = self.buf.at[me.s]
        return [push(ref, ref, self.ss.at[i], self.rs.at[i], me.mate)]

    def send(self, n):
        if n == 0:
            self.local().start()
        for c in self.stage(n):
            c.start()

    def wait(self, n):
        if n == 0:
            self.local().wait()
        for c in self.stage(n):
            c.wait_recv()

    def finish(self):
        for n in range(3):
            for c in self.stage(n):
                c.wait_send()

    def build(self, vecs, heads, own, qw, fw):
        me, buf = self.me, self.buf
        for layer in range(2):
            wide = [buf[layer, tt, zz, 0:8, :][:, 0:own] for zz in range(me.dp) for tt in range(me.tensor)]
            vecs[layer, 0:8, :] = jnp.concatenate(wide, axis=1)
            here = [buf[layer, me.t, zz] for zz in range(me.dp)]
            by = [jnp.concatenate([p[6 + h : 7 + h, 0:qw] for p in here], axis=1) for h in range(heads)]
            qb = []
            for part in range(3):
                qb += [b[:, part * HD : (part + 1) * HD] for b in by] + [jnp.zeros((1, HW - heads * HD), F32)]
            vecs[layer, 6:7, :] = jnp.concatenate(qb, axis=1)
            fb = [p[6 + heads + h : 7 + heads + h, 0:fw] for h in range(heads) for p in here]
            vecs[layer, 7:8, :] = jnp.concatenate(fb, axis=1)


class VectorReduce:
    def __init__(self, me, va, vr, ss, rs):
        self.me, self.va, self.vr, self.ss, self.rs = me, va, vr, ss, rs

    def stage(self, n):
        me, va, vr, ss, rs = self.me, self.va, self.vr, self.ss, self.rs
        peers, base = [([me.mate], 0), (me.ring, 1), (me.group, me.dp)][n]
        return [push(va.at[n], vr.at[base + d], ss.at[base + d], rs.at[base + d], p) for d, p in enumerate(peers)]

    def send(self, n):
        for c in self.stage(n):
            c.start()

    def add(self, n, out):
        base = [0, 1, self.me.dp][n]
        total = jnp.zeros(self.va.shape[1:], F32)
        for d, c in enumerate(self.stage(n)):
            c.wait_recv()
            total = total + self.vr[base + d]
        if n == 2:
            row = lax.broadcasted_iota(jnp.int32, total.shape, 0)
            total = jnp.where(row % 8 < 6, total, 0.0)
        out[...] = self.va[n] + total

    def finish(self):
        for n in range(3):
            for c in self.stage(n):
                c.wait_send()


def rotary_table(pos_ref, fr_ref, tab):
    ang = fr_ref[:, 0:1] * pos_ref[...].astype(F32)
    cs, sn = jnp.cos(ang), jnp.sin(ang)
    one = jnp.ones((HD - ROT, ang.shape[1]), F32)
    tab[:, 0:128] = jnp.concatenate([cs, cs, one] * 2, axis=0).T
    tab[:, 128:256] = jnp.concatenate([-sn, sn, jnp.zeros_like(one)] * 2, axis=0).T


QKV, FC1, FC2, OUT = 0, 1, 2, 3


def columns(model, ff):
    return {"qkv": 0, "fc1": 3 * HW, "fc2": 3 * HW + ff, "out": 3 * HW + 2 * ff, "end": 3 * HW + 2 * ff + HW}


def project_qkv(r0, half, hf, wqkv, vec, tab, n1, n2, q, k, v):
    rows = ds(r0, half)

    def norm(i, _):
        rr = ds(r0 + i * SUB, SUB)
        xc, r = norm_stats(hf[rr, :].astype(F32))
        xh = xc * r
        n1[rr, :] = (xh * vec[0:1, :] + vec[1:2, :]).astype(BF)
        n2[rr, :] = (xh * vec[3:4, :] + vec[4:5, :]).astype(BF)
        return 0

    lax.fori_loop(0, half // SUB, norm, 0)
    a = n1[rows, :]
    for part, dst in enumerate((q, k, v)):
        cols = slice(part * HW, (part + 1) * HW)
        y = dot(a, wqkv[:, cols]) + vec[6:7, cols]
        if part < 2:
            y = turn_lanes(y, tab[rows, :], 1)
        if part == 0:
            y = y * 0.125
        dst[rows, :] = y.astype(BF)


def project_fc1(r0, half, wfc1, vec, n2, g, gp):
    rows = ds(r0, half)
    a = n2[rows, :]
    for b in range(wfc1.shape[1] // 256):
        cols = slice(b * 256, (b + 1) * 256)
        y = dot(a, wfc1[:, cols]) + vec[7:8, cols]
        cdf = 0.5 + 0.5 * lax.erf(y * 0.7071067811865476)
        g[rows, cols] = (y * cdf).astype(BF)
        gp[rows, cols] = (cdf + y * jnp.exp(-0.5 * y * y) * 0.3989422804014327).astype(BF)


def branch_out(r0, half, o, g, wout, wfc2, part):
    rows = ds(r0, half)
    for b in range(part.shape[1] // 256):
        cols = slice(b * 256, (b + 1) * 256)
        y = dg(o[rows, :], wout[cols, :], 1, 1) + dg(g[rows, :], wfc2[cols, :], 1, 1)
        part[rows, cols] = y.astype(BF)


def back_head(r0, half, dyf, hf, g, gp, n2, o, wfc1, wfc2, wout, vec, do, e2, da, acc, vg):
    rows = ds(r0, half)
    model, ff = wfc1.shape
    dy = dyf[rows, :]
    for b in range(ff // 256):
        cols = slice(b * 256, (b + 1) * 256)
        y = dot(dy, wfc2[:, cols]) * gp[rows, cols].astype(F32)
        low = y.astype(BF)
        da[:, cols] = low
        vg[7:8, cols] += jnp.sum(low.astype(F32), axis=0, keepdims=True)
    do[rows, :] = dot(dy, wout[...]).astype(BF)
    xc, r = norm_stats(hf[rows, :].astype(F32))
    xh = xc * r
    for b in range(model // 256):
        cols = slice(b * 256, (b + 1) * 256)
        dn = dg(da[...], wfc1[cols, :], 1, 1)
        vg[3:4, cols] += jnp.sum(dn * xh[:, cols], axis=0, keepdims=True)
        vg[4:5, cols] += jnp.sum(dn, axis=0, keepdims=True)
        e2[rows, cols] = (dn * vec[3:4, cols]).astype(BF)
    n2t = n2[rows, :].T
    dyt = dy.T
    for b in range(ff // 256):
        cols = slice(b * 256, (b + 1) * 256)
        acc[:, cols] += dot(n2t, da[:, cols])
        acc[:, ff + b * 256 : ff + (b + 1) * 256] += dot(dyt, g[rows, cols])
    acc[:, 2 * ff :] += dot(dyt, o[rows, :])


def back_tail(r0, half, dmix, hf, e2, wqkv, vec, part, vg):
    rows = ds(r0, half)
    dm = dmix[rows, :]
    vg[6:7, :] += jnp.sum(dm.astype(F32), axis=0, keepdims=True)
    xc, r = norm_stats(hf[rows, :].astype(F32))
    xh = xc * r
    for b in range(part.shape[1] // 256):
        cols = slice(b * 256, (b + 1) * 256)
        dn = dg(dm, wqkv[cols, :], 1, 1)
        vg[0:1, cols] += jnp.sum(dn * xh[:, cols], axis=0, keepdims=True)
        vg[1:2, cols] += jnp.sum(dn, axis=0, keepdims=True)
        part[rows, cols] = (dn * vec[0:1, cols] + e2[rows, cols].astype(F32)).astype(BF)


def qkv_grad(n1, dmix, acc, half):
    acc[...] = jnp.zeros_like(acc)

    def body(i, _):
        rows = ds(i * half, half)
        n1t = n1[rows, :].T
        for b in range(3):
            cols = slice(b * HW, (b + 1) * HW)
            acc[:, cols] += dot(n1t, dmix[rows, cols])
        return 0

    lax.fori_loop(0, n1.shape[0] // half, body, 0)


def store_low(acc, out):
    def body(i, _):
        rr = ds(i * SUB, SUB)
        out[rr, :] = acc[rr, :].astype(BF)
        return 0

    lax.fori_loop(0, acc.shape[0] // SUB, body, 0)


def residual_out(sc, own, off, vec, dst, dst2=None, dst2_off=None, after=None):
    for h in range(2):
        sc.arrive(h)

        def body(i, _, h=h):
            rr = ds(h * sc.half + i * SUB, SUB)
            base = own[ds(off + h * sc.half + i * SUB, SUB), :].astype(F32)
            y = (base + sc.total(h, i) + vec[2:3, :] + vec[5:6, :]).astype(BF)
            dst[rr, :] = y
            if dst2 is not None:
                dst2[ds(dst2_off + h * sc.half + i * SUB, SUB), :] = y
            return 0

        lax.fori_loop(0, sc.half // SUB, body, 0)
        if after is not None:
            after(h)


def grad_out(sc, dy, dy_off, hf, vec, dst, dst2=None, dst2_off=None, after=None):
    base = sc.t * 2 * sc.half
    for h in range(2):
        sc.arrive(h)

        def body(i, _, h=h):
            off = h * sc.half + i * SUB
            xc, r = norm_stats(hf[ds(base + off, SUB), :].astype(F32))
            xh = xc * r
            e = sc.total(h, i)
            m1 = jnp.mean(e, axis=-1, keepdims=True)
            m2 = jnp.mean(e * xh, axis=-1, keepdims=True)
            du = dy[ds(dy_off + off, SUB), :].astype(F32) + r * (e - m1 - xh * m2)
            low = du.astype(BF)
            dst[ds(off, SUB), :] = low
            if dst2 is not None:
                dst2[ds(dst2_off + off, SUB), :] = low
            return 0

        lax.fori_loop(0, sc.half // SUB, body, 0)
        if after is not None:
            after(h)


def start_half(ga, h):
    for i in (0, 3) if h == 0 else (1, 2):
        ga.plan(i).start()


def column_sum(ref, off, count, vg, row):
    def body(i, acc):
        return acc + jnp.sum(ref[ds(off + i * SUB, SUB), :].astype(F32), axis=0, keepdims=True)

    vg[row : row + 1, :] = lax.fori_loop(0, count // SUB, body, jnp.zeros((1, ref.shape[1]), F32))


def load(pairs, sem):
    copies = [pltpu.make_async_copy(a, b, sem.at[i]) for i, (a, b) in enumerate(pairs)]
    for c in copies:
        c.start()
    return copies


def params(cid, mib=58):
    return pltpu.CompilerParams(collective_id=cid, has_side_effects=True, vmem_limit_bytes=mib << 20)


def cost(us):
    return pl.CostEstimate(flops=int(us * 8e8), bytes_accessed=0, transcendentals=0)


def neighbours():
    t, px, py, pd = places()
    return [{"tensor": px}, {"tensor": py}]


class Stores:
    def __init__(self, pairs, half, sem):
        self.pairs, self.half, self.sem = pairs, half, sem

    def copy(self, n, r0, i):
        src, dst = self.pairs[n]
        rows = ds(r0, self.half)
        return pltpu.make_async_copy(src.at[rows], dst.at[rows], self.sem.at[n, i])

    def start(self, which, r0, i):
        for n in which:
            self.copy(n, r0, i).start()

    def finish(self):
        def body(i, _):
            for n in range(len(self.pairs)):
                self.copy(n, i * self.half, i).wait()
            return 0

        lax.fori_loop(0, 8, body, 0)


def in_kernel(
    cfg, x_ref, w_ref, sv_ref, pos_ref, fr_ref, hf_o, n1_o, n2_o, g_o, gp_o, tab_o, w_o, vecs, q, k, v,
    hf, n1, n2, g, gp, tab, wfull, vb, gss, grs, lsem, ssem, vss, vrs, *wsems,
):
    col, dp, tensor = cfg["col"], cfg["dp"], cfg["tensor"]
    me = Mesh(dp, tensor)
    greet([me.mate] + me.ring + me.group)
    ga = Gather(hf, gss, grs)
    wg = WeightGather(me, 0, w_ref, wfull, cfg["groups"], wsems)
    vg = VectorGather(me, sv_ref, vb, vss, vrs, lsem.at[1])
    st = Stores([(hf, hf_o), (n1, n1_o), (n2, n2_o), (g, g_o), (gp, gp_o)], ga.half, ssem)
    mine = pltpu.make_async_copy(x_ref, hf.at[ds(ga.t * 2 * ga.half, 2 * ga.half)], lsem.at[0])
    mine.start()
    vg.send(0)
    wg.send()
    mine.wait()
    start_half(ga, 0)
    start_half(ga, 1)
    vg.wait(0)
    vg.send(1)
    rotary_table(pos_ref, fr_ref, tab)
    vg.wait(1)
    vg.send(2)
    tab_out = pltpu.make_async_copy(tab, tab_o, lsem.at[2])
    tab_out.start()
    vg.wait(2)
    vg.build(vecs, cfg["heads"], cfg["own"], cfg["qw"], cfg["fw"])
    vec = vecs.at[0]
    wg.wait(0)

    def fc1(i):
        c, h = ga.order(i)
        r0 = (2 * c + h) * ga.half
        project_fc1(r0, ga.half, wfull.at[:, col["fc1"] : col["fc2"]], vec, n2, g, gp)
        st.start((3, 4), r0, i)

    def work(r0, i):
        project_qkv(r0, ga.half, hf, wfull.at[:, 0 : col["fc1"]], vec, tab, n1, n2, q, k, v)
        st.start((0, 1, 2), r0, i)

        @pl.when(i == 4)
        def _():
            wg.wait(1)

        @pl.when(i >= 4)
        def _():
            fc1(i - 4)

    ga.run(work)

    def late(i, _):
        fc1(i)
        return 0

    lax.fori_loop(4, 8, late, 0)
    wg.wait(2)
    w_out = pltpu.make_async_copy(wfull, w_o, lsem.at[3])
    w_out.start()
    st.finish()
    tab_out.wait()
    wg.finish()
    vg.finish()
    w_out.wait()


def layer_in(cfg, x, w, sv, pos, fr):
    seq, model, ff = pos.shape[1], x.shape[1], cfg["ff"]
    dp, tensor = cfg["dp"], cfg["tensor"]
    rows = sds((seq, model), BF)
    heads = sds((seq, HW), BF)
    nv = dp - 1 + tensor
    wide = pltpu.VMEM((seq, model), BF)
    return pl.pallas_call(
        functools.partial(in_kernel, cfg),
        out_shape=(rows, rows, rows, sds((seq, ff), BF), sds((seq, ff), BF), sds((seq, 256), F32),
                   sds((model, w.shape[1]), BF), sds((2, 8, model), F32), heads, heads, heads),
        in_specs=[VMEM] * 5,
        out_specs=(ANY,) * 7 + (VMEM,) * 4,
        scratch_shapes=[
            wide, wide, wide, pltpu.VMEM((seq, ff), BF), pltpu.VMEM((seq, ff), BF), pltpu.VMEM((seq, 256), F32),
            pltpu.VMEM((model, w.shape[1]), BF), pltpu.VMEM((2, tensor, dp) + sv.shape, F32),
            DMA((6,)), DMA((6,)), DMA((4,)), DMA((5, 8)), DMA((nv,)), DMA((nv,)),
        ]
        + WeightGather.scratch(dp, 3),
        compiler_params=params(2),
        cost_estimate=cost(38),
        name="layer_in",
    )(x, w, sv, pos, fr)


def mid_kernel(
    cfg, o, g_in, x_ref, w_ref, w0, vecs, tab_in, h_ref, hf_o, n1_o, n2_o, g_o, gp_o, w_o, q, k, v,
    wout, wfc2, hf, n1, n2, g, gp, tab, wfull, part, r1x, r1y, r2x, r2y, sss, srs, gss, grs, lsem, ssem, *wsems,
):
    col = cfg["col"]
    me = Mesh(cfg["dp"], cfg["tensor"])
    loads = load(
        [
            (w0.at[:, col["out"] : col["end"]], wout),
            (w0.at[:, col["fc2"] : col["out"]], wfc2),
            (g_in, g),
            (tab_in, tab),
        ],
        lsem,
    )
    greet([me.mate] + me.ring + neighbours())
    wg = WeightGather(me, 1, w_ref, wfull, cfg["groups"], wsems)
    wg.send()
    for c in loads:
        c.wait()
    sc = Scatter(part, r1x, r1y, r2x, r2y, sss, srs)
    ga = Gather(hf, gss, grs)
    st = Stores([(hf, hf_o), (n1, n1_o), (n2, n2_o), (g, g_o), (gp, gp_o)], ga.half, ssem)
    sc.run(lambda r0: branch_out(r0, sc.half, o, g, wout, wfc2, part))
    wg.wait(0)
    residual_out(sc, x_ref, 0, vecs.at[0], h_ref, hf, sc.t * 2 * sc.half, lambda h: start_half(ga, h))
    wg.wait(1)
    vec = vecs.at[1]

    def work(r0, i):
        project_qkv(r0, ga.half, hf, wfull.at[:, 0 : col["fc1"]], vec, tab, n1, n2, q, k, v)
        project_fc1(r0, ga.half, wfull.at[:, col["fc1"] : col["fc2"]], vec, n2, g, gp)
        st.start(range(5), r0, i)

    ga.run(work)
    wg.wait(2)
    w_out = pltpu.make_async_copy(wfull, w_o, lsem.at[0])
    w_out.start()
    sc.finish()
    wg.finish()
    st.finish()
    w_out.wait()


def layer_mid(cfg, o, g, x, w, w0, vecs, tab):
    seq, model, ff = tab.shape[0], x.shape[1], cfg["ff"]
    rows = sds((seq, model), BF)
    heads = sds((seq, HW), BF)
    wide = pltpu.VMEM((seq, model), BF)
    return pl.pallas_call(
        functools.partial(mid_kernel, cfg),
        out_shape=(sds(x.shape, BF), rows, rows, rows, sds((seq, ff), BF), sds((seq, ff), BF), sds(w0.shape, BF),
                   heads, heads, heads),
        in_specs=[VMEM, ANY, VMEM, VMEM, ANY, VMEM, ANY],
        out_specs=(VMEM,) + (ANY,) * 6 + (VMEM,) * 3,
        scratch_shapes=[
            pltpu.VMEM((model, HW), BF), pltpu.VMEM((model, ff), BF),
            wide, wide, wide, pltpu.VMEM((seq, ff), BF), pltpu.VMEM((seq, ff), BF), pltpu.VMEM((seq, 256), F32),
            pltpu.VMEM(w0.shape, BF),
        ]
        + scatter_scratch(seq, model)
        + [DMA((6,)), DMA((6,)), DMA((4,)), DMA((5, 8))]
        + WeightGather.scratch(cfg["dp"], 3),
        compiler_params=params(3),
        cost_estimate=cost(65),
        name="layer_mid",
    )(o, g, x, w, w0, vecs, tab)


def turn_kernel(
    cfg, o, g_in, h_ref, hf_in, cot, cx, cy, cd0, cd1, w1, vecs, n2_in, gp_in, y_ref, do, e2_o, gr, vg,
    g, hf, dyf, n2, gp, e2, wout, wfc2, wfc1, da, acc, part, r1x, r1y, r2x, r2y, sss, srs, lsem, ssem,
):
    col = cfg["col"]
    t, px, py, pd = places()
    sc = Scatter(part, r1x, r1y, r2x, r2y, sss, srs)
    half = sc.half

    def rows(c, h, n):
        return dyf.at[ds((2 * c + h) * half, n * half)]

    loads = load(
        [
            (w1.at[:, col["out"] : col["end"]], wout),
            (w1.at[:, col["fc2"] : col["out"]], wfc2),
            (g_in, g),
            (w1.at[:, col["fc1"] : col["fc2"]], wfc1),
            (cot, rows(t, 0, 2)),
            (cx, rows(px, 0, 2)),
            (cy, rows(py, 0, 2)),
            (cd0, rows(pd, 0, 1)),
            (cd1, rows(pd, 1, 1)),
            (gp_in, gp),
            (hf_in, hf),
            (n2_in, n2),
        ],
        lsem,
    )
    greet(neighbours())
    for c in loads[:3]:
        c.wait()
    vec = vecs.at[1]
    st = Stores([(e2, e2_o)], half, ssem)

    def early():
        vg[...] = jnp.zeros_like(vg)
        acc[...] = jnp.zeros_like(acc)
        for c in loads[3:]:
            c.wait()

        def body(i, _):
            r0 = i * half
            back_head(r0, half, dyf, hf, g, gp, n2, o, wfc1, wfc2, wout, vec, do, e2, da, acc, vg)
            st.start((0,), r0, i)
            return 0

        lax.fori_loop(0, 4, body, 0)

    def rest():
        def body(i, _):
            r0 = i * half
            back_head(r0, half, dyf, hf, g, gp, n2, o, wfc1, wfc2, wout, vec, do, e2, da, acc, vg)
            st.start((0,), r0, i)
            return 0

        lax.fori_loop(4, 8, body, 0)
        column_sum(cot_rows, 0, 2 * half, vg, 2)
        store_low(acc, gr)

    cot_rows = dyf.at[ds(2 * t * half, 2 * half)]
    sc.run(lambda r0: branch_out(r0, half, o, g, wout, wfc2, part), early)
    rest()
    residual_out(sc, h_ref, 0, vec, y_ref)
    sc.finish()
    st.finish()


def layer_turn(cfg, o, g, h, hf, cots, w1, vecs, n2, gp):
    seq, model = hf.shape
    ff = cfg["ff"]
    wide, hidden = pltpu.VMEM((seq, model), BF), pltpu.VMEM((seq, ff), BF)
    return pl.pallas_call(
        functools.partial(turn_kernel, cfg),
        out_shape=(
            sds(h.shape, BF),
            sds((seq, HW), BF),
            sds((seq, model), BF),
            sds((model, 2 * ff + HW), BF),
            sds((8, model), F32),
        ),
        in_specs=[VMEM, ANY, VMEM, ANY] + [ANY] * 5 + [ANY, VMEM, ANY, ANY],
        out_specs=(VMEM, VMEM, ANY, VMEM, VMEM),
        scratch_shapes=[
            hidden, wide, wide, wide, hidden, wide,
            pltpu.VMEM((model, HW), BF), pltpu.VMEM((model, ff), BF), pltpu.VMEM((model, ff), BF),
            pltpu.VMEM((seq // 8, ff), BF), pltpu.VMEM((model, 2 * ff + HW), F32),
        ]
        + scatter_scratch(seq, model)
        + [DMA((12,)), DMA((1, 8))],
        compiler_params=params(4, 63),
        cost_estimate=cost(40),
        name="layer_turn",
    )(o, g, h, hf, *cots, w1, vecs, n2, gp)


def back_kernel(
    cfg, dmix, e2_in, cot, hf_in, n1_in, w1, w0, vecs, xf_in, g_in, gp_in, n2_in, o, gr1,
    dh_ref, e2_o, do, vgf, vgd, out1, sba, owna, sbb, ownb,
    a, b, e2, g, gp, wqkv, wout, wfc2, wfc1, dhf, da, acc, gq, gr, got, gotq, sb, rb,
    part, r1x, r1y, r2x, r2y, sss, srs, gss, grs, lsem, ssem, hss, hrs, pss, prs,
):
    col = cfg["col"]
    me = Mesh(cfg["dp"], cfg["tensor"])
    loads = load(
        [
            (w1.at[:, col["qkv"] : col["fc1"]], wqkv),
            (hf_in, a),
            (e2_in, e2),
            (n1_in, b),
            (gr1, gr),
            (w0.at[:, col["out"] : col["end"]], wout),
            (w0.at[:, col["fc2"] : col["out"]], wfc2),
            (w0.at[:, col["fc1"] : col["fc2"]], wfc1),
            (g_in, g),
            (gp_in, gp),
        ],
        lsem,
    )
    greet([me.mate] + me.ring + neighbours())
    ga = Gather(dhf, gss, grs)
    sc = Scatter(part, r1x, r1y, r2x, r2y, sss, srs)
    red1 = GradReduce(me, 1, gr, got, sb, out1, (hss.at[0], hrs.at[0]), rb, (pss, prs))
    redq = GradReduce(me, 1, gq, gotq, sbb, ownb, (hss.at[1], hrs.at[1]))
    red0 = GradReduce(me, 0, gr, got, sba, owna, (hss.at[2], hrs.at[2]))
    st = Stores([(e2, e2_o)], ga.half, ssem)
    red1.send(gr1)
    vgf[...] = jnp.zeros_like(vgf)
    vgd[...] = jnp.zeros_like(vgd)
    for c in loads[:3]:
        c.wait()

    def early():
        loads[3].wait()
        small = acc.at[:, 0 : 3 * HW]
        qkv_grad(b, dmix, small, sc.half)
        store_low(small, gq)
        redq.send()
        loads[4].wait()
        red1.reduce()

    sc.run(lambda r0: back_tail(r0, sc.half, dmix, a, e2, wqkv, vecs.at[1], part, vgf), early)
    acc[...] = jnp.zeros_like(acc)
    again = pltpu.make_async_copy(n2_in, b, lsem.at[10])
    again.start()
    grad_out(sc, cot, 0, a, vecs.at[1], dh_ref, dhf, sc.t * 2 * sc.half, lambda h: start_half(ga, h))
    other = pltpu.make_async_copy(xf_in, a, lsem.at[11])
    other.start()
    for c in loads[5:]:
        c.wait()
    redq.reduce()
    again.wait()
    other.wait()

    def work(r0, i):
        back_head(r0, ga.half, dhf, a, g, gp, b, o, wfc1, wfc2, wout, vecs.at[0], do, e2, da, acc, vgd)
        st.start((0,), r0, i)

    ga.run(work)
    red1.collect()
    red1.finish(gr1)
    store_low(acc, gr)
    red0.send()
    column_sum(dh_ref, 0, dh_ref.shape[0], vgd, 2)
    red0.reduce()
    sc.finish()
    st.finish()
    redq.finish()
    red0.finish()


def layer_back(cfg, dmix, e2, cot, hf, n1, w1, w0, vecs, xf, g, gp, n2, o, gr1):
    seq, model = hf.shape
    ff, dp = cfg["ff"], cfg["dp"]
    rows, nr, nq = model // dp, 2 * ff + HW, 3 * HW
    wide, hidden = pltpu.VMEM((seq, model), BF), pltpu.VMEM((seq, ff), BF)
    return pl.pallas_call(
        functools.partial(back_kernel, cfg),
        out_shape=(
            sds(cot.shape, BF),
            sds((seq, model), BF),
            sds((seq, HW), BF),
            sds((8, model), F32),
            sds((8, model), F32),
            sds((rows, nr), F32),
            sds((dp - 1, rows, nr), BF),
            sds((rows, nr), F32),
            sds((dp - 1, rows, nq), BF),
            sds((rows, nq), F32),
        ),
        in_specs=[VMEM, ANY, VMEM, ANY, ANY, ANY, ANY, VMEM, ANY, ANY, ANY, ANY, VMEM, ANY],
        out_specs=(VMEM, ANY) + (VMEM,) * 8,
        scratch_shapes=[
            wide, wide, wide, hidden, hidden,
            pltpu.VMEM((model, nq), BF), pltpu.VMEM((model, HW), BF), pltpu.VMEM((model, ff), BF),
            pltpu.VMEM((model, ff), BF), wide, pltpu.VMEM((seq // 8, ff), BF), pltpu.VMEM((model, nr), F32),
            pltpu.VMEM((model, nq), BF), pltpu.VMEM((model, nr), BF), pltpu.VMEM((model, nr), BF),
            pltpu.VMEM((model, nq), BF), pltpu.VMEM((dp - 1, rows, nr), BF), pltpu.VMEM((dp - 1, rows, nr), BF),
        ]
        + scatter_scratch(seq, model)
        + [DMA((6,)), DMA((6,)), DMA((12,)), DMA((1, 8)), DMA((3,)), DMA((3,)), DMA((dp - 1,)), DMA((dp - 1,))],
        compiler_params=pltpu.CompilerParams(collective_id=5, has_side_effects=True, vmem_limit_bytes=67043328),
        cost_estimate=cost(65),
        name="layer_back",
    )(dmix, e2, cot, hf, n1, w1, w0, vecs, xf, g, gp, n2, o, gr1)


def last_kernel(
    cfg, dmix, e2_in, dh, xf_in, n1_in, w0, vecs, vf1, vd1, vd0, dx_ref, gqo, vout,
    xf, n1, e2, wqkv, acc, gq, got, sb, rb, vgf, va, vr,
    part, r1x, r1y, r2x, r2y, sss, srs, lsem, hss, hrs, pss, prs, vss, vrs,
):
    col = cfg["col"]
    me = Mesh(cfg["dp"], cfg["tensor"])
    loads = load([(w0.at[:, col["qkv"] : col["fc1"]], wqkv), (xf_in, xf), (e2_in, e2), (n1_in, n1)], lsem)
    greet([me.mate] + me.ring + me.group)
    sc = Scatter(part, r1x, r1y, r2x, r2y, sss, srs)
    red = GradReduce(me, 0, gq, got, sb, gqo, (hss.at[0], hrs.at[0]), rb, (pss, prs))
    vr_ = VectorReduce(me, va, vr, vss, vrs)
    vgf[...] = jnp.zeros_like(vgf)
    for c in loads[:3]:
        c.wait()

    def early():
        va[0, 0:8, :] = vgf[...] + vd0[...]
        va[0, 8:16, :] = vf1[...] + vd1[...]
        loads[3].wait()
        qkv_grad(n1, dmix, acc, sc.half)
        store_low(acc, gq)
        red.send()
        vr_.send(0)
        red.reduce()
        vr_.add(0, va.at[1])

    sc.run(lambda r0: back_tail(r0, sc.half, dmix, xf, e2, wqkv, vecs.at[0], part, vgf), early)
    vr_.send(1)
    red.finish()
    vr_.add(1, va.at[2])
    vr_.send(2)
    grad_out(sc, dh, 0, xf, vecs.at[0], dx_ref)
    red.collect()
    vr_.add(2, vout)
    vr_.finish()
    sc.finish()


def layer_last(cfg, dmix, e2, dh, xf, n1, w0, vecs, vf1, vd1, vd0):
    seq, model = xf.shape
    dp, tensor = cfg["dp"], cfg["tensor"]
    rows, nq = model // dp, 3 * HW
    nv = dp + tensor - 1
    wide = pltpu.VMEM((seq, model), BF)
    return pl.pallas_call(
        functools.partial(last_kernel, cfg),
        out_shape=(sds(dh.shape, BF), sds((rows, nq), F32), sds((16, model), F32)),
        in_specs=[VMEM, ANY, VMEM, ANY, ANY, ANY] + [VMEM] * 4,
        out_specs=(VMEM,) * 3,
        scratch_shapes=[
            wide, wide, wide, pltpu.VMEM((model, nq), BF), pltpu.VMEM((model, nq), F32),
            pltpu.VMEM((model, nq), BF), pltpu.VMEM((model, nq), BF),
            pltpu.VMEM((dp - 1, rows, nq), BF), pltpu.VMEM((dp - 1, rows, nq), BF),
            pltpu.VMEM((8, model), F32), pltpu.VMEM((3, 16, model), F32), pltpu.VMEM((nv, 16, model), F32),
        ]
        + scatter_scratch(seq, model)
        + [DMA((4,)), DMA((1,)), DMA((1,)), DMA((dp - 1,)), DMA((dp - 1,)), DMA((nv,)), DMA((nv,))],
        compiler_params=params(6),
        cost_estimate=cost(35),
        name="layer_last",
    )(dmix, e2, dh, xf, n1, w0, vecs, vf1, vd1, vd0)


def attention_plan(seg, live):
    seq = seg.shape[0]
    counter = jnp.arange(seq, dtype=jnp.int32)
    before = [jnp.sum((seg == v).astype(jnp.int32)) for v in range(3)]
    start = sum(jnp.where(seg > v, before[v], 0) for v in range(3))
    kc = jnp.where(counter < live * LIVE, seg, -1)
    lo = start[::QB] // QB
    hi = jnp.minimum(jnp.arange(seq // QB, dtype=jnp.int32), (live * LIVE + QB - 1) // QB)
    bounds = jnp.stack([jnp.minimum(lo, hi), hi]).astype(jnp.int32)
    return bounds, (counter - start)[None, :], seg[None, :], kc[:, None]


def by_part(w):
    rows = w.shape[0]
    heads = w.shape[1] // (3 * HD)
    w = w.reshape(rows, heads, 3, HD).transpose(0, 2, 1, 3).reshape(rows, 3, heads * HD)
    return jnp.pad(w, ((0, 0), (0, 0), (0, HW - heads * HD))).reshape(rows, 3 * HW)


def by_head(w, heads):
    rows = w.shape[0]
    w = w.reshape(rows, 3, HW)[:, :, : heads * HD].reshape(rows, 3, heads, HD)
    return w.transpose(0, 2, 1, 3).reshape(rows, heads * 3 * HD)


def shards(
    dp, tensor, inputs, cotangent, segments, live_blocks, ln1_gain, ln1_bias, qkv_weight, qkv_bias,
    out_weight, out_bias, ln2_gain, ln2_bias, fc1_weight, fc1_bias, fc2_weight, fc2_bias,
):
    s, z, t = lax.axis_index("section"), lax.axis_index("dp"), lax.axis_index("tensor")
    model = inputs.shape[-1]
    ff = fc1_weight.shape[2]
    heads = qkv_bias.shape[1]
    col = columns(model, ff)

    def mine(a):
        return lax.dynamic_index_in_dim(a, s, 0, keepdims=False)[0]

    x, cot, seg, live = mine(inputs), mine(cotangent), mine(segments), mine(live_blocks)
    bounds, pos, sr, kc = attention_plan(seg, live)
    wout = jnp.pad(out_weight[0].T, ((0, 0), (0, HW - heads * HD)))
    w = jnp.concatenate([by_part(qkv_weight[0]), fc1_weight[0], fc2_weight[0].T, wout], axis=1)
    small = jnp.stack([ln1_gain[0], ln1_bias[0], out_bias[0], ln2_gain[0], ln2_bias[0], fc2_bias[0]])
    own = small.shape[1]

    def lanes(a):
        return jnp.pad(a.astype(F32), ((0, 0), (0, 128 - a.shape[1])))

    sv = jnp.concatenate([lanes(small), lanes(qkv_bias[0]), lanes(fc1_bias[0])], axis=0)
    sv = jnp.pad(sv, ((0, -sv.shape[0] % 8), (0, 0)))
    fr = 10000.0 ** (-(jnp.arange(ROT // 2, dtype=F32) * (2.0 / ROT)))
    fr = jnp.broadcast_to(fr[:, None], (ROT // 2, 128))
    cfg = {
        "col": col, "ff": ff, "heads": heads, "dp": dp, "tensor": tensor, "own": own,
        "qw": qkv_bias.shape[2], "fw": fc1_bias.shape[2],
        "groups": [(0, col["fc1"]), (col["fc1"], col["fc2"]), (col["fc2"], col["end"])],
    }
    t_pairs = [[(i, i + 1 - 2 * (i % 2)) for i in range(tensor)], [(i, (i + 2) % tensor) for i in range(tensor)]]

    xf, n1a, n2a, ga, gpa, tab, w0, vecs, qa, ka, va = layer_in(cfg, x, w, sv, pos, fr)
    half = cot.shape[0] // 2
    cot_, _ = lax.optimization_barrier((cot, qa))
    cx = lax.ppermute(cot_, "tensor", t_pairs[0])
    cy = lax.ppermute(cot_, "tensor", t_pairs[1])
    oa, lsea = attn_fwd(heads, bounds, qa, ka, va, sr, kc)
    h, hf, n1b, n2b, gb, gpb, w1, qb, kb, vb = layer_mid(cfg, oa, ga, x, w, w0, vecs, tab)
    cx_, cy_, _ = lax.optimization_barrier((cx, cy, qb))
    cd0 = lax.ppermute(cx_[:half], "tensor", t_pairs[1])
    cd1 = lax.ppermute(cy_[half:], "tensor", t_pairs[0])
    ob, lseb = attn_fwd(heads, bounds, qb, kb, vb, sr, kc)
    y, dob, e2b, grb, vdb = layer_turn(cfg, ob, gb, h, hf, (cot, cx, cy, cd0, cd1), w1, vecs, n2b, gpb)
    dmb = attn_bwd(heads, bounds, qb, kb, vb, ob, dob, lseb, sr, kc, tab)
    dh, e2a, doa, vfb, vda, gr1, sba, owna, sbb, ownb = layer_back(
        cfg, dmb, e2b, cot, hf, n1b, w1, w0, vecs, xf, ga, gpa, n2a, oa, grb
    )

    def over_dp(blocks, section):
        def pairs(d):
            return [(section * dp + i, section * dp + (i + d) % dp) for i in range(dp)]

        return [lax.ppermute(blocks[d - 1], ("section", "dp"), pairs(d)) for d in range(1, dp)]

    got_r = over_dp(sba, 0)
    got_q = over_dp(sbb, 1)
    dma = attn_bwd(heads, bounds, qa, ka, va, oa, doa, lsea, sr, kc, tab)
    dx, gq0, gv = layer_last(cfg, dma, e2a, dh, xf, n1a, w0, vecs, vfb, vdb, vda)
    first = s == 0
    gr = jnp.where(first, owna + sum(a.astype(F32) for a in got_r), gr1)
    gq = jnp.where(first, gq0, ownb + sum(a.astype(F32) for a in got_q))

    def swapped(a0, a1):
        got = lax.ppermute(jnp.where(first, a1, a0), "section", [(0, 1), (1, 0)])
        keep = jnp.where(first, a0, a1)
        return jnp.stack([jnp.where(first, keep, got), jnp.where(first, got, keep)])[None, :, None]

    section_outputs = swapped(h, y)
    input_grads = swapped(dx, dh)
    gv = lax.dynamic_index_in_dim(gv.reshape(2, 8, model), s, 0, keepdims=False)
    short = lax.dynamic_slice_in_dim(gv[:6], (z * tensor + t) * own, own, 1)
    gqb_ = by_head(gv[6:7], heads).reshape(heads, 3 * HD)
    gqb_ = lax.dynamic_slice_in_dim(gqb_, z * cfg["qw"], cfg["qw"], 1)[None]
    gfb = lax.dynamic_slice_in_dim(gv[7].reshape(heads, ff // heads), z * cfg["fw"], cfg["fw"], 1)[None]
    gqkv = by_head(gq, heads)[None]
    gfc1 = gr[:, :ff][None]
    gfc2 = gr[:, ff : 2 * ff].T[None]
    gout = gr[:, 2 * ff : 2 * ff + heads * HD].T[None]
    return (
        section_outputs,
        input_grads,
        short[0:1],
        short[1:2],
        gqkv,
        gqb_,
        gout,
        short[2:3],
        short[3:4],
        short[4:5],
        gfc1,
        gfb,
        gfc2,
        short[2:3],
    )


def solution(mesh):
    both = ("dp", "tensor")
    in_specs = (
        P(None, "dp", "tensor", None),
        P(None, "dp", "tensor", None),
        P(None, "dp", None),
        P(None, "dp"),
        P("section", both),
        P("section", both),
        P("section", "dp", "tensor"),
        P("section", "tensor", "dp"),
        P("section", "tensor", "dp"),
        P("section", both),
        P("section", both),
        P("section", both),
        P("section", "dp", "tensor"),
        P("section", "tensor", "dp"),
        P("section", "tensor", "dp"),
        P("section", both),
    )
    out_specs = (
        P("section", None, "dp", "tensor", None),
        P("section", None, "dp", "tensor", None),
        P("section", both),
        P("section", both),
        P("section", "dp", "tensor"),
        P("section", "tensor", "dp"),
        P("section", "tensor", "dp"),
        P("section", both),
        P("section", both),
        P("section", both),
        P("section", "dp", "tensor"),
        P("section", "tensor", "dp"),
        P("section", "tensor", "dp"),
        P("section", both),
    )
    body = functools.partial(shards, mesh.shape["dp"], mesh.shape["tensor"])
    return jax.shard_map(body, mesh=mesh, in_specs=in_specs, out_specs=out_specs, check_vma=False)
```

time: 643 us -> 439 us (0.68)
  Pallas kernels: 586 us -> 364 us
  starting transfers between devices: 0.01 us -> 19.3 us
  local copies, waits for them, and re-layouts: 44.2 us -> 30.1 us
  other arithmetic: 13.2 us -> 20.9 us
    pallas_call x7 -> x5, Pallas kernels: 495 us -> 277 us  [the longest x1 76.5 us: layer_back(): pl.pallas_call(functools.partial(back_kernel, cfg), out_shape=(sds(cot.sh...]
    ppermute x0 -> x10, starting transfers between devices: none -> 18.8 us  [the longest x6 14.1 us: over_dp(): lax.ppermute(blocks[d - 1], ('section', 'dp'), pairs(d))]
    unnamed x75 -> x93, local copies, waits for them, and re-layouts: 26.8 us -> 13.7 us
  transfers between devices with their start and end apart: 2 -> 12, of which waited for: 0 -> 0; matrix products, arithmetic and copies ran while one was open for 3% -> 5% of each run, Pallas kernels for 23% -> 39%
where the time goes in v2:
time: 439 us; the launch traced here: 436 us
  Pallas kernels  364 us (83%)
  local copies, waits for them, and re-layouts  30.1 us (7%)
  other arithmetic  20.9 us (5%)
  starting transfers between devices  19.3 us (4%)
    pallas_call x1, Pallas kernels, layer_back(): pl.pallas_call(functools.partial(back_kernel, cfg), out_shape=(sds(cot.sh...  76.5 us
    pallas_call x1, Pallas kernels, layer_mid(): pl.pallas_call(functools.partial(mid_kernel, cfg), out_shape=(sds(x.shape...  73.9 us
    pallas_call x2, Pallas kernels, attn_bwd(): pl.pallas_call(functools.partial(attn_bwd_kernel, heads), out_shape=sds((...  61.6 us
    pallas_call x1, Pallas kernels, layer_in(): pl.pallas_call(functools.partial(in_kernel, cfg), out_shape=(rows, rows,...  55.7 us
    pallas_call x1, Pallas kernels, layer_last(): pl.pallas_call(functools.partial(last_kernel, cfg), out_shape=(sds(dh.sha...  41.9 us
    pallas_call x1, Pallas kernels, layer_turn(): pl.pallas_call(functools.partial(turn_kernel, cfg), out_shape=(sds(h.shap...  28.8 us
    pallas_call x2, Pallas kernels, attn_fwd(): pl.pallas_call(functools.partial(attn_fwd_kernel, heads), out_shape=(sds(...  25.3 us
    ppermute x6, starting transfers between devices, over_dp(): lax.ppermute(blocks[d - 1], ('section', 'dp'), pairs(d))  14.1 us
  transfers between devices with their start and end apart: 12, of which 0 were waited for; matrix products, arithmetic and copies ran while one was open for 5% of the time, Pallas kernels for 39%

profile of v2, /device:TPU:0, one launch (start us, length us, event | category | flops | bytes accessed | tf_op | source)
XLA Modules:
  0.0 436.0 jit_solution(17276950161111841331)
XLA Ops:
  3.8 2.2 dynamic-slice_bitcast_fusion
  6.0 2.6 fusion.10.pos_ref
  8.5 2.0 fusion.2.w_ref
  11.2 55.7 %layer_in.1 = (bf16[2048,768]{1,0:T(8,128)(2,1)}, bf16[2048,768]{1,0:T(8,128)(2,1)}, bf16[2048,768]{1,0:T(8,128)(2,1)}, bf16[2048,768]{1,0:T(8,128)(2,1)}, bf16[...) custom-call(bf16[512,768]{1,0:T(8,128)(2,1)} %get-tuple-element.159., ...), custom_call_target="tpu_custom_call" | custom-call | flops 30400000000 | tf_op jit(solution)/shard_map/layer_in/pallas_call | solution.py:905
  67.6 1.4 collective-permute-start.1
  70.3 2.0 fusion.4
  72.4 1.3 copy.41
  73.7 2.1 fusion.1.kc_ref
  75.9 12.7 %attn_fwd.2 = (bf16[2048,256]{1,0:T(8,128)(2,1)S(1)}, f32[8,2048]{1,0:T(8,128)S(1)}) custom-call(s32[2,8]{1,0:T(2,128)S(1)} %pad_add_fusion.b_ref, bf16[2048,256]{1,0:T(8,128)(2,1)S(1)} %copy-done.5, bf16[2048,256]{1,0:T(8,128)(2,1)S(1)} %copy-done.7, bf16[2048,256]{1,0:T(8,128)(2,1)S(1)} %copy-done.9, s32[1,2048]{1,0:T(1,128)S(1)} %get-tuple-element.152.sr_ref, ...), custom_call_target="tpu_custom_call" | custom-call | flops 12000000000 | tf_op jit(solution)/shard_map/attn_fwd/pallas_call | solution.py:124
  89.5 73.9 %layer_mid.1 = (bf16[512,768]{1,0:T(8,128)(2,1)}, bf16[2048,768]{1,0:T(8,128)(2,1)}, bf16[2048,768]{1,0:T(8,128)(2,1)}, bf16[2048,768]{1,0:T(8,128)(2,1)}, bf16[...) custom-call(bf16[2048,256]{1,0:T(8,128)(2,1)} %copy-done.11, ...), custom_call_target="tpu_custom_call" | custom-call | flops 51999997952 | tf_op jit(solution)/shard_map/layer_mid/pallas_call | solution.py:972
  164.4 1.7 collective-permute-start.2
  171.8 12.7 %attn_fwd.3 = (bf16[2048,256]{1,0:T(8,128)(2,1)S(1)}, f32[8,2048]{1,0:T(8,128)S(1)}) custom-call(s32[2,8]{1,0:T(2,128)S(1)} %pad_add_fusion.b_ref, bf16[2048,256]{1,0:T(8,128)(2,1)S(1)} %copy-done.12, bf16[2048,256]{1,0:T(8,128)(2,1)S(1)} %copy-done.14, bf16[2048,256]{1,0:T(8,128)(2,1)S(1)} %copy-done.16, s32[1,2048]{1,0:T(1,128)S(1)} %get-tuple-element.152.sr_ref, ...), custom_call_target="tpu_custom_call" | custom-call | flops 12000000000 | tf_op jit(solution)/shard_map/attn_fwd/pallas_call | solution.py:124
  185.4 28.8 %layer_turn.1 = (bf16[512,768]{1,0:T(8,128)(2,1)}, bf16[2048,256]{1,0:T(8,128)(2,1)}, bf16[2048,768]{1,0:T(8,128)(2,1)}, bf16[768,1792]{1,0:T(8,128)(2,1)}, f32[8,768]{1,0:T(8,128)}) custom-call(bf16[2048,256]{1,0:T(8,128)(2,1)} %copy-done.18, bf16[2048,768]{1,0:T(8,128)(2,1)} %get-tuple-element.73.g_in, bf16[512,768]{1,0:T(8,128)(2,1)} %get-tuple-element.68.h_ref, ...), custom_call_target="tpu_custom_call" | custom-call | flops 32000000000 | tf_op jit(solution)/shard_map/layer_turn/pallas_call | solution.py:1064
  217.9 30.8 %attn_bwd.2.dmix = bf16[2048,768]{1,0:T(8,128)(2,1)} custom-call(s32[2,8]{1,0:T(2,128)S(1)} %pad_add_fusion.b_ref, bf16[2048,256]{1,0:T(8,128)(2,1)S(1)} %copy-done.13, bf16[2048,256]{1,0:T(8,128)(2,1)S(1)} %copy-done.15, bf16[2048,256]{1,0:T(8,128)(2,1)S(1)} %copy-done.17, bf16[2048,256]{1,0:T(8,128)(2,1)} %copy-done.18, ...), custom_call_target="tpu_custom_call" | custom-call | flops 28000000000 | tf_op jit(solution)/shard_map/attn_bwd/pallas_call | solution.py:218
  248.7 76.5 %layer_back.1 = (bf16[512,768]{1,0:T(8,128)(2,1)}, bf16[2048,768]{1,0:T(8,128)(2,1)}, bf16[2048,256]{1,0:T(8,128)(2,1)}, f32[8,768]{1,0:T(8,128)}, f32[8,768]{1,...) custom-call(bf16[2048,768]{1,0:T(8,128)(2,1)} %attn_bwd.2.dmix, ...), custom_call_target="tpu_custom_call" | custom-call | flops 51999997952 | tf_op jit(solution)/shard_map/layer_back/pallas_call | solution.py:1168
  325.3 3.1 slice_bitcast_fusion.2
  328.3 4.8 %collective-permute-start.10 = (bf16[192,1792]{1,0:T(8,128)(2,1)}, bf16[192,1792]{1,0:T(8,128)(2,1)}, u32[]{:S(2)}, u32[]{:S(2)}) collective-permute-start(bf16[192,1792]{1,0:T(8,128)(2,1)} %get-tuple-element.145), channel_id=1, source_target_pairs={{0,8},{4,12},{8,0},{12,4},{1,9},{5,13},{9,1},{13,5},{2,10},{6,14},... | collective-permute-start | bytes 2064392 | tf_op jit(solution)/shard_map/ppermute | solution.py:1343
  333.1 4.6 %collective-permute-start.11 = (bf16[192,1792]{1,0:T(8,128)(2,1)}, bf16[192,1792]{1,0:T(8,128)(2,1)}, u32[]{:S(2)}, u32[]{:S(2)}) collective-permute-start(bf16[192,1792]{1,0:T(8,128)(2,1)} %get-tuple-element.144), channel_id=1, source_target_pairs={{0,12},{4,0},{8,4},{12,8},{1,13},{5,1},{9,5},{13,9},{2,14},{6,2},{... | collective-permute-start | bytes 2064392 | tf_op jit(solution)/shard_map/ppermute | solution.py:1343
  337.7 1.9 collective-permute-start.9
  340.4 1.4 collective-permute-start.7
  341.9 30.8 %attn_bwd.3.dmix = bf16[2048,768]{1,0:T(8,128)(2,1)} custom-call(s32[2,8]{1,0:T(2,128)S(1)} %copy-done.4, bf16[2048,256]{1,0:T(8,128)(2,1)S(1)} %copy-done.6, bf16[2048,256]{1,0:T(8,128)(2,1)S(1)} %copy-done.8, bf16[2048,256]{1,0:T(8,128)(2,1)S(1)} %copy-done.10, bf16[2048,256]{1,0:T(8,128)(2,1)} %copy-done.11, bf16[2048,256]{1,0:T(8,128)(2,1)} %get-tuple-element.90.do_ref, ...), custom_call_target="tpu_custom_call" | custom-call | flops 28000000000 | tf_op jit(solution)/shard_map/attn_bwd/pallas_call | solution.py:218
  372.7 41.9 %layer_last.1 = (bf16[512,768]{1,0:T(8,128)(2,1)}, f32[192,768]{1,0:T(8,128)}, f32[16,768]{1,0:T(8,128)}) custom-call(bf16[2048,768]{1,0:T(8,128)(2,1)} %attn_bwd.3.dmix, bf16[2048,768]{1,0:T(8,128)(2,1)} %get-tuple-element.92.e2_in, bf16[512,768]{1,0:T(8,128)(2,1)} %get-tuple-element.93.dh, bf16[2048,768]{1,0:T(8,128)(2,1)} %get-tuple-element.86.xf_in, ...), custom_call_target="tpu_custom_call" | custom-call | flops 28000000000 | tf_op jit(solution)/shard_map/layer_last/pallas_call | solution.py:1244
  414.6 1.5 dynamic-slice_reduce_fusion
  425.5 2.3 add_select_fusion
  (151 shorter events, 35.7 us)
Async XLA Ops:
  3.8 210.4 %copy-start.1 = (s32[1,2048]{1,0:T(1,128)}, s32[1,2048]{1,0:T(1,128)S(1)}, u32[]{:S(2)}) copy-start(s32[1,2048]{1,0:T(1,128)S(1)} %get-tuple-element.152.sr_ref) | copy-start | bytes 24580
  6.0 61.6 %copy-start.27 = (bf16[512,768]{1,0:T(8,128)(2,1)}, bf16[512,768]{1,0:T(8,128)(2,1)S(1)}, u32[]{:S(2)}) copy-start(bf16[512,768]{1,0:T(8,128)(2,1)S(1)} %get-tuple-element.75.cot) | copy-start | bytes 2359300
  11.2 57.8 %copy-start.43 = (s32[2,1]{0,1:T(1,128)S(1)}, s32[2,1]{0,1:T(1,128)}, u32[]{:S(2)}) copy-start(s32[2,1]{0,1:T(1,128)} %param.19) | copy-start | bytes 28
  67.0 96.4 %collective-permute-start = (bf16[512,768]{1,0:T(8,128)(2,1)S(1)}, bf16[512,768]{1,0:T(8,128)(2,1)}, u32[]{:S(2)}, u32[]{:S(2)}) collective-permute-start(bf16[512,768]{1,0:T(8,128)(2,1)S(1)} %get-tuple-element.75.cot), channel_id=1, source_target_pairs={{0,1},{1,0},{2,3},{3,2},{4,5},{5,4},{6,7},{7,6},{8,9},{9,8},{10,11... | collective-permute-start | bytes 2359304 | tf_op jit(solution)/shard_map/ppermute | solution.py:1325
  67.6 95.8 %collective-permute-start.1 = (bf16[512,768]{1,0:T(8,128)(2,1)S(1)}, bf16[512,768]{1,0:T(8,128)(2,1)}, u32[]{:S(2)}, u32[]{:S(2)}) collective-permute-start(bf16[512,768]{1,0:T(8,128)(2,1)S(1)} %get-tuple-element.75.cot), channel_id=1, source_target_pairs={{0,2},{1,3},{2,0},{3,1},{4,6},{5,7},{6,4},{7,5},{8,10},{9,11},{10,... | collective-permute-start | bytes 2359304 | tf_op jit(solution)/shard_map/ppermute | solution.py:1326
  75.8 92.3 %copy-start = (s32[2048,1]{1,0:T(8,128)}, s32[2048,1]{1,0:T(8,128)S(1)}, u32[]{:S(2)}) copy-start(s32[2048,1]{1,0:T(8,128)S(1)} %fusion.1.kc_ref) | copy-start | bytes 24580
  75.8 138.4 %copy-start.3 = (s32[2,8]{1,0:T(2,128)}, s32[2,8]{1,0:T(2,128)S(1)}, u32[]{:S(2)}) copy-start(s32[2,8]{1,0:T(2,128)S(1)} %pad_add_fusion.b_ref) | copy-start | bytes 196
  89.5 73.9 %copy-start.19 = (f32[8,2048]{1,0:T(8,128)}, f32[8,2048]{1,0:T(8,128)S(1)}, u32[]{:S(2)}) copy-start(f32[8,2048]{1,0:T(8,128)S(1)} %get-tuple-element.91.lse_ref) | copy-start | bytes 196612
  164.4 21.0 %collective-permute-start.2 = (bf16[256,768]{1,0:T(8,128)(2,1)S(1)}, bf16[256,768]{1,0:T(8,128)(2,1)}, u32[]{:S(2)}, u32[]{:S(2)}) collective-permute-start(bf16[256,768]{1,0:T(8,128)(2,1)S(1)} %slice.86), channel_id=1, source_target_pairs={{0,2},{1,3},{2,0},{3,1},{4,6},{5,7},{6,4},{7,5},{8,10},{9,11},{10,... | collective-permute-start | bytes 1179656 | tf_op jit(solution)/shard_map/ppermute | solution.py:1330
  167.1 18.3 %collective-permute-start.3 = (bf16[256,768]{1,0:T(8,128)(2,1)S(1)}, bf16[256,768]{1,0:T(8,128)(2,1)}, u32[]{:S(2)}, u32[]{:S(2)}) collective-permute-start(bf16[256,768]{1,0:T(8,128)(2,1)S(1)} %slice.87), channel_id=1, source_target_pairs={{0,1},{1,0},{2,3},{3,2},{4,5},{5,4},{6,7},{7,6},{8,9},{9,8},{10,11... | collective-permute-start | bytes 1179656 | tf_op jit(solution)/shard_map/ppermute | solution.py:1331
  325.2 16.6 %copy-start.2 = (s32[1,2048]{1,0:T(1,128)S(1)}, s32[1,2048]{1,0:T(1,128)}, u32[]{:S(2)}) copy-start(s32[1,2048]{1,0:T(1,128)} %copy-done.1) | copy-start | bytes 24580
  325.2 16.6 %copy-start.4 = (s32[2,8]{1,0:T(2,128)S(1)}, s32[2,8]{1,0:T(2,128)}, u32[]{:S(2)}) copy-start(s32[2,8]{1,0:T(2,128)} %copy-done.3) | copy-start | bytes 196
  325.2 16.6 %copy-start.6 = (bf16[2048,256]{1,0:T(8,128)(2,1)S(1)}, bf16[2048,256]{1,0:T(8,128)(2,1)}, u32[]{:S(2)}) copy-start(bf16[2048,256]{1,0:T(8,128)(2,1)} %get-tuple-element.60.q_ref) | copy-start | bytes 3145732
  325.2 16.6 %copy-start.8 = (bf16[2048,256]{1,0:T(8,128)(2,1)S(1)}, bf16[2048,256]{1,0:T(8,128)(2,1)}, u32[]{:S(2)}) copy-start(bf16[2048,256]{1,0:T(8,128)(2,1)} %get-tuple-element.61.k_ref) | copy-start | bytes 3145732
  328.3 97.1 %collective-permute-start.10 = (bf16[192,1792]{1,0:T(8,128)(2,1)}, bf16[192,1792]{1,0:T(8,128)(2,1)}, u32[]{:S(2)}, u32[]{:S(2)}) collective-permute-start(bf16[192,1792]{1,0:T(8,128)(2,1)} %get-tuple-element.145), channel_id=1, source_target_pairs={{0,8},{4,12},{8,0},{12,4},{1,9},{5,13},{9,1},{13,5},{2,10},{6,14},... | collective-permute-start | bytes 2064392 | tf_op jit(solution)/shard_map/ppermute | solution.py:1343
  333.1 92.3 %collective-permute-start.11 = (bf16[192,1792]{1,0:T(8,128)(2,1)}, bf16[192,1792]{1,0:T(8,128)(2,1)}, u32[]{:S(2)}, u32[]{:S(2)}) collective-permute-start(bf16[192,1792]{1,0:T(8,128)(2,1)} %get-tuple-element.144), channel_id=1, source_target_pairs={{0,12},{4,0},{8,4},{12,8},{1,13},{5,1},{9,5},{13,9},{2,14},{6,2},{... | collective-permute-start | bytes 2064392 | tf_op jit(solution)/shard_map/ppermute | solution.py:1343
  337.7 87.7 %collective-permute-start.9 = (bf16[192,1792]{1,0:T(8,128)(2,1)}, bf16[192,1792]{1,0:T(8,128)(2,1)}, u32[]{:S(2)}, u32[]{:S(2)}) collective-permute-start(bf16[192,1792]{1,0:T(8,128)(2,1)} %get-tuple-element.143), channel_id=1, source_target_pairs={{0,4},{4,8},{8,12},{12,0},{1,5},{5,9},{9,13},{13,1},{2,6},{6,10},{... | collective-permute-start | bytes 2064392 | tf_op jit(solution)/shard_map/ppermute | solution.py:1343
  339.7 79.6 %collective-permute-start.6 = (bf16[192,768]{1,0:T(8,128)(2,1)S(1)}, bf16[192,768]{1,0:T(8,128)(2,1)S(1)}, u32[]{:S(2)}, u32[]{:S(2)}) collective-permute-start(bf16[192,768]{1,0:T(8,128)(2,1)S(1)} %get-tuple-element.148), channel_id=1, source_target_pairs={{16,20},{20,24},{24,28},{28,16},{17,21},{21,25},{25,29},{29,17},{1... | collective-permute-start | bytes 884744 | tf_op jit(solution)/shard_map/ppermute | solution.py:1343
  340.4 81.7 %collective-permute-start.7 = (bf16[192,768]{1,0:T(8,128)(2,1)S(1)}, bf16[192,768]{1,0:T(8,128)(2,1)}, u32[]{:S(2)}, u32[]{:S(2)}) collective-permute-start(bf16[192,768]{1,0:T(8,128)(2,1)S(1)} %get-tuple-element.150), channel_id=1, source_target_pairs={{16,24},{20,28},{24,16},{28,20},{17,25},{21,29},{25,17},{29,21},{1... | collective-permute-start | bytes 884744 | tf_op jit(solution)/shard_map/ppermute | solution.py:1343
  372.7 45.6 %copy-start.23 = (bf16[512,768]{1,0:T(8,128)(2,1)S(1)}, bf16[512,768]{1,0:T(8,128)(2,1)}, u32[]{:S(2)}) copy-start(bf16[512,768]{1,0:T(8,128)(2,1)} %get-tuple-element.93.dh) | copy-start | bytes 2359300
  417.6 17.9 %copy-start.42 = (f32[1,48]{1,0:T(1,128)}, f32[1,48]{1,0:T(1,128)S(1)}, u32[]{:S(2)}) copy-start(f32[1,48]{1,0:T(1,128)S(1)} %get-tuple-element.187) | copy-start | bytes 580
  419.3 2.9 collective-permute-start.8
  422.2 7.5 %collective-permute-start.5 = (bf16[512,768]{1,0:T(8,128)(2,1)}, bf16[512,768]{1,0:T(8,128)(2,1)}, u32[]{:S(2)}, u32[]{:S(2)}) collective-permute-start(bf16[512,768]{1,0:T(8,128)(2,1)} %broadcast_select_fusion), channel_id=1, source_target_pairs={{0,16},{16,0},{1,17},{17,1},{2,18},{18,2},{3,19},{19,3},{4,20},{20... | collective-permute-start | bytes 2359304 | tf_op jit(solution)/shard_map/ppermute | solution.py:1354
  422.2 10.8 %collective-permute-start.4 = (bf16[512,768]{1,0:T(8,128)(2,1)}, bf16[512,768]{1,0:T(8,128)(2,1)}, u32[]{:S(2)}, u32[]{:S(2)}) collective-permute-start(bf16[512,768]{1,0:T(8,128)(2,1)} %broadcast_select_fusion.2), channel_id=1, source_target_pairs={{0,16},{16,0},{1,17},{17,1},{2,18},{18,2},{3,19},{19,3},{4,20},{20... | collective-permute-start | bytes 2359304 | tf_op jit(solution)/shard_map/ppermute | solution.py:1354
  (32 other events, 129.3 us)

commit v3 on v2

v3 whole, which is shorter than its diff:
```python
import functools

import jax
import jax.numpy as jnp
import numpy as np
from jax import lax
from jax.experimental import pallas as pl
from jax.experimental.pallas import tpu as pltpu
from jax.sharding import PartitionSpec as P

F32 = jnp.float32
BF = jnp.bfloat16
MESH = pl.DeviceIdType.MESH
HD = 64
ROT = 16
LIVE = 128
DOCS = 4
DOC_MAX = 1024
QB = 256
HW = 256
SUB = 256
EPS = 1e-05
NEG = -1e30
VMEM = pl.BlockSpec(memory_space=pltpu.VMEM)
ANY = pl.BlockSpec(memory_space=pltpu.HBM)
SMEM = pl.BlockSpec(memory_space=pltpu.SMEM)
DMA = pltpu.SemaphoreType.DMA


def sds(shape, dtype):
    return jax.ShapeDtypeStruct(shape, dtype)


def dg(a, b, ca, cb):
    return lax.dot_general(a, b, (((ca,), (cb,)), ((), ())), preferred_element_type=F32)


def dot(a, b):
    return jnp.dot(a, b, preferred_element_type=F32)


def ds(start, size):
    return pl.ds(pl.multiple_of(start, size), size)


def norm_stats(x):
    mu = jnp.mean(x, axis=-1, keepdims=True)
    xc = x - mu
    var = jnp.mean(xc * xc, axis=-1, keepdims=True)
    return xc, lax.rsqrt(var + EPS)


def head_lanes(width, heads):
    lane = lax.broadcasted_iota(jnp.int32, (1, width), 1)
    return [(lane >= h * HD) & (lane < (h + 1) * HD) for h in range(heads)]


def allow_mask(kc, sq, diag):
    m = kc == sq
    if diag:
        r = lax.broadcasted_iota(jnp.int32, (QB, QB), 0)
        c = lax.broadcasted_iota(jnp.int32, (QB, QB), 1)
        m = (m & (r <= c)) | (r == c)
    return m


def block_bounds(seg, live, i, n):
    s = lax.axis_index("tensor") // 2
    doc = seg[s, 0, i * QB]

    def body(j, count):
        return count + jnp.where((j < i) & (seg[s, 0, (j + 1) * QB - 1] == doc), 1, 0)

    hi = jnp.minimum(i, (live[s, 0] * LIVE + QB - 1) // QB)
    return jnp.minimum(i - lax.fori_loop(0, n, body, 0), hi), hi


def turn_blocks(src, dst):
    def turn(i, _):
        dst[:, ds(i * QB, QB)] = src[ds(i * QB, QB), :].T
        return 0

    lax.fori_loop(0, src.shape[0] // QB, turn, 0)


def attn_fwd_block(i, lo, hi, heads, q_ref, k_ref, vt, sr_ref, kc_ref, s_scr, o_ref, lse_ref):
    width = q_ref.shape[1]
    qi = ds(i * QB, QB)
    q = q_ref[qi, :]
    qm = [jnp.where(m, q, jnp.zeros_like(q)) for m in head_lanes(width, heads)]
    sq = sr_ref[0:1, qi]

    def scores(j, slot, ms, diag):
        kj = ds(j * QB, QB)
        k = k_ref[kj, :]
        mask = allow_mask(kc_ref[kj, 0:1], sq, diag)
        out = []
        for h in range(heads):
            s = jnp.where(mask, dg(k, qm[h], 1, 1), NEG)
            s_scr[h, ds(slot * QB, QB), :] = s
            out.append(jnp.maximum(ms[h], jnp.max(s, axis=0, keepdims=True)))
        return tuple(out)

    ms = tuple(jnp.full((1, QB), NEG, F32) for _ in range(heads))
    ms = scores(i, 0, ms, True)
    ms = lax.fori_loop(lo, hi, lambda j, ms: scores(j, j - lo + 1, ms, False), ms)

    def weigh(j, slot, st):
        kj = ds(j * QB, QB)
        out = []
        for h in range(heads):
            total, acc = st[h]
            p = jnp.exp(s_scr[h, ds(slot * QB, QB), :] - ms[h])
            total = total + jnp.sum(p, axis=0, keepdims=True)
            acc = acc + dot(vt[h * HD : (h + 1) * HD, kj], p.astype(BF))
            out.append((total, acc))
        return tuple(out)

    st = tuple((jnp.zeros((1, QB), F32), jnp.zeros((HD, QB), F32)) for _ in range(heads))
    st = weigh(i, 0, st)
    st = lax.fori_loop(lo, hi, lambda j, st: weigh(j, j - lo + 1, st), st)
    ot = [st[h][1] * (1.0 / st[h][0]) for h in range(heads)]
    ot = jnp.concatenate(ot + [jnp.zeros((width - heads * HD, QB), F32)], axis=0)
    o_ref[qi, :] = ot.T.astype(BF)
    lse = [ms[h] + jnp.log(st[h][0]) for h in range(heads)]
    lse_ref[:, qi] = jnp.concatenate(lse + [jnp.zeros((8 - heads, QB), F32)], axis=0)


def attn_fwd_kernel(heads, seg, live, q_in, k_in, v_in, sr_ref, kc_ref, o_out, lse_ref, q, k, v, o, vt, s_scr, lsem, osem):
    n = q.shape[0] // QB
    loads = load([(v_in, v), (q_in, q), (k_in, k)], lsem)
    loads[0].wait()
    turn_blocks(v, vt)
    loads[1].wait()
    loads[2].wait()

    def out(i):
        rows = ds(i * QB, QB)
        return pltpu.make_async_copy(o.at[rows], o_out.at[rows], osem.at[i])

    def qloop(i, _):
        lo, hi = block_bounds(seg, live, i, n)
        attn_fwd_block(i, lo, hi, heads, q, k, vt, sr_ref, kc_ref, s_scr, o, lse_ref)
        out(i).start()
        return 0

    lax.fori_loop(0, n, qloop, 0)

    def drain(i, _):
        out(i).wait()
        return 0

    lax.fori_loop(0, n, drain, 0)


def attn_fwd(heads, seg, live, q, k, v, sr, kc):
    rows, width = q.shape
    buf = pltpu.VMEM((rows, width), BF)
    return pl.pallas_call(
        functools.partial(attn_fwd_kernel, heads),
        out_shape=(sds((rows, width), BF), sds((8, rows), F32)),
        in_specs=[SMEM, SMEM, ANY, ANY, ANY, VMEM, VMEM],
        out_specs=(ANY, VMEM),
        scratch_shapes=[buf, buf, buf, buf, pltpu.VMEM((width, rows), BF), pltpu.VMEM((heads, rows + QB, QB), F32),
                        DMA((3,)), DMA((rows // QB,))],
        compiler_params=pltpu.CompilerParams(vmem_limit_bytes=67043328),
        cost_estimate=cost(12),
        name="attn_fwd",
    )(seg, live, q, k, v, sr, kc)


def turn_lanes(x, tab, sign):
    width = x.shape[1]
    c, sn = [jnp.concatenate([tab[:, a * 128 : (a + 1) * 128]] * (width // 128), axis=1) for a in range(2)]
    lane = lax.broadcasted_iota(jnp.int32, (1, width), 1) % HD
    moved = jnp.where(lane < ROT // 2, pltpu.roll(x, width - ROT // 2, 1), pltpu.roll(x, ROT // 2, 1)) * sn
    return x * c + moved if sign > 0 else x * c - moved


def attn_bwd_block(i, lo, hi, heads, q_ref, k_ref, v_ref, o_ref, do_ref, kt, lse_ref, sr_ref, kc_ref, tab, dk, dv, out):
    width = q_ref.shape[1]
    hm = head_lanes(width, heads)
    rowid = lax.broadcasted_iota(jnp.int32, (8, width), 0)
    lane = lax.broadcasted_iota(jnp.int32, (8, width), 1)
    sel = ((lane >= rowid * HD) & (lane < (rowid + 1) * HD)).astype(F32).astype(BF)
    qi = ds(i * QB, QB)
    q = q_ref[qi, :]
    do = do_ref[qi, :]
    z = jnp.zeros_like(q)
    qm = [jnp.where(hm[h], q, z) for h in range(heads)]
    dom = [jnp.where(hm[h], do, z) for h in range(heads)]
    qcat = jnp.concatenate(qm, axis=0)
    docat = jnp.concatenate(dom, axis=0)
    prod = do.astype(F32) * o_ref[qi, :].astype(F32)
    high = prod.astype(BF)
    low = (prod - high.astype(F32)).astype(BF)
    delta = dg(sel, high, 1, 1) + dg(sel, low, 1, 1)
    lse = lse_ref[:, qi]
    sq = sr_ref[0:1, qi]

    def step(j, dqs, diag):
        kj = ds(j * QB, QB)
        k = k_ref[kj, :]
        v = v_ref[kj, :]
        mask = allow_mask(kc_ref[kj, 0:1], sq, diag)
        ps, dss, res = [], [], []
        for h in range(heads):
            s = dg(k, qm[h], 1, 1)
            dp = dg(v, dom[h], 1, 1)
            p = jnp.exp(jnp.where(mask, s - lse[h : h + 1, :], NEG))
            score_grad = (p * (dp - delta[h : h + 1, :])).astype(BF)
            ps.append(p.astype(BF))
            dss.append(score_grad)
            res.append(dqs[h] + dot(kt[h * HD : (h + 1) * HD, kj], score_grad))
        dv[kj, :] += dot(jnp.concatenate(ps, axis=1), docat)
        dk[kj, :] += dot(jnp.concatenate(dss, axis=1), qcat)
        return tuple(res)

    dqs = tuple(jnp.zeros((HD, QB), F32) for _ in range(heads))
    dqs = step(i, dqs, True)
    dqs = lax.fori_loop(lo, hi, lambda j, d: step(j, d, False), dqs)
    dq = jnp.concatenate(list(dqs) + [jnp.zeros((width - heads * HD, QB), F32)], axis=0).T * 0.125
    out[qi, 0:width] = turn_lanes(dq, tab[qi, :], -1).astype(BF)


def attn_bwd_kernel(
    heads, seg, live, q_in, k_in, v_in, o_in, do_in, lse_ref, sr_ref, kc_ref, tab_in, out_ref,
    q, k, v, o, do, tab, out, kt, dk, dv, lsem, osem,
):
    rows, width = q.shape
    n = rows // QB
    loads = load([(k_in, k), (q_in, q), (v_in, v), (do_in, do), (o_in, o), (tab_in, tab)], lsem)
    dk[...] = jnp.zeros_like(dk)
    dv[...] = jnp.zeros_like(dv)
    loads[0].wait()
    turn_blocks(k, kt)
    for c in loads[1:]:
        c.wait()

    def qloop(i, _):
        lo, hi = block_bounds(seg, live, i, n)
        attn_bwd_block(i, lo, hi, heads, q, k, v, o, do, kt, lse_ref, sr_ref, kc_ref, tab, dk, dv, out)
        return 0

    lax.fori_loop(0, n, qloop, 0)

    def leave(i):
        rr = ds(i * QB, QB)
        return pltpu.make_async_copy(out.at[rr], out_ref.at[rr], osem.at[i])

    def finish(i, _):
        ii = ds(i * QB, QB)
        out[ii, width : 2 * width] = turn_lanes(dk[ii, :], tab[ii, :], -1).astype(BF)
        out[ii, 2 * width : 3 * width] = dv[ii, :].astype(BF)
        leave(i).start()
        return 0

    lax.fori_loop(0, n, finish, 0)

    def drain(i, _):
        leave(i).wait()
        return 0

    lax.fori_loop(0, n, drain, 0)


def attn_bwd(heads, seg, live, q, k, v, o, do, lse, sr, kc, tab):
    rows, width = q.shape
    buf = pltpu.VMEM((rows, width), BF)
    return pl.pallas_call(
        functools.partial(attn_bwd_kernel, heads),
        out_shape=sds((rows, 3 * width), BF),
        in_specs=[SMEM, SMEM] + [ANY] * 5 + [VMEM] * 3 + [ANY],
        out_specs=ANY,
        scratch_shapes=[buf, buf, buf, buf, buf, pltpu.VMEM(tab.shape, F32), pltpu.VMEM((rows, 3 * width), BF),
                        pltpu.VMEM((width, rows), BF), pltpu.VMEM((rows, width), F32), pltpu.VMEM((rows, width), F32),
                        DMA((6,)), DMA((rows // QB,))],
        compiler_params=pltpu.CompilerParams(vmem_limit_bytes=67043328),
        cost_estimate=cost(26),
        name="attn_bwd",
    )(seg, live, q, k, v, o, do, lse, sr, kc, tab)


class Mesh:
    def __init__(self, dp, tensor):
        self.dp, self.tensor = dp, tensor
        self.s, self.z, self.t = lax.axis_index("section"), lax.axis_index("dp"), lax.axis_index("tensor")
        self.x, self.y = self.t % 2, self.t // 2
        self.px, self.py = 2 * self.y + (1 - self.x), 2 * (1 - self.y) + self.x
        self.mate = {"section": 1 - self.s}
        self.beside = {"tensor": self.px}
        self.beside_mate = {"tensor": self.px, "section": 1 - self.s}
        self.across = {"tensor": self.py}
        self.across_mate = {"tensor": self.py, "section": 1 - self.s}
        self.ring = [{"dp": (self.z + d) % dp} for d in range(1, dp)]
        self.group = [{"tensor": (self.t + d) % tensor} for d in range(1, tensor)]
        self.quarter = 2 * self.s + self.x

    def across_core(self, core):
        return {"tensor": self.py, "section": core}


def greet(peers):
    bar = pltpu.get_barrier_semaphore()
    for peer in peers:
        pl.semaphore_signal(bar, inc=1, device_id=peer, device_id_type=MESH)
    pl.semaphore_wait(bar, len(peers))


def push(src, dst, ssem, rsem, peer):
    return pltpu.make_async_remote_copy(
        src_ref=src, dst_ref=dst, send_sem=ssem, recv_sem=rsem, device_id=peer, device_id_type=MESH
    )


def pick(i, values):
    out = values[-1]
    for n in range(len(values) - 2, -1, -1):
        out = jnp.where(i == n, values[n], out)
    return out


class Tokens:
    def __init__(self, me, seq):
        self.me, self.half = me, seq // 8

    def start_of(self, a, b, h):
        return (4 * a + 2 * b + h) * self.half

    def rows(self, a, b, h):
        return ds(self.start_of(a, b, h), self.half)

    def own(self, a):
        return self.start_of(a, self.me.x, self.me.s)


class Gather(Tokens):
    def __init__(self, me, full, ssem, rsem, first=0):
        super().__init__(me, full.shape[0])
        self.full, self.ssem, self.rsem, self.first = full, ssem, rsem, first

    def side(self, n):
        return self.first if n == 0 else 1 - self.first

    def plan(self, i):
        me, a = self.me, self.side(i % 2)
        ref = self.full.at[self.rows(a, (1 - me.x) if i >= 4 else me.x, me.s)]
        return push(ref, ref, self.ssem.at[i], self.rsem.at[i], me.beside if i in (2, 3) else me.mate)

    def start(self, n):
        self.plan(n).start()
        self.plan(2 + n).start()

    def order(self, i):
        me = self.me
        a = pick(i, [self.side(n) for n in (0, 1, 0, 1, 0, 0, 1, 1)])
        b = jnp.where(i < 4, me.x, 1 - me.x)
        h = pick(i, [me.s, me.s, 1 - me.s, 1 - me.s, me.s, 1 - me.s, me.s, 1 - me.s])
        return self.start_of(a, b, h)

    def step(self, i):
        if i in (2, 3):
            self.plan(i - 2).wait_recv()
        if i in (4, 6):
            n = i // 2 - 2
            self.plan(2 + n).wait_recv()
            self.plan(4 + n).start()
        if i in (5, 7):
            self.plan(4 + i // 2 - 2).wait_recv()

    def arrive(self, i):
        for n in range(2, 8):

            @pl.when(i == n)
            def _(n=n):
                self.step(n)

    def finish(self):
        for i in range(6):
            self.plan(i).wait_send()

    def run(self, work):
        def body(i, _):
            self.arrive(i)
            work(self.order(i), i)
            return 0

        lax.fori_loop(0, 8, body, 0)
        self.finish()


class Scatter(Tokens):
    def __init__(self, me, part, mr, xr, ssem, rsem, first=0):
        super().__init__(me, part.shape[0])
        self.part, self.mr, self.xr, self.ssem, self.rsem, self.first = part, mr, xr, ssem, rsem, first

    def side(self, n):
        return self.first if n == 0 else 1 - self.first

    def plan(self, i):
        me = self.me
        if i < 4:
            b = (1 - me.x) if i < 2 else me.x
            src, dst, peer = self.rows(self.side(i % 2), b, 1 - me.s), self.mr.at[i], me.mate
        else:
            src, dst, peer = self.rows(self.side(i - 4), 1 - me.x, me.s), self.xr.at[i - 4], me.beside
        return push(self.part.at[src], dst, self.ssem.at[i], self.rsem.at[i], peer)

    def run(self, work, early=None):
        me = self.me

        def body(i, _):
            k = i // 2
            b = jnp.where(k < 2, 1 - me.x, me.x)
            h = jnp.where(i % 2 == 0, 1 - me.s, me.s)
            work(self.start_of(jnp.where(k % 2 == 0, self.side(0), self.side(1)), b, h), i)
            for n in range(4):

                @pl.when(i == 2 * n)
                def _(n=n):
                    self.plan(n).start()

            for n in range(2):

                @pl.when(i == 2 * n + 1)
                def _(n=n):
                    self.plan(n).wait_recv()
                    base = self.start_of(self.side(n), 1 - me.x, me.s)

                    def add(j, _):
                        rr = ds(base + j * SUB, SUB)
                        got = self.mr[n, ds(j * SUB, SUB), :].astype(F32)
                        self.part[rr, :] = (self.part[rr, :].astype(F32) + got).astype(BF)
                        return 0

                    lax.fori_loop(0, self.half // SUB, add, 0)
                    self.plan(4 + n).start()

            return 0

        lax.fori_loop(0, 8, body, 0)
        if early is not None:
            early()

    def arrive(self, n):
        self.plan(2 + n).wait_recv()
        self.plan(4 + n).wait_recv()

    def total(self, n, i):
        rr = ds(self.own(self.side(n)) + i * SUB, SUB)
        sub = ds(i * SUB, SUB)
        return self.part[rr, :].astype(F32) + self.mr[2 + n, sub, :].astype(F32) + self.xr[n, sub, :].astype(F32)

    def finish(self):
        for i in range(6):
            self.plan(i).wait_send()


def scatter_scratch(rows, width):
    half = rows // 8
    return [
        pltpu.VMEM((rows, width), BF),
        pltpu.VMEM((4, half, width), BF),
        pltpu.VMEM((2, half, width), BF),
        DMA((6,)),
        DMA((6,)),
    ]


class WeightGather:
    def __init__(self, me, layer, shard, full, gat, groups, sems):
        self.me, self.layer, self.shard, self.full, self.gat, self.groups = me, layer, shard, full, gat, groups
        self.own, self.wss, self.wrs, self.fss, self.frs, self.yss, self.yrs = sems
        self.rows = shard.shape[0]
        self.collects = me.s == layer
        self.keeps = me.y == layer

    def block(self, ref, zz, g):
        a, b = self.groups[g]
        return ref.at[ds(zz * self.rows, self.rows), a:b]

    def mine(self, g):
        a, b = self.groups[g]
        return self.shard.at[:, a:b]

    def local(self, g):
        return pltpu.make_async_copy(self.mine(g), self.block(self.full, self.me.z, g), self.own.at[g])

    def out(self, g, d, ref):
        dst = self.block(ref, self.me.z, g)
        return push(self.mine(g), dst, self.wss.at[g, d], self.wrs.at[g, d], self.me.ring[d])

    def hand(self, g, d, ref, across):
        zz = (self.me.z + self.me.dp - d) % self.me.dp
        src = self.mine(g) if d == 0 else self.block(ref, zz, g)
        ss, rs = (self.yss, self.yrs) if across else (self.fss, self.frs)
        peer = self.me.across_core(self.me.y) if across else self.me.mate
        return push(src, self.block(self.full, zz, g), ss.at[g, d], rs.at[g, d], peer)

    def both(self, do):
        @pl.when(self.collects & self.keeps)
        def _():
            do(self.full, True)

        @pl.when(self.collects & jnp.logical_not(self.keeps))
        def _():
            do(self.gat, False)

    def send_ring(self):
        def do(ref, keeps):
            for g in range(len(self.groups)):
                for d in range(self.me.dp - 1):
                    self.out(g, d, ref).start()

        self.both(do)

    def send_own(self, g):
        def do(ref, keeps):
            self.hand(g, 0, ref, True).start()
            if keeps:
                self.local(g).start()
            else:
                self.hand(g, 0, ref, False).start()

        self.both(do)

    def forward(self, g, blocks=None):
        def do(ref, keeps):
            for d in range(self.me.dp - 1) if blocks is None else blocks:
                self.out(g, d, ref).wait_recv()
                self.hand(g, d + 1, ref, True).start()
                if not keeps:
                    self.hand(g, d + 1, ref, False).start()

        self.both(do)

    def ready(self, g):
        me = self.me

        @pl.when(self.collects & self.keeps)
        def _():
            self.local(g).wait()

        @pl.when(me.s != me.y)
        def _():
            for d in range(me.dp):
                self.hand(g, d, self.full, True).wait_recv()

        @pl.when((me.s == me.y) & jnp.logical_not(self.collects))
        def _():
            for d in range(me.dp):
                self.hand(g, d, self.full, False).wait_recv()

    def finish(self):
        def do(ref, keeps):
            for g in range(len(self.groups)):
                for d in range(self.me.dp - 1):
                    self.out(g, d, ref).wait_send()
                for d in range(self.me.dp):
                    self.hand(g, d, ref, True).wait_send()
                    if not keeps:
                        self.hand(g, d, ref, False).wait_send()

        self.both(do)

    @staticmethod
    def scratch(dp, n):
        return [DMA((n,)), DMA((n, dp - 1)), DMA((n, dp - 1))] + [DMA((n, dp))] * 4


class GradReduce:
    def __init__(self, me, layer, src, mine, got, across, sb, rb, own, sems):
        self.me, self.layer, self.src, self.mine, self.got, self.across = me, layer, src, mine, got, across
        self.sb, self.rb, self.own = sb, rb, own
        self.hss, self.hrs, self.yss, self.yrs, self.pss, self.prs = sems
        self.rows = own.shape[0]
        self.sums = me.s == layer
        self.holds = me.y == layer

    @staticmethod
    def scratch(dp):
        return [DMA((1,)), DMA((1,)), DMA((dp,)), DMA((dp,)), DMA((dp - 1,)), DMA((dp - 1,))]

    def hand(self):
        return push(self.src, self.got, self.hss.at[0], self.hrs.at[0], self.me.mate)

    def zz(self, d):
        return (self.me.z + d + 1) % self.me.dp

    def over(self, d):
        rr = ds(self.zz(d) * self.rows, self.rows)
        peer = self.me.across_core(self.layer)
        return push(self.src.at[rr], self.across.at[rr], self.yss.at[d], self.yrs.at[d], peer)

    def out(self, d):
        return push(self.sb.at[d], self.rb.at[d], self.pss.at[d], self.prs.at[d], self.me.ring[d])

    def send(self):
        me = self.me

        @pl.when(me.s != me.y)
        def _():
            for d in range(me.dp):
                self.over(d).start()

        @pl.when((me.s == me.y) & jnp.logical_not(self.sums))
        def _():
            self.hand().start()

    def step(self, d):
        me = self.me

        @pl.when(self.sums)
        def _():
            if d == 0:

                @pl.when(jnp.logical_not(self.holds))
                def _():
                    self.hand().wait_recv()

            self.over(d).wait_recv()
            last = d == me.dp - 1

            def add(ref):
                def body(i, _):
                    rr = ds(self.zz(d) * self.rows + i * 16, 16)
                    value = ref[rr, :].astype(F32) + self.across[rr, :].astype(F32)
                    if last:
                        self.own[ds(i * 16, 16), :] = value
                    else:
                        self.sb[d, ds(i * 16, 16), :] = value.astype(BF)
                    return 0

                lax.fori_loop(0, self.rows // 16, body, 0)

            if self.mine is self.got:
                add(self.mine)
            else:

                @pl.when(self.holds)
                def _():
                    add(self.mine)

                @pl.when(jnp.logical_not(self.holds))
                def _():
                    add(self.got)

            if not last:
                self.out(d).start()

    def collect(self):
        me = self.me

        @pl.when(self.sums)
        def _():
            for d in range(me.dp - 1):
                self.out(d).wait_recv()

                def add(i, _, d=d):
                    rr = ds(i * 16, 16)
                    self.own[rr, :] += self.rb[d, rr, :].astype(F32)
                    return 0

                lax.fori_loop(0, self.rows // 16, add, 0)
            for d in range(me.dp - 1):
                self.out(d).wait_send()

    def finish(self):
        me = self.me

        @pl.when(me.s != me.y)
        def _():
            for d in range(me.dp):
                self.over(d).wait_send()

        @pl.when((me.s == me.y) & jnp.logical_not(self.sums))
        def _():
            self.hand().wait_send()


class VectorGather:
    def __init__(self, me, sv, buf, ss, rs, own):
        self.me, self.sv, self.buf, self.ss, self.rs, self.own = me, sv, buf, ss, rs, own

    def local(self):
        me = self.me
        return pltpu.make_async_copy(self.sv, self.buf.at[me.s, me.t, me.z], self.own)

    def stage(self, n):
        me = self.me
        if n == 0:
            dst = self.buf.at[me.s, me.t, me.z]
            return [push(self.sv, dst, self.ss.at[d], self.rs.at[d], peer) for d, peer in enumerate(me.ring)]
        base = me.dp - 1
        if n == 1:
            ref = self.buf.at[me.s, me.t]
            return [
                push(ref, ref, self.ss.at[base + d], self.rs.at[base + d], peer) for d, peer in enumerate(me.group)
            ]
        i = base + me.tensor - 1
        ref = self.buf.at[me.s]
        return [push(ref, ref, self.ss.at[i], self.rs.at[i], me.mate)]

    def send(self, n):
        if n == 0:
            self.local().start()
        for c in self.stage(n):
            c.start()

    def wait(self, n):
        if n == 0:
            self.local().wait()
        for c in self.stage(n):
            c.wait_recv()

    def finish(self):
        for n in range(3):
            for c in self.stage(n):
                c.wait_send()

    def build(self, vecs, heads, own, qw, fw):
        me, buf = self.me, self.buf
        for layer in range(2):
            wide = [buf[layer, tt, zz, 0:8, :][:, 0:own] for zz in range(me.dp) for tt in range(me.tensor)]
            vecs[layer, 0:8, :] = jnp.concatenate(wide, axis=1)
            here = [buf[layer, me.quarter, zz] for zz in range(me.dp)]
            by = [jnp.concatenate([p[6 + h : 7 + h, 0:qw] for p in here], axis=1) for h in range(heads)]
            qb = []
            for part in range(3):
                qb += [b[:, part * HD : (part + 1) * HD] for b in by] + [jnp.zeros((1, HW - heads * HD), F32)]
            vecs[layer, 6:7, :] = jnp.concatenate(qb, axis=1)
            fb = [p[6 + heads + h : 7 + heads + h, 0:fw] for h in range(heads) for p in here]
            vecs[layer, 7:8, :] = jnp.concatenate(fb, axis=1)


class VectorReduce:
    def __init__(self, me, va, vr, ss, rs):
        self.me, self.va, self.vr, self.ss, self.rs = me, va, vr, ss, rs

    def stage(self, n):
        me, va, vr, ss, rs = self.me, self.va, self.vr, self.ss, self.rs
        peers, base = [([me.across], 0), (me.ring, 1), ([me.mate, me.beside, me.beside_mate], me.dp)][n]
        return [push(va.at[n], vr.at[base + d], ss.at[base + d], rs.at[base + d], p) for d, p in enumerate(peers)]

    def send(self, n):
        for c in self.stage(n):
            c.start()

    def add(self, n, out):
        base = [0, 1, self.me.dp][n]
        for c in self.stage(n):
            c.wait_recv()
        if n < 2:
            total = self.va[n]
            for d in range(len(self.stage(n))):
                total = total + self.vr[base + d]
            out[...] = total
            return
        mine, mate = self.va[2], self.vr[base]
        row = lax.broadcasted_iota(jnp.int32, mine.shape, 0)
        quarter = jnp.where(self.me.s == self.me.y, mine, mate)
        out[...] = jnp.where(row % 8 < 6, mine + mate + self.vr[base + 1] + self.vr[base + 2], quarter)

    def finish(self):
        for n in range(3):
            for c in self.stage(n):
                c.wait_send()


def document_tables(seg, live, fr_ref, tab, srow, kcol):
    seq = seg.shape[1]
    count = lax.broadcasted_iota(jnp.int32, seg.shape, 1)
    start = jnp.zeros_like(seg)
    for doc in range(DOCS - 1):
        before = jnp.sum(jnp.where(seg == doc, 1.0, 0.0), axis=1, keepdims=True).astype(jnp.int32)
        start = start + jnp.where(seg > doc, before, 0)
    ang = fr_ref[:, 0:1] * (count - start).astype(F32)
    cs, sn = jnp.cos(ang), jnp.sin(ang)
    one = jnp.ones((HD - ROT, seq), F32)
    tab[:, 0:128] = jnp.concatenate([cs, cs, one] * 2, axis=0).T
    tab[:, 128:256] = jnp.concatenate([-sn, sn, jnp.zeros_like(one)] * 2, axis=0).T
    srow[...] = jnp.broadcast_to(seg, srow.shape)
    keys = jnp.where(count < live * LIVE, seg, -1).astype(F32)
    for b in range(seq // QB):
        part = jnp.broadcast_to(keys[:, b * QB : (b + 1) * QB], (128, QB))
        kcol[b * QB : (b + 1) * QB, :] = part.T.astype(jnp.int32)


QKV, FC1, FC2, OUT = 0, 1, 2, 3


def columns(model, ff):
    return {"qkv": 0, "fc1": 3 * HW, "fc2": 3 * HW + ff, "out": 3 * HW + 2 * ff, "end": 3 * HW + 2 * ff + HW}


def project_norm(r0, half, hf, vec, n1, n2):
    rows = ds(r0, half)
    xc, r = norm_stats(hf[rows, :].astype(F32))
    xh = xc * r
    n1[rows, :] = (xh * vec[0:1, :] + vec[1:2, :]).astype(BF)
    n2[rows, :] = (xh * vec[3:4, :] + vec[4:5, :]).astype(BF)


def project_qkv(r0, half, wqkv, vec, tab, n1, q, k, v):
    rows = ds(r0, half)
    a = n1[rows, :]
    for part, dst in enumerate((q, k, v)):
        cols = slice(part * HW, (part + 1) * HW)
        y = dot(a, wqkv[:, cols]) + vec[6:7, cols]
        if part < 2:
            y = turn_lanes(y, tab[rows, :], 1)
        if part == 0:
            y = y * 0.125
        dst[rows, :] = y.astype(BF)


def project_fc1(r0, half, wfc1, vec, n2, g, gp):
    rows = ds(r0, half)
    a = n2[rows, :]
    for b in range(wfc1.shape[1] // 256):
        cols = slice(b * 256, (b + 1) * 256)
        y = dot(a, wfc1[:, cols]) + vec[7:8, cols]
        cdf = 0.5 + 0.5 * lax.erf(y * 0.7071067811865476)
        g[rows, cols] = (y * cdf).astype(BF)
        gp[rows, cols] = (cdf + y * jnp.exp(-0.5 * y * y) * 0.3989422804014327).astype(BF)


def branch_out(r0, half, o, g, wout, wfc2, part):
    rows = ds(r0, half)
    for b in range(part.shape[1] // 256):
        cols = slice(b * 256, (b + 1) * 256)
        y = dg(o[rows, :], wout[cols, :], 1, 1) + dg(g[rows, :], wfc2[cols, :], 1, 1)
        part[rows, cols] = y.astype(BF)


def back_head(r0, half, dyf, hf, g, gp, n2, o, wfc1, wfc2, wout, vec, do, e2, da, acc, vg):
    rows = ds(r0, half)
    model, ff = wfc1.shape
    dy = dyf[rows, :]
    for b in range(ff // 256):
        cols = slice(b * 256, (b + 1) * 256)
        y = dot(dy, wfc2[:, cols]) * gp[rows, cols].astype(F32)
        low = y.astype(BF)
        da[:, cols] = low
        vg[7:8, cols] += jnp.sum(low.astype(F32), axis=0, keepdims=True)
    do[rows, :] = dot(dy, wout[...]).astype(BF)
    xc, r = norm_stats(hf[rows, :].astype(F32))
    xh = xc * r
    for b in range(model // 256):
        cols = slice(b * 256, (b + 1) * 256)
        dn = dg(da[...], wfc1[cols, :], 1, 1)
        vg[3:4, cols] += jnp.sum(dn * xh[:, cols], axis=0, keepdims=True)
        vg[4:5, cols] += jnp.sum(dn, axis=0, keepdims=True)
        e2[rows, cols] = (dn * vec[3:4, cols]).astype(BF)
    n2t = n2[rows, :].T
    dyt = dy.T
    for b in range(ff // 256):
        cols = slice(b * 256, (b + 1) * 256)
        acc[:, cols] += dot(n2t, da[:, cols])
        acc[:, ff + b * 256 : ff + (b + 1) * 256] += dot(dyt, g[rows, cols])
    acc[:, 2 * ff :] += dot(dyt, o[rows, :])


def back_tail(r0, half, dmix, hf, e2, wqkv, vec, part, vg):
    rows = ds(r0, half)
    dm = dmix[rows, :]
    vg[6:7, :] += jnp.sum(dm.astype(F32), axis=0, keepdims=True)
    xc, r = norm_stats(hf[rows, :].astype(F32))
    xh = xc * r
    for b in range(part.shape[1] // 256):
        cols = slice(b * 256, (b + 1) * 256)
        dn = dg(dm, wqkv[cols, :], 1, 1)
        vg[0:1, cols] += jnp.sum(dn * xh[:, cols], axis=0, keepdims=True)
        vg[1:2, cols] += jnp.sum(dn, axis=0, keepdims=True)
        part[rows, cols] = (dn * vec[0:1, cols] + e2[rows, cols].astype(F32)).astype(BF)


def qkv_grad(n1, dmix, acc, half):
    acc[...] = jnp.zeros_like(acc)

    def body(i, _):
        rows = ds(i * half, half)
        n1t = n1[rows, :].T
        for b in range(3):
            cols = slice(b * HW, (b + 1) * HW)
            acc[:, cols] += dot(n1t, dmix[rows, cols])
        return 0

    lax.fori_loop(0, n1.shape[0] // half, body, 0)


def store_low(acc, out):
    def body(i, _):
        rr = ds(i * SUB, SUB)
        out[rr, :] = acc[rr, :].astype(BF)
        return 0

    lax.fori_loop(0, acc.shape[0] // SUB, body, 0)


def residual_out(sc, own, vec, write, after=None):
    for a in range(2):
        sc.arrive(a)

        def body(i, _, a=a):
            base = own[ds(sc.own(sc.side(a)) + i * SUB, SUB), :].astype(F32)
            write(a, i, (base + sc.total(a, i) + vec[2:3, :] + vec[5:6, :]).astype(BF))
            return 0

        lax.fori_loop(0, sc.half // SUB, body, 0)
        if after is not None:
            after(a)


def grad_out(sc, dy, hf, vec, write, after=None):
    for a in range(2):
        sc.arrive(a)

        def body(i, _, a=a):
            rr = ds(sc.own(sc.side(a)) + i * SUB, SUB)
            xc, r = norm_stats(hf[rr, :].astype(F32))
            xh = xc * r
            e = sc.total(a, i)
            m1 = jnp.mean(e, axis=-1, keepdims=True)
            m2 = jnp.mean(e * xh, axis=-1, keepdims=True)
            write(a, i, (dy(a, i).astype(F32) + r * (e - m1 - xh * m2)).astype(BF))
            return 0

        lax.fori_loop(0, sc.half // SUB, body, 0)
        if after is not None:
            after(a)


def column_sum(tok, ref, vg, row):
    total = jnp.zeros((1, ref.shape[1]), F32)
    for a in range(2):

        def body(i, acc, a=a):
            return acc + jnp.sum(ref[ds(tok.own(a) + i * SUB, SUB), :].astype(F32), axis=0, keepdims=True)

        total = lax.fori_loop(0, tok.half // SUB, body, total)
    vg[row : row + 1, :] = total


def load(pairs, sem):
    copies = [pltpu.make_async_copy(a, b, sem.at[i]) for i, (a, b) in enumerate(pairs)]
    for c in copies:
        c.start()
    return copies


def params(cid):
    return pltpu.CompilerParams(collective_id=cid, has_side_effects=True, vmem_limit_bytes=67043328)


def cost(us):
    return pl.CostEstimate(flops=int(us * 8e8), bytes_accessed=0, transcendentals=0)


class Stores:
    def __init__(self, pairs, half, sem):
        self.pairs, self.half, self.sem = pairs, half, sem

    def copy(self, n, r0, i):
        src, dst = self.pairs[n]
        rows = ds(r0, self.half)
        return pltpu.make_async_copy(src.at[rows], dst.at[rows], self.sem.at[n, i])

    def start(self, which, r0, i):
        for n in which:
            self.copy(n, r0, i).start()

    def finish(self):
        def body(i, _):
            for n in range(len(self.pairs)):
                self.copy(n, i * self.half, i).wait()
            return 0

        lax.fori_loop(0, 8, body, 0)


def in_kernel(
    cfg, in_ref, cot_ref, seg_ref, live, w_ref, sv_ref, fr_ref,
    hf_o, n1_o, n2_o, g_o, gp_o, tab_o, w_o, q_o, k_o, v_o, cf_o, vecs, srow, kcol,
    hf, n1, n2, g, gp, tab, q, k, v, wfull, gat, vb, cot, gss, grs, css, crs, yss, yrs, lsem, ssem, vss, vrs, *wsems,
):
    col, dp, tensor = cfg["col"], cfg["dp"], cfg["tensor"]
    me = Mesh(dp, tensor)
    ga = Gather(me, hf, gss, grs, me.y)
    gc = Gather(me, cf_o, css, crs, me.y)
    half = ga.half
    part = ds(me.s * half, half)
    first = pltpu.make_async_copy(in_ref.at[me.y, 0, part], hf.at[ds(ga.own(me.y), half)], lsem.at[0])
    first.start()
    up = pltpu.make_async_copy(cot_ref.at[me.y, 0, part], cot, lsem.at[4])
    up.start()
    greet([me.mate, me.across_mate] + me.ring + me.group)
    over = [
        push(ref.at[1 - me.y, 0, part], full.at[ds(ga.own(me.y), half)], yss.at[n], yrs.at[n], me.across)
        for n, (ref, full) in enumerate(((in_ref, hf), (cot_ref, cf_o)))
    ]
    wg = WeightGather(me, 0, w_ref, wfull, gat, cfg["groups"], wsems)
    vg = VectorGather(me, sv_ref, vb, vss, vrs, lsem.at[1])
    st = Stores([(hf, hf_o), (n1, n1_o), (n2, n2_o), (g, g_o), (gp, gp_o), (q, q_o), (k, k_o), (v, v_o)], half, ssem)
    vg.send(0)
    wg.send_ring()
    first.wait()
    document_tables(seg_ref[me.y], live[me.y, 0], fr_ref, tab, srow, kcol)
    vg.wait(0)
    vg.send(1)
    ga.start(0)
    over[0].start()
    wg.send_own(0)
    tab_out = pltpu.make_async_copy(tab, tab_o, lsem.at[2])
    tab_out.start()
    vg.wait(1)
    vg.send(2)
    up.wait()
    cot_out = pltpu.make_async_copy(cot, cf_o.at[ds(gc.own(me.y), half)], lsem.at[5])
    cot_out.start()
    vg.wait(2)
    vg.build(vecs, cfg["heads"], cfg["own"], cfg["qw"], cfg["fw"])
    vec = vecs.at[0]

    def norm(r0, i):
        project_norm(r0, half, hf, vec, n1, n2)
        st.start((0, 1, 2), r0, i)

        @pl.when(i == 0)
        def _():
            over[0].wait_recv()
            ga.start(1)

        @pl.when(i == 1)
        def _():
            wg.forward(0)
            wg.send_own(1)
            wg.send_own(2)

    ga.run(norm)
    cot_out.wait()
    gc.start(0)
    wg.ready(0)

    def qkv(i, _):
        r0 = ga.order(i)
        project_qkv(r0, half, wfull.at[:, 0 : col["fc1"]], vec, tab, n1, q, k, v)
        st.start((5, 6, 7), r0, i)
        return 0

    lax.fori_loop(0, 8, qkv, 0)
    wg.forward(1)
    over[1].start()
    wg.ready(1)

    def fc1(i, _):
        r0 = ga.order(i)
        project_fc1(r0, half, wfull.at[:, col["fc1"] : col["fc2"]], vec, n2, g, gp)
        st.start((3, 4), r0, i)

        @pl.when(i == 6)
        def _():
            wg.forward(2)

        return 0

    lax.fori_loop(0, 8, fc1, 0)
    gc.step(2)
    gc.step(4)
    over[1].wait_recv()
    gc.start(1)
    st.finish()
    tab_out.wait()
    wg.ready(2)
    w_out = pltpu.make_async_copy(wfull, w_o, lsem.at[3])
    w_out.start()
    for n in (3, 5, 6, 7):
        gc.step(n)
    wg.finish()
    vg.finish()
    gc.finish()
    for c in over:
        c.wait_send()
    w_out.wait()


def layer_in(cfg, inputs, cotangent, segments, live, w, sv, fr):
    seq, model, ff = segments.shape[2], inputs.shape[3], cfg["ff"]
    dp, tensor = cfg["dp"], cfg["tensor"]
    rows, hidden = sds((seq, model), BF), sds((seq, ff), BF)
    heads = sds((seq, HW), BF)
    nv = dp - 1 + tensor
    wide, wide_h, wide_q = pltpu.VMEM((seq, model), BF), pltpu.VMEM((seq, ff), BF), pltpu.VMEM((seq, HW), BF)
    weights = pltpu.VMEM((model, w.shape[1]), BF)
    return pl.pallas_call(
        functools.partial(in_kernel, cfg),
        out_shape=(rows, rows, rows, hidden, hidden, sds((seq, 256), F32), sds((model, w.shape[1]), BF),
                   heads, heads, heads, rows,
                   sds((2, 8, model), F32), sds((8, seq), jnp.int32), sds((seq, 128), jnp.int32)),
        in_specs=[ANY, ANY, VMEM, SMEM, VMEM, VMEM, VMEM],
        out_specs=(ANY,) * 11 + (VMEM,) * 3,
        scratch_shapes=[
            wide, wide, wide, wide_h, wide_h, pltpu.VMEM((seq, 256), F32), wide_q, wide_q, wide_q,
            weights, weights, pltpu.VMEM((2, tensor, dp) + sv.shape, F32),
            pltpu.VMEM((seq // 8, model), BF),
            DMA((6,)), DMA((6,)), DMA((6,)), DMA((6,)), DMA((2,)), DMA((2,)), DMA((6,)), DMA((8, 8)),
            DMA((nv,)), DMA((nv,)),
        ]
        + WeightGather.scratch(dp, 3),
        compiler_params=params(2),
        cost_estimate=cost(45),
        name="layer_in",
    )(inputs, cotangent, segments, live, w, sv, fr)


def mid_kernel(
    cfg, q_in, k_in, v_in, srow, kcol, g_in, x_in, w_ref, w0, vecs, tab_in,
    o_o, lse, hf_o, n1_o, n2_o, g_o, gp_o, w_o, q_o, k_o, v_o,
    wout, wfc2, hf, n1, n2, g, gp, tab, wfull, gat, q, k, v, o, vt, s_scr,
    part, mr, xr, sss, srs, gss, grs, lsem, ssem, osem, *wsems,
):
    col, heads = cfg["col"], cfg["heads"]
    me = Mesh(cfg["dp"], cfg["tensor"])
    sc = Scatter(me, part, mr, xr, sss, srs)
    ga = Gather(me, hf, gss, grs)
    half = sc.half
    loads = load(
        [
            (v_in, v),
            (q_in, q),
            (k_in, k),
            (w0.at[:, col["out"] : col["end"]], wout),
            (w0.at[:, col["fc2"] : col["out"]], wfc2),
            (g_in, g),
            (tab_in, tab),
        ]
        + [(x_in.at[ds(sc.own(a), half)], hf.at[ds(sc.own(a), half)]) for a in range(2)],
        lsem,
    )
    greet([me.mate, me.beside, me.across, me.across_mate] + me.ring)
    wg = WeightGather(me, 1, w_ref, wfull, gat, cfg["groups"], wsems)
    wg.send_ring()
    for n in range(3):
        wg.send_own(n)
    loads[0].wait()
    turn_blocks(v, vt)
    for c in loads[1:]:
        c.wait()
    st = Stores([(hf, hf_o), (n1, n1_o), (n2, n2_o), (g, g_o), (gp, gp_o), (q, q_o), (k, k_o), (v, v_o)], half, ssem)
    st_o = Stores([(o, o_o)], half, osem)

    def out(r0, i):
        b = r0 // QB
        attn_fwd_block(b, jnp.maximum(b - DOC_MAX // QB, 0), b, heads, q, k, vt, srow, kcol, s_scr, o, lse)
        st_o.start((0,), r0, i)
        branch_out(r0, half, o, g, wout, wfc2, part)

        @pl.when(i == 6)
        def _():
            wg.forward(0)

    sc.run(out)

    def write(a, i, value):
        hf[ds(sc.own(a) + i * SUB, SUB), :] = value

    residual_out(sc, hf, vecs.at[0], write, ga.start)
    wg.forward(1)
    vec = vecs.at[1]

    def fc1(i):
        r0 = ga.order(i)
        project_fc1(r0, half, wfull.at[:, col["fc1"] : col["fc2"]], vec, n2, g, gp)
        st.start((3, 4), r0, i)

    def work(r0, i):
        project_norm(r0, half, hf, vec, n1, n2)

        @pl.when(i == 0)
        def _():
            wg.ready(0)

        project_qkv(r0, half, wfull.at[:, 0 : col["fc1"]], vec, tab, n1, q, k, v)
        st.start((0, 1, 2, 5, 6, 7), r0, i)

        @pl.when(i == 4)
        def _():
            wg.ready(1)

        @pl.when(i >= 4)
        def _():
            fc1(i - 4)

        @pl.when(i == 5)
        def _():
            wg.forward(2)

    ga.run(work)

    def late(i, _):
        fc1(i)
        return 0

    lax.fori_loop(4, 8, late, 0)
    st.finish()
    wg.ready(2)
    w_out = pltpu.make_async_copy(wfull, w_o, lsem.at[0])
    w_out.start()
    sc.finish()
    wg.finish()
    st_o.finish()
    w_out.wait()


def layer_mid(cfg, q, k, v, srow, kcol, g, xf, w, w0, vecs, tab):
    seq, model, ff = tab.shape[0], xf.shape[1], cfg["ff"]
    rows, hidden, heads = sds((seq, model), BF), sds((seq, ff), BF), sds((seq, HW), BF)
    wide, wide_h, wide_q = pltpu.VMEM((seq, model), BF), pltpu.VMEM((seq, ff), BF), pltpu.VMEM((seq, HW), BF)
    return pl.pallas_call(
        functools.partial(mid_kernel, cfg),
        out_shape=(heads, sds((8, seq), F32), rows, rows, rows, hidden, hidden, sds(w0.shape, BF), heads, heads, heads),
        in_specs=[ANY, ANY, ANY, VMEM, VMEM, ANY, ANY, VMEM, ANY, VMEM, ANY],
        out_specs=(ANY, VMEM) + (ANY,) * 9,
        scratch_shapes=[
            pltpu.VMEM((model, HW), BF), pltpu.VMEM((model, ff), BF),
            wide, wide, wide, wide_h, wide_h, pltpu.VMEM((seq, 256), F32),
            pltpu.VMEM(w0.shape, BF), pltpu.VMEM(w0.shape, BF),
            wide_q, wide_q, wide_q, wide_q, pltpu.VMEM((HW, seq), BF),
            pltpu.VMEM((cfg["heads"], DOC_MAX + QB, QB), F32),
        ]
        + scatter_scratch(seq, model)
        + [DMA((6,)), DMA((6,)), DMA((9,)), DMA((8, 8)), DMA((1, 8))]
        + WeightGather.scratch(cfg["dp"], 3),
        compiler_params=params(3),
        cost_estimate=cost(70),
        name="layer_mid",
    )(q, k, v, srow, kcol, g, xf, w, w0, vecs, tab)


def turn_kernel(
    cfg, o_in, g_in, hf_in, cf, w1, vecs, n2_in, gp_in, y_o, do_o, e2_o, gr_o, vg,
    o, g, hf, dyf, n2, gp, e2, do, y, gr, wout, wfc2, wfc1, da, acc,
    part, mr, xr, sss, srs, lsem, ssem,
):
    col = cfg["col"]
    me = Mesh(cfg["dp"], cfg["tensor"])
    sc = Scatter(me, part, mr, xr, sss, srs)
    half = sc.half
    loads = load(
        [
            (w1.at[:, col["out"] : col["end"]], wout),
            (w1.at[:, col["fc2"] : col["out"]], wfc2),
            (o_in, o),
            (g_in, g),
            (w1.at[:, col["fc1"] : col["fc2"]], wfc1),
            (cf, dyf),
            (gp_in, gp),
            (hf_in, hf),
            (n2_in, n2),
        ],
        lsem,
    )
    greet([me.mate, me.beside])
    for c in loads[:4]:
        c.wait()
    vec = vecs.at[1]
    st = Stores([(e2, e2_o), (do, do_o)], half, ssem)

    def early():
        vg[...] = jnp.zeros_like(vg)
        acc[...] = jnp.zeros_like(acc)
        for c in loads[4:]:
            c.wait()

        def head(i, _):
            r0 = i * half
            back_head(r0, half, dyf, hf, g, gp, n2, o, wfc1, wfc2, wout, vec, do, e2, da, acc, vg)
            st.start((0, 1), r0, i)
            return 0

        lax.fori_loop(0, 8, head, 0)

    sc.run(lambda r0, i: branch_out(r0, half, o, g, wout, wfc2, part), early)
    column_sum(sc, dyf, vg, 2)
    store_low(acc, gr)
    gr_out = pltpu.make_async_copy(gr, gr_o, lsem.at[0])
    gr_out.start()

    def write(a, i, value):
        y[a, ds(i * SUB, SUB), :] = value

    residual_out(sc, hf, vec, write)
    y_out = pltpu.make_async_copy(y, y_o, lsem.at[1])
    y_out.start()
    sc.finish()
    st.finish()
    gr_out.wait()
    y_out.wait()


def layer_turn(cfg, o, g, hf, cf, w1, vecs, n2, gp):
    seq, model = hf.shape
    ff = cfg["ff"]
    wide, hidden, heads = pltpu.VMEM((seq, model), BF), pltpu.VMEM((seq, ff), BF), pltpu.VMEM((seq, HW), BF)
    owned = (2, seq // 8, model)
    return pl.pallas_call(
        functools.partial(turn_kernel, cfg),
        out_shape=(
            sds(owned, BF),
            sds((seq, HW), BF),
            sds((seq, model), BF),
            sds((model, 2 * ff + HW), BF),
            sds((8, model), F32),
        ),
        in_specs=[ANY] * 5 + [VMEM, ANY, ANY],
        out_specs=(ANY,) * 4 + (VMEM,),
        scratch_shapes=[
            heads, hidden, wide, wide, wide, hidden, wide, heads, pltpu.VMEM(owned, BF),
            pltpu.VMEM((model, 2 * ff + HW), BF),
            pltpu.VMEM((model, HW), BF), pltpu.VMEM((model, ff), BF), pltpu.VMEM((model, ff), BF),
            pltpu.VMEM((seq // 8, ff), BF), pltpu.VMEM((model, 2 * ff + HW), F32),
        ]
        + scatter_scratch(seq, model)
        + [DMA((9,)), DMA((2, 8))],
        compiler_params=params(4),
        cost_estimate=cost(40),
        name="layer_turn",
    )(o, g, hf, cf, w1, vecs, n2, gp)


def back_kernel(
    cfg, dm_in, e2_in, cf, hf_in, n1_in, w1, w0, vecs, xf_in, g_in, gp_in, n2_in, o_in, gr1,
    dh_o, e2_o, do_o, vgf, vgd, out1_o, outq_o, gr_o,
    dmix, o, do, a, b, e2, g, gp, wqkv, wout, wfc2, wfc1, dhf, da, acc, gq, gr, got, gotq, acrq,
    sb, rb, sbq, rbq, out1, outq, part, mr, xr, sss, srs, gss, grs, lsem, ssem, *rsems,
):
    col, dp = cfg["col"], cfg["dp"]
    me = Mesh(dp, cfg["tensor"])
    ga = Gather(me, dhf, gss, grs)
    sc = Scatter(me, part, mr, xr, sss, srs)
    half = sc.half
    own = [ds(sc.own(n), half) for n in range(2)]
    loads = load(
        [
            (w1.at[:, col["qkv"] : col["fc1"]], wqkv),
            (dm_in, dmix),
            (hf_in, a),
            (e2_in, e2),
            (n1_in, b),
            (w0.at[:, col["out"] : col["end"]], wout),
            (w0.at[:, col["fc2"] : col["out"]], wfc2),
            (w0.at[:, col["fc1"] : col["fc2"]], wfc1),
            (g_in, g),
            (gp_in, gp),
            (o_in, o),
        ]
        + [(cf.at[rr], dhf.at[rr]) for rr in own],
        lsem,
    )
    gr_load = pltpu.make_async_copy(gr1, gr, lsem.at[13])
    holds = (me.s == 1) & (me.y == 1)

    @pl.when(holds)
    def _():
        gr_load.start()

    greet([me.mate, me.beside, me.across, me.across_mate] + me.ring)
    red1 = GradReduce(me, 1, gr1, gr, gr, got, sb, rb, out1, rsems[:6])
    redq = GradReduce(me, 1, gq, gq, gotq, acrq, sbq, rbq, outq, rsems[6:])
    st = Stores([(e2, e2_o), (do, do_o), (dhf, dh_o)], half, ssem)
    red1.send()
    vgf[...] = jnp.zeros_like(vgf)
    vgd[...] = jnp.zeros_like(vgd)
    for c in loads[:4]:
        c.wait()

    def early():
        loads[4].wait()
        small = acc.at[:, 0 : 3 * HW]
        qkv_grad(b, dmix, small, half)
        store_low(small, gq)
        redq.send()

        @pl.when(holds)
        def _():
            gr_load.wait()

        red1.step(0)

    sc.run(lambda r0, i: back_tail(r0, half, dmix, a, e2, wqkv, vecs.at[1], part, vgf), early)
    acc[...] = jnp.zeros_like(acc)
    again = pltpu.make_async_copy(n2_in, b, lsem.at[14])
    again.start()
    for c in loads[5:]:
        c.wait()
    for d in range(1, dp // 2):
        red1.step(d)

    def write(n, i, value):
        dhf[ds(sc.own(n) + i * SUB, SUB), :] = value

    grad_out(sc, lambda n, i: dhf[ds(sc.own(n) + i * SUB, SUB), :], a, vecs.at[1], write, ga.start)
    other = pltpu.make_async_copy(xf_in, a, lsem.at[15])
    other.start()
    again.wait()
    other.wait()

    def work(r0, i):
        back_head(r0, half, dhf, a, g, gp, b, o, wfc1, wfc2, wout, vecs.at[0], do, e2, da, acc, vgd)
        st.start((0, 1, 2), r0, i)

        @pl.when(i == 1)
        def _():
            for d in range(dp // 2, dp - 1):
                red1.step(d)

        @pl.when(i == 3)
        def _():
            red1.step(dp - 1)

        @pl.when(i == 5)
        def _():
            redq.step(0)

    ga.run(work)
    for d in range(1, dp):
        redq.step(d)
    store_low(acc, gr)
    gr_out = pltpu.make_async_copy(gr, gr_o, lsem.at[0])
    gr_out.start()
    column_sum(sc, dhf, vgd, 2)
    red1.collect()
    redq.collect()
    outs = [pltpu.make_async_copy(out1, out1_o, lsem.at[1]), pltpu.make_async_copy(outq, outq_o, lsem.at[2])]
    for c in outs:
        c.start()
    red1.finish()
    redq.finish()
    sc.finish()
    st.finish()
    gr_out.wait()
    for c in outs:
        c.wait()


def layer_back(cfg, dmix, e2, cf, hf, n1, w1, w0, vecs, xf, g, gp, n2, o, gr1):
    seq, model = hf.shape
    ff, dp = cfg["ff"], cfg["dp"]
    rows, nr, nq = model // dp, 2 * ff + HW, 3 * HW
    wide, hidden, heads = pltpu.VMEM((seq, model), BF), pltpu.VMEM((seq, ff), BF), pltpu.VMEM((seq, HW), BF)
    return pl.pallas_call(
        functools.partial(back_kernel, cfg),
        out_shape=(
            sds((seq, model), BF),
            sds((seq, model), BF),
            sds((seq, HW), BF),
            sds((8, model), F32),
            sds((8, model), F32),
            sds((rows, nr), F32),
            sds((rows, nq), F32),
            sds((model, nr), BF),
        ),
        in_specs=[ANY] * 7 + [VMEM] + [ANY] * 6,
        out_specs=(ANY, ANY, ANY, VMEM, VMEM, ANY, ANY, ANY),
        scratch_shapes=[
            pltpu.VMEM((seq, nq), BF), heads, heads, wide, wide, wide, hidden, hidden,
            pltpu.VMEM((model, nq), BF), pltpu.VMEM((model, HW), BF), pltpu.VMEM((model, ff), BF),
            pltpu.VMEM((model, ff), BF), wide, pltpu.VMEM((seq // 8, ff), BF), pltpu.VMEM((model, nr), F32),
            pltpu.VMEM((model, nq), BF), pltpu.VMEM((model, nr), BF), pltpu.VMEM((model, nr), BF),
            pltpu.VMEM((model, nq), BF), pltpu.VMEM((model, nq), BF),
            pltpu.VMEM((dp - 1, rows, nr), BF), pltpu.VMEM((dp - 1, rows, nr), BF),
            pltpu.VMEM((dp - 1, rows, nq), BF), pltpu.VMEM((dp - 1, rows, nq), BF),
            pltpu.VMEM((rows, nr), F32), pltpu.VMEM((rows, nq), F32),
        ]
        + scatter_scratch(seq, model)
        + [DMA((6,)), DMA((6,)), DMA((16,)), DMA((3, 8))]
        + GradReduce.scratch(dp) * 2,
        compiler_params=params(5),
        cost_estimate=cost(70),
        name="layer_back",
    )(dmix, e2, cf, hf, n1, w1, w0, vecs, xf, g, gp, n2, o, gr1)


def last_kernel(
    cfg, q_in, k_in, v_in, o_in, do_in, lse, srow, kcol, tab_in, e2_in, dh_in, xf_in, n1_in, w0, vecs, vf1, vd1, vd0,
    gr0, out1, outq, hf_in, y_in, so, ig, fq_o, fr_o, vec_o,
    q, k, v, o, do, tab, kt, dk, dv, dmix, dh, dx, xf, n1, e2, wqkv, gq, gotq, acrq, sbq, rbq, gr, got, sb, rb, fq, fr,
    vgf, va, vr, vout, part, mr, xr, sss, srs, lsem, vss, vrs, oss, ors, *rsems,
):
    col, heads, dp = cfg["col"], cfg["heads"], cfg["dp"]
    me = Mesh(dp, cfg["tensor"])
    sc = Scatter(me, part, mr, xr, sss, srs, 1 - me.y)
    half = sc.half
    seq = xf.shape[0]
    width = q.shape[1]
    own = [ds(sc.own(n), half) for n in range(2)]
    loads = load(
        [
            (k_in, k),
            (q_in, q),
            (v_in, v),
            (do_in, do),
            (o_in, o),
            (tab_in, tab),
            (w0.at[:, col["qkv"] : col["fc1"]], wqkv),
            (xf_in, xf),
            (e2_in, e2),
            (n1_in, n1),
        ]
        + [(dh_in.at[rr], dh.at[n]) for n, rr in enumerate(own)],
        lsem,
    )
    gr_load = pltpu.make_async_copy(gr0, gr, lsem.at[12])
    holds = (me.s == 0) & (me.y == 0)

    @pl.when(holds)
    def _():
        gr_load.start()

    greet([me.mate, me.beside, me.beside_mate, me.across, me.across_mate] + me.ring)
    redr = GradReduce(me, 0, gr0, gr, gr, got, sb, rb, fr, rsems[:6])
    redq = GradReduce(me, 0, gq, gq, gotq, acrq, sbq, rbq, fq, rsems[6:])
    vr_ = VectorReduce(me, va, vr, vss, vrs)
    redr.send()

    def at(dst, h):
        return dst.at[0, me.y, 0, pl.ds(h * half, half)]

    def full_out(src, dst, i):
        chunk = 2 * half
        mine, theirs = ds(me.t * chunk, chunk), ds(me.py * chunk, chunk)
        return [
            pltpu.make_async_copy(src.at[mine], dst.at[0, me.y, 0], lsem.at[13]),
            push(src.at[theirs], dst.at[0, me.y, 0], oss.at[i], ors.at[i], me.across),
        ]

    def owned_out(src, dst, core, i):
        here, far = src.at[me.y], src.at[1 - me.y]
        place = dst.at[0, me.y, 0, ds(me.s * half, half)]
        across = push(far, place, oss.at[i], ors.at[i + me.s], me.across_core(core))
        local = pltpu.make_async_copy(here, place, lsem.at[14])
        mate = push(here, place, oss.at[i + 2], ors.at[i + 2], me.mate)
        return across, local, mate

    def whole(n):
        return full_out(hf_in, so, 0) if n == 0 else full_out(dh_in, ig, 0)

    for n in range(2):

        @pl.when(me.s == n)
        def _(n=n):
            for c in whole(n):
                c.start()

    def start_here(src, dst, core, i):
        across, local, mate = owned_out(src, dst, core, i)

        @pl.when(me.s == core)
        def _():
            local.start()

        @pl.when(me.s != core)
        def _():
            mate.start()

    def wait_owned(src, dst, core, i):
        across, local, mate = owned_out(src, dst, core, i)
        across.wait_send()

        @pl.when(me.s == core)
        def _():
            local.wait()
            mate.wait_recv()
            for n in range(2):
                push(src.at[0], at(dst, n), oss.at[i], ors.at[i + n], me.across_core(core)).wait_recv()

        @pl.when(me.s != core)
        def _():
            mate.wait_send()

    owned_out(y_in, so, 1, 1)[0].start()
    start_here(y_in, so, 1, 1)
    old = [pltpu.make_async_copy(out1, fr, lsem.at[15]), pltpu.make_async_copy(outq, fq, lsem.at[16])]

    @pl.when(me.s == 1)
    def _():
        for c in old:
            c.start()

    vgf[...] = jnp.zeros_like(vgf)
    dk[...] = jnp.zeros_like(dk)
    dv[...] = jnp.zeros_like(dv)
    loads[0].wait()
    turn_blocks(k, kt)
    for c in loads[1:6]:
        c.wait()

    @pl.when(holds)
    def _():
        gr_load.wait()

    n_blocks = seq // QB

    def qloop(i, _):
        lo = jnp.maximum(i - DOC_MAX // QB, 0)
        attn_bwd_block(i, lo, i, heads, q, k, v, o, do, kt, lse, srow, kcol, tab, dk, dv, dmix)
        for at_block, steps in (
            (n_blocks // 2 - 1, range(0, 1)),
            (n_blocks // 2, range(1, dp // 2)),
            (n_blocks // 2 + 1, range(dp // 2, dp - 1)),
            (n_blocks - 2, range(dp - 1, dp)),
        ):

            @pl.when(i == at_block)
            def _(steps=steps):
                for d in steps:
                    redr.step(d)

        return 0

    lax.fori_loop(0, n_blocks, qloop, 0)

    def close(i, _):
        ii = ds(i * QB, QB)
        dmix[ii, width : 2 * width] = turn_lanes(dk[ii, :], tab[ii, :], -1).astype(BF)
        dmix[ii, 2 * width : 3 * width] = dv[ii, :].astype(BF)
        return 0

    lax.fori_loop(0, n_blocks, close, 0)
    for c in loads[6:]:
        c.wait()

    def early():
        va[0, 0:8, :] = vgf[...] + vd0[...]
        va[0, 8:16, :] = vf1[...] + vd1[...]
        vr_.send(0)
        nf = gq.shape[0]
        accs = [dk.at[0:nf], dk.at[nf : 2 * nf], dv.at[0:nf]]
        for acc in accs:
            acc[...] = jnp.zeros_like(acc)

        def body(i, _):
            rows = ds(i * half, half)
            n1t = n1[rows, :].T
            for p, acc in enumerate(accs):
                acc[...] += dot(n1t, dmix[rows, p * HW : (p + 1) * HW])
            return 0

        lax.fori_loop(0, 8, body, 0)
        for p, acc in enumerate(accs):
            gq[:, p * HW : (p + 1) * HW] = acc[...].astype(BF)
        vr_.add(0, va.at[1])
        vr_.send(1)
        redq.send()
        vr_.add(1, va.at[2])
        vr_.send(2)
        redq.step(0)

    sc.run(lambda r0, i: back_tail(r0, half, dmix, xf, e2, wqkv, vecs.at[0], part, vgf), early)
    for d in range(1, dp - 1):
        redq.step(d)

    def write(n, i, value):
        dx[sc.side(n), ds(i * SUB, SUB), :] = value

    def leave(n):
        if n == 0:
            owned_out(dx, ig, 0, 4)[0].start()
        else:
            start_here(dx, ig, 0, 4)

    grad_out(sc, lambda n, i: dh[sc.side(n), ds(i * SUB, SUB), :], xf, vecs.at[0], write, leave)
    redq.step(dp - 1)
    vr_.add(2, vout)
    vec_o[...] = jnp.where(me.s == 0, vout[0:8, :], vout[8:16, :])
    redr.collect()
    redq.collect()

    @pl.when(me.s == 1)
    def _():
        for c in old:
            c.wait()

    ends = [pltpu.make_async_copy(fr, fr_o, lsem.at[0]), pltpu.make_async_copy(fq, fq_o, lsem.at[1])]
    for c in ends:
        c.start()
    redr.finish()
    redq.finish()
    vr_.finish()
    sc.finish()
    for n in range(2):

        @pl.when(me.s == n)
        def _(n=n):
            for c in whole(n):
                c.wait()

    wait_owned(y_in, so, 1, 1)
    wait_owned(dx, ig, 0, 4)
    for c in ends:
        c.wait()


def layer_last(cfg, q, k, v, o, do, lse, sr, kc, tab, e2, dh, xf, n1, w0, vecs, vf1, vd1, vd0, gr0, out1, outq, hf, y):
    seq, model = xf.shape
    dp, tensor, ff = cfg["dp"], cfg["tensor"], cfg["ff"]
    rows, nr, nq = model // dp, 2 * ff + HW, 3 * HW
    nv = dp + tensor - 1
    wide, owned, heads = pltpu.VMEM((seq, model), BF), pltpu.VMEM((2, seq // 8, model), BF), pltpu.VMEM((seq, HW), BF)
    both = sds((1, 2, 1, seq // 4, model), BF)
    return pl.pallas_call(
        functools.partial(last_kernel, cfg),
        out_shape=(both, both, sds((rows, nq), F32), sds((rows, nr), F32), sds((8, model), F32)),
        in_specs=[ANY] * 5 + [VMEM] * 3 + [ANY] * 6 + [VMEM] * 4 + [ANY] * 5,
        out_specs=(ANY, ANY, ANY, ANY, VMEM),
        scratch_shapes=[
            heads, heads, heads, heads, heads, pltpu.VMEM(tab.shape, F32), pltpu.VMEM((HW, seq), BF),
            pltpu.VMEM((seq, HW), F32), pltpu.VMEM((seq, HW), F32), pltpu.VMEM((seq, nq), BF), owned, owned,
            wide, wide, wide, pltpu.VMEM((model, nq), BF),
            pltpu.VMEM((model, nq), BF), pltpu.VMEM((model, nq), BF), pltpu.VMEM((model, nq), BF),
            pltpu.VMEM((dp - 1, rows, nq), BF), pltpu.VMEM((dp - 1, rows, nq), BF),
            pltpu.VMEM((model, nr), BF), pltpu.VMEM((model, nr), BF),
            pltpu.VMEM((dp - 1, rows, nr), BF), pltpu.VMEM((dp - 1, rows, nr), BF),
            pltpu.VMEM((rows, nq), F32), pltpu.VMEM((rows, nr), F32),
            pltpu.VMEM((8, model), F32), pltpu.VMEM((3, 16, model), F32), pltpu.VMEM((nv, 16, model), F32),
            pltpu.VMEM((16, model), F32),
        ]
        + scatter_scratch(seq, model)
        + [DMA((17,)), DMA((nv,)), DMA((nv,)), DMA((7,)), DMA((7,))]
        + GradReduce.scratch(dp) * 2,
        compiler_params=params(6),
        cost_estimate=cost(80),
        name="layer_last",
    )(q, k, v, o, do, lse, sr, kc, tab, e2, dh, xf, n1, w0, vecs, vf1, vd1, vd0, gr0, out1, outq, hf, y)


def finish_kernel(
    cfg, so_in, ig_in, fq_in, fr_in, vec, so, ig, bg1, bb1, gqkv, bqkv, gout, bdy, bdy2, bg2, bb2, gfc1, bfc1, gfc2,
    a, b, fq, fr, lsem, osem,
):
    heads, ff, own, qw, fw = cfg["heads"], cfg["ff"], cfg["own"], cfg["qw"], cfg["fw"]
    me = Mesh(cfg["dp"], cfg["tensor"])
    loads = load([(fr_in, fr), (fq_in, fq), (so_in, a), (ig_in, b)], lsem)
    model = vec.shape[1]
    short = pltpu.roll(vec[...], (model - (me.z * me.tensor + me.t) * own) % model, 1)
    for row, ref in ((0, bg1), (1, bb1), (2, bdy), (2, bdy2), (3, bg2), (4, bb2)):
        ref[...] = short[row : row + 1, 0:own]
    for h in range(heads):
        parts = [vec[6:7, p * HW + h * HD : p * HW + (h + 1) * HD] for p in range(3)]
        one = jnp.concatenate(parts + [jnp.zeros((1, HW - 3 * HD), F32)], axis=1)
        one = jnp.broadcast_to(one, (8, HW))
        bqkv[h] = pltpu.roll(one, (HW - me.z * qw) % HW, 1)[0:1, 0:qw]
        wide = ff // heads
        one = jnp.broadcast_to(vec[7:8, h * wide : (h + 1) * wide], (8, wide))
        bfc1[h] = pltpu.roll(one, (wide - me.z * fw) % wide, 1)[0:1, 0:fw]
    loads[0].wait()
    gfc1[0] = fr[:, 0:ff]
    gfc2[...] = fr[:, ff : 2 * ff]
    gout[0] = fr[:, 2 * ff : 2 * ff + HW].T[0 : heads * HD, :]
    loads[2].wait()
    loads[3].wait()
    outs = [pltpu.make_async_copy(a, so, osem.at[0]), pltpu.make_async_copy(b, ig, osem.at[1])]
    for c in outs:
        c.start()
    loads[1].wait()
    pieces = [fq[:, p * HW + h * HD : p * HW + (h + 1) * HD] for h in range(heads) for p in range(3)]
    gqkv[0] = jnp.concatenate(pieces, axis=1)
    for c in outs:
        c.wait()


def finish(cfg, so, ig, fq, fr, vec):
    heads, ff, rows = cfg["heads"], cfg["ff"], fq.shape[0]
    line = sds((1, cfg["own"]), F32)
    return pl.pallas_call(
        functools.partial(finish_kernel, cfg),
        out_shape=(sds(so.shape, BF), sds(ig.shape, BF), line, line, sds((1, rows, heads * 3 * HD), F32),
                   sds((heads, 1, cfg["qw"]), F32), sds((1, heads * HD, rows), F32), line, line, line, line,
                   sds((1, rows, ff), F32), sds((heads, 1, cfg["fw"]), F32), sds((rows, ff), F32)),
        in_specs=[ANY] * 4 + [VMEM],
        out_specs=(ANY, ANY) + (VMEM,) * 12,
        scratch_shapes=[
            pltpu.VMEM(so.shape, BF), pltpu.VMEM(ig.shape, BF), pltpu.VMEM(fq.shape, F32), pltpu.VMEM(fr.shape, F32),
            DMA((4,)), DMA((2,)),
        ],
        compiler_params=pltpu.CompilerParams(vmem_limit_bytes=67043328),
        cost_estimate=cost(5),
        name="finish",
    )(so, ig, fq, fr, vec)


def by_part(w):
    rows = w.shape[0]
    heads = w.shape[1] // (3 * HD)
    w = w.reshape(rows, heads, 3, HD).transpose(0, 2, 1, 3).reshape(rows, 3, heads * HD)
    return jnp.pad(w, ((0, 0), (0, 0), (0, HW - heads * HD))).reshape(rows, 3 * HW)


def shards(
    dp, tensor, inputs, cotangent, segments, live_blocks, ln1_gain, ln1_bias, qkv_weight, qkv_bias,
    out_weight, out_bias, ln2_gain, ln2_bias, fc1_weight, fc1_bias, fc2_weight, fc2_bias,
):
    model = inputs.shape[-1]
    ff = fc1_weight.shape[2]
    heads = qkv_bias.shape[1]
    col = columns(model, ff)
    wout = jnp.pad(out_weight[0].T, ((0, 0), (0, HW - heads * HD)))
    w = jnp.concatenate([by_part(qkv_weight[0]), fc1_weight[0], fc2_weight[0].T, wout], axis=1)
    small = jnp.stack([ln1_gain[0], ln1_bias[0], out_bias[0], ln2_gain[0], ln2_bias[0], fc2_bias[0]])

    def lanes(a):
        return jnp.pad(a.astype(F32), ((0, 0), (0, 128 - a.shape[1])))

    sv = jnp.concatenate([lanes(small), lanes(qkv_bias[0]), lanes(fc1_bias[0])], axis=0)
    sv = jnp.pad(sv, ((0, -sv.shape[0] % 8), (0, 0)))
    fr = np.float32(10000.0) ** (-(np.arange(ROT // 2, dtype=np.float32) * np.float32(2.0 / ROT)))
    fr = jnp.asarray(np.broadcast_to(fr[:, None], (ROT // 2, 128)).astype(np.float32))
    cfg = {
        "col": col, "ff": ff, "heads": heads, "dp": dp, "tensor": tensor, "own": small.shape[1],
        "qw": qkv_bias.shape[2], "fw": fc1_bias.shape[2],
        "groups": [(0, col["fc1"]), (col["fc1"], col["fc2"]), (col["fc2"], col["end"])],
    }

    xf, n1a, n2a, ga, gpa, tab, w0, qa, ka, va, cf, vecs, sr, kc = layer_in(
        cfg, inputs, cotangent, segments, live_blocks, w, sv, fr
    )
    oa, lsea, hf, n1b, n2b, gb, gpb, w1, qb, kb, vb = layer_mid(cfg, qa, ka, va, sr, kc, ga, xf, w, w0, vecs, tab)
    ob, lseb = attn_fwd(heads, segments, live_blocks, qb, kb, vb, sr, kc)
    y, dob, e2b, grb, vdb = layer_turn(cfg, ob, gb, hf, cf, w1, vecs, n2b, gpb)
    dmb = attn_bwd(heads, segments, live_blocks, qb, kb, vb, ob, dob, lseb, sr, kc, tab)
    dhf, e2a, doa, vfb, vda, out1, outq, gra = layer_back(
        cfg, dmb, e2b, cf, hf, n1b, w1, w0, vecs, xf, ga, gpa, n2a, oa, grb
    )
    last_part = finish(
        cfg,
        *layer_last(
            cfg, qa, ka, va, oa, doa, lsea, sr, kc, tab, e2a, dhf, xf, n1a, w0, vecs, vfb, vdb, vda, gra, out1, outq, hf, y
        ),
    )
    so, ig, bg1, bb1, gqkv, bqkv, gout, bdy, bdy2, bg2, bb2, gfc1, bfc1, gfc2 = last_part
    bqkv, bfc1, gfc2 = bqkv.transpose(1, 0, 2), bfc1.transpose(1, 0, 2), gfc2.T[None]
    return (so, ig, bg1, bb1, gqkv, bqkv, gout, bdy, bg2, bb2, gfc1, bfc1, gfc2, bdy2)


def solution(mesh):
    both = ("dp", "tensor")
    in_specs = (
        P(None, "dp", "tensor", None),
        P(None, "dp", "tensor", None),
        P(None, "dp", None),
        P(None, "dp"),
        P("section", both),
        P("section", both),
        P("section", "dp", "tensor"),
        P("section", "tensor", "dp"),
        P("section", "tensor", "dp"),
        P("section", both),
        P("section", both),
        P("section", both),
        P("section", "dp", "tensor"),
        P("section", "tensor", "dp"),
        P("section", "tensor", "dp"),
        P("section", both),
    )
    out_specs = (
        P("section", None, "dp", "tensor", None),
        P("section", None, "dp", "tensor", None),
        P("section", both),
        P("section", both),
        P("section", "dp", "tensor"),
        P("section", "tensor", "dp"),
        P("section", "tensor", "dp"),
        P("section", both),
        P("section", both),
        P("section", both),
        P("section", "dp", "tensor"),
        P("section", "tensor", "dp"),
        P("section", "tensor", "dp"),
        P("section", both),
    )
    body = functools.partial(shards, mesh.shape["dp"], mesh.shape["tensor"])
    return jax.shard_map(body, mesh=mesh, in_specs=in_specs, out_specs=out_specs, check_vma=False)
```

time: 439 us -> 397 us (0.904)
  local copies, waits for them, and re-layouts: 30.1 us -> 4.44 us
  Pallas kernels: 364 us -> 387 us
  starting transfers between devices: 19.3 us -> 0 us
  other arithmetic: 20.9 us -> 2.33 us
    pallas_call x4 -> x5, Pallas kernels: 221 us -> 253 us  [the longest x1 108 us: layer_last(): pl.pallas_call(functools.partial(last_kernel, cfg), out_shape=(both, both...]
    pallas_call x2 -> x1, Pallas kernels: 61.6 us -> 36.1 us  [attn_bwd(): pl.pallas_call(functools.partial(attn_bwd_kernel, heads), out_shape=sds((...]
    pallas_call x1, Pallas kernels: 55.7 us -> 78.6 us  [layer_in(): pl.pallas_call(functools.partial(in_kernel, cfg), out_shape=(rows, rows,...]
    ppermute x12 -> x0, starting transfers between devices: 19.3 us -> none  [the longest x6 14.1 us: over_dp(): lax.ppermute(blocks[d - 1], ('section', 'dp'), pairs(d))]
    unnamed x93 -> x7, local copies, waits for them, and re-layouts: 13.7 us -> 3.45 us
    select_n x5 -> x0, other arithmetic: 7.35 us -> none  [the longest x1 2.25 us: shards(): gr = jnp.where(first, owna + sum((a.astype(F32) for a in got_r)), gr1)]
    squeeze x4 -> x0, local copies, waits for them, and re-layouts: 6.64 us -> none  [the longest x2 3.51 us: mine(): return lax.dynamic_index_in_dim(a, s, 0, keepdims=False)[0]]
    pallas_call x2 -> x1, Pallas kernels: 25.3 us -> 19.1 us  [attn_fwd(): pl.pallas_call(functools.partial(attn_fwd_kernel, heads), out_shape=(sds(...]
  transfers between devices with their start and end apart: 12 -> 0, of which waited for: 0 -> 0; matrix products, arithmetic and copies ran while one was open for 5% -> 0% of each run, Pallas kernels for 39% -> 0%
where the time goes in v3:
time: 397 us; the launch traced here: 395 us
  Pallas kernels  387 us (97%)
  local copies, waits for them, and re-layouts  4.44 us (1%)
    pallas_call x1, Pallas kernels, layer_last(): pl.pallas_call(functools.partial(last_kernel, cfg), out_shape=(both, both...  108 us
    pallas_call x1, Pallas kernels, layer_in(): pl.pallas_call(functools.partial(in_kernel, cfg), out_shape=(rows, rows,...  78.6 us
    pallas_call x1, Pallas kernels, layer_mid(): pl.pallas_call(functools.partial(mid_kernel, cfg), out_shape=(heads, sds(...  59.1 us
    pallas_call x1, Pallas kernels, layer_back(): pl.pallas_call(functools.partial(back_kernel, cfg), out_shape=(sds((seq,...  51 us
    pallas_call x1, Pallas kernels, attn_bwd(): pl.pallas_call(functools.partial(attn_bwd_kernel, heads), out_shape=sds((...  36.1 us
    pallas_call x1, Pallas kernels, layer_turn(): pl.pallas_call(functools.partial(turn_kernel, cfg), out_shape=(sds(owned,...  29 us
    pallas_call x1, Pallas kernels, attn_fwd(): pl.pallas_call(functools.partial(attn_fwd_kernel, heads), out_shape=(sds(...  19.1 us

profile of v3, /device:TPU:0, one launch (start us, length us, event | category | flops | bytes accessed | tf_op | source)
XLA Modules:
  0.0 394.6 jit_solution(5625849016736982977)
XLA Ops:
  0.6 0.0 copy-start
  0.7 0.0 copy-start.1
  0.7 1.4 copy.40.live
  2.0 0.8 stack.3
  2.8 0.7 fusion.7
  3.5 0.6 pad_convert_fusion.sv_ref
  4.1 1.0 copy.39
  5.1 1.1 copy.36
  6.3 0.2 copy.43
  6.4 0.0 copy-done
  6.5 0.0 copy-done.1
  6.5 1.0 fusion.1.w_ref
  7.5 78.6 %layer_in.1 = (bf16[2048,768]{1,0:T(8,128)(2,1)}, bf16[2048,768]{1,0:T(8,128)(2,1)}, bf16[2048,768]{1,0:T(8,128)(2,1)}, bf16[2048,768]{1,0:T(8,128)(2,1)}, bf16[...) custom-call(bf16[2,1,512,768]{3,2,1,0:T(8,128)(2,1)} %in_ref.1, ...), custom_call_target="tpu_custom_call" | custom-call | flops 35999997952 | tf_op jit(solution)/shard_map/layer_in/pallas_call | solution.py:1095
  86.1 59.1 %layer_mid.1 = (bf16[2048,256]{1,0:T(8,128)(2,1)}, f32[8,2048]{1,0:T(8,128)}, bf16[2048,768]{1,0:T(8,128)(2,1)}, bf16[2048,768]{1,0:T(8,128)(2,1)}, bf16[2048,76...) custom-call(bf16[2048,256]{1,0:T(8,128)(2,1)} %get-tuple-element.73., ...), custom_call_target="tpu_custom_call" | custom-call | flops 56000000000 | tf_op jit(solution)/shard_map/layer_mid/pallas_call | solution.py:1219
  145.2 19.1 %attn_fwd.1 = (bf16[2048,256]{1,0:T(8,128)(2,1)}, f32[8,2048]{1,0:T(8,128)}) custom-call(s32[2,1,2048]{2,1,0:T(1,128)} %seg.3, s32[2,1]{1,0:T(2,128)} %copy.40.live, bf16[2048,256]{1,0:T(8,128)(2,1)} %get-tuple-element.84.q_in, bf16[2048,256]{1,0:T(8,128)(2,1)} %get-tuple-element.85.k_in, bf16[2048,256]{1,0:T(8,128)(2,1)} %get-tuple-element.86.v_in, ...), custom_call_target="tpu_custom_call" | custom-call | flops 9600000000 | tf_op jit(solution)/shard_map/attn_fwd/pallas_call | solution.py:159
  164.4 29.0 %layer_turn.1 = (bf16[2,256,768]{2,1,0:T(8,128)(2,1)}, bf16[2048,256]{1,0:T(8,128)(2,1)}, bf16[2048,768]{1,0:T(8,128)(2,1)}, bf16[768,1792]{1,0:T(8,128)(2,1)}, f32[8,768]{1,0:T(8,128)}) custom-call(bf16[2048,256]{1,0:T(8,128)(2,1)} %get-tuple-element.87.o_in, bf16[2048,768]{1,0:T(8,128)(2,1)} %get-tuple-element.88.g_in, ...), custom_call_target="tpu_custom_call" | custom-call | flops 32000000000 | tf_op jit(solution)/shard_map/layer_turn/pallas_call | solution.py:1306
  193.4 36.1 %attn_bwd.1.dm_in = bf16[2048,768]{1,0:T(8,128)(2,1)} custom-call(s32[2,1,2048]{2,1,0:T(1,128)} %seg.3, s32[2,1]{1,0:T(2,128)} %copy.40.live, bf16[2048,256]{1,0:T(8,128)(2,1)} %get-tuple-element.84.q_in, bf16[2048,256]{1,0:T(8,128)(2,1)} %get-tuple-element.85.k_in, bf16[2048,256]{1,0:T(8,128)(2,1)} %get-tuple-element.86.v_in, ...), custom_call_target="tpu_custom_call" | custom-call | flops 20800000000 | tf_op jit(solution)/shard_map/attn_bwd/pallas_call | solution.py:270
  229.5 51.0 %layer_back.1 = (bf16[2048,768]{1,0:T(8,128)(2,1)}, bf16[2048,768]{1,0:T(8,128)(2,1)}, bf16[2048,256]{1,0:T(8,128)(2,1)}, f32[8,768]{1,0:T(8,128)}, f32[8,768]{1...) custom-call(bf16[2048,768]{1,0:T(8,128)(2,1)} %attn_bwd.1.dm_in, ...), custom_call_target="tpu_custom_call" | custom-call | flops 56000000000 | tf_op jit(solution)/shard_map/layer_back/pallas_call | solution.py:1451
  280.5 107.7 %layer_last.1 = (bf16[1,2,1,512,768]{4,3,2,1,0:T(8,128)(2,1)}, bf16[1,2,1,512,768]{4,3,2,1,0:T(8,128)(2,1)}, f32[192,768]{1,0:T(8,128)}, f32[192,1792]{1,0:T(8,128)}, f32[8,768]{1,0:T(8,128)}) custom-call(bf16[2048,256]{1,0:T(8,128)(2,1)} %get-tuple-element.73.q_in, bf16[2048,256]{1,0:T(8,128)(2,1)} %get-tuple-element.74.k_in, ...), custom_call_target="tpu_custom_call" | custom-call | flops 64000000000 | tf_op jit(solution)/shard_map/layer_last/pallas_call | solution.py:1711
  388.2 6.2 %finish.1 = (bf16[1,2,1,512,768]{4,3,2,1,0:T(8,128)(2,1)}, bf16[1,2,1,512,768]{4,3,2,1,0:T(8,128)(2,1)}, f32[1,48]{1,0:T(1,128)}, f32[1,48]{1,0:T(1,128)}, f32[1...) custom-call(bf16[1,2,1,512,768]{4,3,2,1,0:T(8,128)(2,1)} %get-tuple-, ...), custom_call_target="tpu_custom_call" | custom-call | flops 4000000000 | tf_op jit(solution)/shard_map/finish/pallas_call | solution.py:1775
  (2 shorter events, 0.1 us)
Async XLA Ops:
  0.6 5.8 %copy-start = (bf16[1,768,192]{1,2,0:T(8,128)(2,1)S(1)}, bf16[1,768,192]{1,2,0:T(8,128)(2,1)}, u32[]{:S(2)}) copy-start(bf16[1,768,192]{1,2,0:T(8,128)(2,1)} %param.31) | copy-start | bytes 884740
  0.7 5.8 %copy-start.1 = (bf16[1,192,768]{2,1,0:T(8,128)(2,1)S(1)}, bf16[1,192,768]{2,1,0:T(8,128)(2,1)}, u32[]{:S(2)}) copy-start(bf16[1,192,768]{2,1,0:T(8,128)(2,1)} %param.29) | copy-start | bytes 884740

commit v4 on v3

--- a/solution.py
+++ b/solution.py
@@ -71,7 +71,7 @@
     def body(j, count):
         return count + jnp.where((j < i) & (seg[s, 0, (j + 1) * QB - 1] == doc), 1, 0)
 
-    hi = jnp.minimum(i, (live[s, 0] * LIVE + QB - 1) // QB)
+    hi = jnp.minimum(i, (live[0, s] * LIVE + QB - 1) // QB)
     return jnp.minimum(i - lax.fori_loop(0, n, body, 0), hi), hi
 
 
@@ -574,6 +574,7 @@
         self.sb, self.rb, self.own = sb, rb, own
         self.hss, self.hrs, self.yss, self.yrs, self.pss, self.prs = sems
         self.rows = own.shape[0]
+        self.some = 96 if self.rows % 96 == 0 else 48
         self.sums = me.s == layer
         self.holds = me.y == layer
 
@@ -620,18 +621,19 @@
 
             self.over(d).wait_recv()
             last = d == me.dp - 1
+            step = self.some
 
             def add(ref):
                 def body(i, _):
-                    rr = ds(self.zz(d) * self.rows + i * 16, 16)
+                    rr = ds(self.zz(d) * self.rows + i * step, step)
                     value = ref[rr, :].astype(F32) + self.across[rr, :].astype(F32)
                     if last:
-                        self.own[ds(i * 16, 16), :] = value
+                        self.own[ds(i * step, step), :] = value
                     else:
-                        self.sb[d, ds(i * 16, 16), :] = value.astype(BF)
+                        self.sb[d, ds(i * step, step), :] = value.astype(BF)
                     return 0
 
-                lax.fori_loop(0, self.rows // 16, body, 0)
+                lax.fori_loop(0, self.rows // step, body, 0)
 
             if self.mine is self.got:
                 add(self.mine)
@@ -657,11 +659,11 @@
                 self.out(d).wait_recv()
 
                 def add(i, _, d=d):
-                    rr = ds(i * 16, 16)
+                    rr = ds(i * self.some, self.some)
                     self.own[rr, :] += self.rb[d, rr, :].astype(F32)
                     return 0
 
-                lax.fori_loop(0, self.rows // 16, add, 0)
+                lax.fori_loop(0, self.rows // self.some, add, 0)
             for d in range(me.dp - 1):
                 self.out(d).wait_send()
 
@@ -1005,7 +1007,7 @@
     vg.send(0)
     wg.send_ring()
     first.wait()
-    document_tables(seg_ref[me.y], live[me.y, 0], fr_ref, tab, srow, kcol)
+    document_tables(seg_ref[me.y], live[0, me.y], fr_ref, tab, srow, kcol)
     vg.wait(0)
     vg.send(1)
     ga.start(0)
@@ -1800,6 +1802,7 @@
     dp, tensor, inputs, cotangent, segments, live_blocks, ln1_gain, ln1_bias, qkv_weight, qkv_bias,
     out_weight, out_bias, ln2_gain, ln2_bias, fc1_weight, fc1_bias, fc2_weight, fc2_bias,
 ):
+    live_blocks = live_blocks.T
     model = inputs.shape[-1]
     ff = fc1_weight.shape[2]
     heads = qkv_bias.shape[1]

time: 397 us -> 395 us (level)
  no operation moved by 1% of the time
where the time goes in v4:
time: 395 us; the launch traced here: 396 us
  Pallas kernels  390 us (99%)
    pallas_call x1, Pallas kernels, layer_last(): pl.pallas_call(functools.partial(last_kernel, cfg), out_shape=(both, both...  107 us
    pallas_call x1, Pallas kernels, layer_in(): pl.pallas_call(functools.partial(in_kernel, cfg), out_shape=(rows, rows,...  78.6 us
    pallas_call x1, Pallas kernels, layer_mid(): pl.pallas_call(functools.partial(mid_kernel, cfg), out_shape=(heads, sds(...  59.1 us
    pallas_call x1, Pallas kernels, layer_back(): pl.pallas_call(functools.partial(back_kernel, cfg), out_shape=(sds((seq,...  51.3 us
    pallas_call x1, Pallas kernels, attn_bwd(): pl.pallas_call(functools.partial(attn_bwd_kernel, heads), out_shape=sds((...  38.4 us
    pallas_call x1, Pallas kernels, layer_turn(): pl.pallas_call(functools.partial(turn_kernel, cfg), out_shape=(sds(owned,...  29 us
    pallas_call x1, Pallas kernels, attn_fwd(): pl.pallas_call(functools.partial(attn_fwd_kernel, heads), out_shape=(sds(...  20.3 us

profile of v4, /device:TPU:0, one launch (start us, length us, event | category | flops | bytes accessed | tf_op | source)
XLA Modules:
  0.0 396.2 jit_solution(11039871816079574088)
XLA Ops:
  0.6 0.0 copy-start
  0.7 0.0 copy-start.1
  0.7 0.8 stack.3
  1.5 0.7 fusion.7
  2.2 0.6 pad_convert_fusion.sv_ref
  2.8 1.0 copy.36
  3.8 1.1 copy.33
  5.0 0.2 copy.37
  5.1 0.0 copy-done
  5.2 0.0 copy-done.1
  5.2 1.0 fusion.1.w_ref
  6.2 78.6 %layer_in.1 = (bf16[2048,768]{1,0:T(8,128)(2,1)}, bf16[2048,768]{1,0:T(8,128)(2,1)}, bf16[2048,768]{1,0:T(8,128)(2,1)}, bf16[2048,768]{1,0:T(8,128)(2,1)}, bf16[...) custom-call(bf16[2,1,512,768]{3,2,1,0:T(8,128)(2,1)} %in_ref.1, ...), custom_call_target="tpu_custom_call" | custom-call | flops 35999997952 | tf_op jit(solution)/shard_map/layer_in/pallas_call | solution.py:1097
  84.8 59.1 %layer_mid.1 = (bf16[2048,256]{1,0:T(8,128)(2,1)}, f32[8,2048]{1,0:T(8,128)}, bf16[2048,768]{1,0:T(8,128)(2,1)}, bf16[2048,768]{1,0:T(8,128)(2,1)}, bf16[2048,76...) custom-call(bf16[2048,256]{1,0:T(8,128)(2,1)} %get-tuple-element.73., ...), custom_call_target="tpu_custom_call" | custom-call | flops 56000000000 | tf_op jit(solution)/shard_map/layer_mid/pallas_call | solution.py:1221
  143.9 20.3 %attn_fwd.1 = (bf16[2048,256]{1,0:T(8,128)(2,1)}, f32[8,2048]{1,0:T(8,128)}) custom-call(s32[2,1,2048]{2,1,0:T(1,128)} %seg.3, s32[1,2]{1,0:T(1,128)} %bitcast.29, bf16[2048,256]{1,0:T(8,128)(2,1)} %get-tuple-element.84.q_in, bf16[2048,256]{1,0:T(8,128)(2,1)} %get-tuple-element.85.k_in, bf16[2048,256]{1,0:T(8,128)(2,1)} %get-tuple-element.86.v_in, ...), custom_call_target="tpu_custom_call" | custom-call | flops 9600000000 | tf_op jit(solution)/shard_map/attn_fwd/pallas_call | solution.py:159
  164.2 29.0 %layer_turn.1 = (bf16[2,256,768]{2,1,0:T(8,128)(2,1)}, bf16[2048,256]{1,0:T(8,128)(2,1)}, bf16[2048,768]{1,0:T(8,128)(2,1)}, bf16[768,1792]{1,0:T(8,128)(2,1)}, f32[8,768]{1,0:T(8,128)}) custom-call(bf16[2048,256]{1,0:T(8,128)(2,1)} %get-tuple-element.87.o_in, bf16[2048,768]{1,0:T(8,128)(2,1)} %get-tuple-element.88.g_in, ...), custom_call_target="tpu_custom_call" | custom-call | flops 32000000000 | tf_op jit(solution)/shard_map/layer_turn/pallas_call | solution.py:1308
  193.2 38.4 %attn_bwd.1.dm_in = bf16[2048,768]{1,0:T(8,128)(2,1)} custom-call(s32[2,1,2048]{2,1,0:T(1,128)} %seg.3, s32[1,2]{1,0:T(1,128)} %bitcast.30, bf16[2048,256]{1,0:T(8,128)(2,1)} %get-tuple-element.84.q_in, bf16[2048,256]{1,0:T(8,128)(2,1)} %get-tuple-element.85.k_in, bf16[2048,256]{1,0:T(8,128)(2,1)} %get-tuple-element.86.v_in, ...), custom_call_target="tpu_custom_call" | custom-call | flops 20800000000 | tf_op jit(solution)/shard_map/attn_bwd/pallas_call | solution.py:270
  231.6 51.3 %layer_back.1 = (bf16[2048,768]{1,0:T(8,128)(2,1)}, bf16[2048,768]{1,0:T(8,128)(2,1)}, bf16[2048,256]{1,0:T(8,128)(2,1)}, f32[8,768]{1,0:T(8,128)}, f32[8,768]{1...) custom-call(bf16[2048,768]{1,0:T(8,128)(2,1)} %attn_bwd.1.dm_in, ...), custom_call_target="tpu_custom_call" | custom-call | flops 56000000000 | tf_op jit(solution)/shard_map/layer_back/pallas_call | solution.py:1453
  282.9 106.9 %layer_last.1 = (bf16[1,2,1,512,768]{4,3,2,1,0:T(8,128)(2,1)}, bf16[1,2,1,512,768]{4,3,2,1,0:T(8,128)(2,1)}, f32[192,768]{1,0:T(8,128)}, f32[192,1792]{1,0:T(8,128)}, f32[8,768]{1,0:T(8,128)}) custom-call(bf16[2048,256]{1,0:T(8,128)(2,1)} %get-tuple-element.73.q_in, bf16[2048,256]{1,0:T(8,128)(2,1)} %get-tuple-element.74.k_in, ...), custom_call_target="tpu_custom_call" | custom-call | flops 64000000000 | tf_op jit(solution)/shard_map/layer_last/pallas_call | solution.py:1713
  389.8 6.2 %finish.1 = (bf16[1,2,1,512,768]{4,3,2,1,0:T(8,128)(2,1)}, bf16[1,2,1,512,768]{4,3,2,1,0:T(8,128)(2,1)}, f32[1,48]{1,0:T(1,128)}, f32[1,48]{1,0:T(1,128)}, f32[1...) custom-call(bf16[1,2,1,512,768]{4,3,2,1,0:T(8,128)(2,1)} %get-tuple-, ...), custom_call_target="tpu_custom_call" | custom-call | flops 4000000000 | tf_op jit(solution)/shard_map/finish/pallas_call | solution.py:1777
  (2 shorter events, 0.1 us)
Async XLA Ops:
  0.6 4.5 %copy-start = (bf16[1,768,192]{1,2,0:T(8,128)(2,1)S(1)}, bf16[1,768,192]{1,2,0:T(8,128)(2,1)}, u32[]{:S(2)}) copy-start(bf16[1,768,192]{1,2,0:T(8,128)(2,1)} %param.31) | copy-start | bytes 884740
  0.7 4.5 %copy-start.1 = (bf16[1,192,768]{2,1,0:T(8,128)(2,1)S(1)}, bf16[1,192,768]{2,1,0:T(8,128)(2,1)}, u32[]{:S(2)}) copy-start(bf16[1,192,768]{2,1,0:T(8,128)(2,1)} %param.29) | copy-start | bytes 884740

commit v5 on v4

--- a/solution.py
+++ b/solution.py
@@ -959,6 +959,49 @@
     return pl.CostEstimate(flops=int(us * 8e8), bytes_accessed=0, transcendentals=0)
 
 
+class OwnedOut:
+    def __init__(self, me, src, dst, core, ss, rs, local):
+        self.me, self.src, self.dst, self.core, self.ss, self.rs, self.local = me, src, dst, core, ss, rs, local
+
+    def place(self):
+        return self.dst.at[self.me.y, self.me.s]
+
+    def far(self):
+        me = self.me
+        return push(self.src.at[1 - me.y], self.place(), self.ss.at[0], self.rs.at[me.s], me.across_core(self.core))
+
+    def mate(self):
+        return push(self.src.at[self.me.y], self.place(), self.ss.at[1], self.rs.at[2], self.me.mate)
+
+    def here(self):
+        return pltpu.make_async_copy(self.src.at[self.me.y], self.place(), self.local)
+
+    def start_here(self):
+        @pl.when(self.me.s == self.core)
+        def _():
+            self.here().start()
+
+        @pl.when(self.me.s != self.core)
+        def _():
+            self.mate().start()
+
+    def wait(self):
+        me = self.me
+        self.far().wait_send()
+
+        @pl.when(me.s == self.core)
+        def _():
+            self.here().wait()
+            self.mate().wait_recv()
+            for n in range(2):
+                place = self.dst.at[1 - me.y, n]
+                push(self.src.at[0], place, self.ss.at[0], self.rs.at[n], me.across_core(self.core)).wait_recv()
+
+        @pl.when(me.s != self.core)
+        def _():
+            self.mate().wait_send()
+
+
 class Stores:
     def __init__(self, pairs, half, sem):
         self.pairs, self.half, self.sem = pairs, half, sem
@@ -997,10 +1040,7 @@
     up = pltpu.make_async_copy(cot_ref.at[me.y, 0, part], cot, lsem.at[4])
     up.start()
     greet([me.mate, me.across_mate] + me.ring + me.group)
-    over = [
-        push(ref.at[1 - me.y, 0, part], full.at[ds(ga.own(me.y), half)], yss.at[n], yrs.at[n], me.across)
-        for n, (ref, full) in enumerate(((in_ref, hf), (cot_ref, cf_o)))
-    ]
+    over = push(in_ref.at[1 - me.y, 0, part], hf.at[ds(ga.own(me.y), half)], yss.at[0], yrs.at[0], me.across)
     wg = WeightGather(me, 0, w_ref, wfull, gat, cfg["groups"], wsems)
     vg = VectorGather(me, sv_ref, vb, vss, vrs, lsem.at[1])
     st = Stores([(hf, hf_o), (n1, n1_o), (n2, n2_o), (g, g_o), (gp, gp_o), (q, q_o), (k, k_o), (v, v_o)], half, ssem)
@@ -1011,7 +1051,7 @@
     vg.wait(0)
     vg.send(1)
     ga.start(0)
-    over[0].start()
+    over.start()
     wg.send_own(0)
     tab_out = pltpu.make_async_copy(tab, tab_o, lsem.at[2])
     tab_out.start()
@@ -1030,18 +1070,18 @@
 
         @pl.when(i == 0)
         def _():
-            over[0].wait_recv()
+            over.wait_recv()
             ga.start(1)
 
         @pl.when(i == 1)
         def _():
             wg.forward(0)
             wg.send_own(1)
-            wg.send_own(2)
 
     ga.run(norm)
     cot_out.wait()
-    gc.start(0)
+    gc.plan(0).start()
+    gc.plan(2).start()
     wg.ready(0)
 
     def qkv(i, _):
@@ -1052,37 +1092,37 @@
 
     lax.fori_loop(0, 8, qkv, 0)
     wg.forward(1)
-    over[1].start()
+    wg.send_own(2)
+    wg.send_own(3)
     wg.ready(1)
+    wg.forward(2)
 
     def fc1(i, _):
         r0 = ga.order(i)
         project_fc1(r0, half, wfull.at[:, col["fc1"] : col["fc2"]], vec, n2, g, gp)
         st.start((3, 4), r0, i)
 
-        @pl.when(i == 6)
-        def _():
-            wg.forward(2)
+        @pl.when(i == 5)
+        def _():
+            wg.forward(3)
 
         return 0
 
     lax.fori_loop(0, 8, fc1, 0)
     gc.step(2)
     gc.step(4)
-    over[1].wait_recv()
-    gc.start(1)
+    gc.step(5)
     st.finish()
     tab_out.wait()
     wg.ready(2)
+    wg.ready(3)
     w_out = pltpu.make_async_copy(wfull, w_o, lsem.at[3])
     w_out.start()
-    for n in (3, 5, 6, 7):
-        gc.step(n)
     wg.finish()
     vg.finish()
-    gc.finish()
-    for c in over:
-        c.wait_send()
+    for n in (0, 2, 4):
+        gc.plan(n).wait_send()
+    over.wait_send()
     w_out.wait()
 
 
@@ -1105,10 +1145,10 @@
             wide, wide, wide, wide_h, wide_h, pltpu.VMEM((seq, 256), F32), wide_q, wide_q, wide_q,
             weights, weights, pltpu.VMEM((2, tensor, dp) + sv.shape, F32),
             pltpu.VMEM((seq // 8, model), BF),
-            DMA((6,)), DMA((6,)), DMA((6,)), DMA((6,)), DMA((2,)), DMA((2,)), DMA((6,)), DMA((8, 8)),
+            DMA((6,)), DMA((6,)), DMA((6,)), DMA((6,)), DMA((1,)), DMA((1,)), DMA((6,)), DMA((8, 8)),
             DMA((nv,)), DMA((nv,)),
         ]
-        + WeightGather.scratch(dp, 3),
+        + WeightGather.scratch(dp, 4),
         compiler_params=params(2),
         cost_estimate=cost(45),
         name="layer_in",
@@ -1142,7 +1182,7 @@
     greet([me.mate, me.beside, me.across, me.across_mate] + me.ring)
     wg = WeightGather(me, 1, w_ref, wfull, gat, cfg["groups"], wsems)
     wg.send_ring()
-    for n in range(3):
+    for n in range(4):
         wg.send_own(n)
     loads[0].wait()
     turn_blocks(v, vt)
@@ -1197,6 +1237,10 @@
         def _():
             wg.forward(2)
 
+        @pl.when(i == 7)
+        def _():
+            wg.forward(3)
+
     ga.run(work)
 
     def late(i, _):
@@ -1206,6 +1250,7 @@
     lax.fori_loop(4, 8, late, 0)
     st.finish()
     wg.ready(2)
+    wg.ready(3)
     w_out = pltpu.make_async_copy(wfull, w_o, lsem.at[0])
     w_out.start()
     sc.finish()
@@ -1232,7 +1277,7 @@
         ]
         + scatter_scratch(seq, model)
         + [DMA((6,)), DMA((6,)), DMA((9,)), DMA((8, 8)), DMA((1, 8))]
-        + WeightGather.scratch(cfg["dp"], 3),
+        + WeightGather.scratch(cfg["dp"], 4),
         compiler_params=params(3),
         cost_estimate=cost(70),
         name="layer_mid",
@@ -1240,14 +1285,16 @@
 
 
 def turn_kernel(
-    cfg, o_in, g_in, hf_in, cf, w1, vecs, n2_in, gp_in, y_o, do_o, e2_o, gr_o, vg,
+    cfg, o_in, g_in, hf_in, cf, cot_ref, w1, vecs, n2_in, gp_in, y_o, do_o, e2_o, gr_o, hx, cy, vg,
     o, g, hf, dyf, n2, gp, e2, do, y, gr, wout, wfc2, wfc1, da, acc,
-    part, mr, xr, sss, srs, lsem, ssem,
+    part, mr, xr, sss, srs, gss, grs, yss, yrs, lsem, ssem,
 ):
     col = cfg["col"]
     me = Mesh(cfg["dp"], cfg["tensor"])
     sc = Scatter(me, part, mr, xr, sss, srs)
     half = sc.half
+    gt = Gather(me, dyf, gss, grs, me.y)
+    near = ds(4 * me.y * half, 4 * half)
     loads = load(
         [
             (w1.at[:, col["out"] : col["end"]], wout),
@@ -1255,14 +1302,25 @@
             (o_in, o),
             (g_in, g),
             (w1.at[:, col["fc1"] : col["fc2"]], wfc1),
-            (cf, dyf),
+            (cf.at[near], dyf.at[near]),
             (gp_in, gp),
             (hf_in, hf),
             (n2_in, n2),
         ],
         lsem,
     )
-    greet([me.mate, me.beside])
+    greet([me.mate, me.beside, me.across])
+    over = push(
+        cot_ref.at[1 - me.y, 0, ds(me.s * half, half)], dyf.at[ds(gt.own(me.y), half)], yss.at[0], yrs.at[0], me.across
+    )
+    over.start()
+    cy_out = pltpu.make_async_copy(dyf.at[ds(gt.own(1 - me.y), half)], cy, lsem.at[2])
+    h_over = push(hf_in.at[ds(me.py * 2 * half, 2 * half)], hx, yss.at[1], yrs.at[1], me.across)
+
+    @pl.when(me.s == 0)
+    def _():
+        h_over.start()
+
     for c in loads[:4]:
         c.wait()
     vec = vecs.at[1]
@@ -1273,9 +1331,20 @@
         acc[...] = jnp.zeros_like(acc)
         for c in loads[4:]:
             c.wait()
+        over.wait_recv()
+        gt.start(1)
+        cy_out.start()
 
         def head(i, _):
-            r0 = i * half
+            for n, step in ((5, 3), (6, 6), (7, 7)):
+
+                @pl.when(i == n)
+                def _(step=step):
+                    gt.step(step)
+
+            far_b = jnp.where(i < 6, me.x, 1 - me.x)
+            far_h = jnp.where(i % 2 == 0, me.s, 1 - me.s)
+            r0 = jnp.where(i < 4, (4 * me.y + i) * half, gt.start_of(1 - me.y, far_b, far_h))
             back_head(r0, half, dyf, hf, g, gp, n2, o, wfc1, wfc2, wout, vec, do, e2, da, acc, vg)
             st.start((0, 1), r0, i)
             return 0
@@ -1296,11 +1365,20 @@
     y_out.start()
     sc.finish()
     st.finish()
+    cy_out.wait()
+    over.wait_send()
+    for n in (1, 3, 5):
+        gt.plan(n).wait_send()
+
+    @pl.when(me.s == 0)
+    def _():
+        h_over.wait()
+
     gr_out.wait()
     y_out.wait()
 
 
-def layer_turn(cfg, o, g, hf, cf, w1, vecs, n2, gp):
+def layer_turn(cfg, o, g, hf, cf, cotangent, w1, vecs, n2, gp):
     seq, model = hf.shape
     ff = cfg["ff"]
     wide, hidden, heads = pltpu.VMEM((seq, model), BF), pltpu.VMEM((seq, ff), BF), pltpu.VMEM((seq, HW), BF)
@@ -1312,10 +1390,12 @@
             sds((seq, HW), BF),
             sds((seq, model), BF),
             sds((model, 2 * ff + HW), BF),
+            sds((seq // 4, model), BF),
+            sds((seq // 8, model), BF),
             sds((8, model), F32),
         ),
-        in_specs=[ANY] * 5 + [VMEM, ANY, ANY],
-        out_specs=(ANY,) * 4 + (VMEM,),
+        in_specs=[ANY] * 6 + [VMEM, ANY, ANY],
+        out_specs=(ANY,) * 6 + (VMEM,),
         scratch_shapes=[
             heads, hidden, wide, wide, wide, hidden, wide, heads, pltpu.VMEM(owned, BF),
             pltpu.VMEM((model, 2 * ff + HW), BF),
@@ -1323,25 +1403,24 @@
             pltpu.VMEM((seq // 8, ff), BF), pltpu.VMEM((model, 2 * ff + HW), F32),
         ]
         + scatter_scratch(seq, model)
-        + [DMA((9,)), DMA((2, 8))],
+        + [DMA((6,)), DMA((6,)), DMA((2,)), DMA((2,)), DMA((9,)), DMA((2, 8))],
         compiler_params=params(4),
         cost_estimate=cost(40),
         name="layer_turn",
-    )(o, g, hf, cf, w1, vecs, n2, gp)
+    )(o, g, hf, cf, cotangent, w1, vecs, n2, gp)
 
 
 def back_kernel(
-    cfg, dm_in, e2_in, cf, hf_in, n1_in, w1, w0, vecs, xf_in, g_in, gp_in, n2_in, o_in, gr1,
-    dh_o, e2_o, do_o, vgf, vgd, out1_o, outq_o, gr_o,
+    cfg, dm_in, e2_in, cf, cy, hf_in, n1_in, w1, w0, vecs, xf_in, g_in, gp_in, n2_in, o_in, gr1, y_in,
+    dh_o, e2_o, do_o, vgf, vgd, out1_o, outq_o, gr_o, yx,
     dmix, o, do, a, b, e2, g, gp, wqkv, wout, wfc2, wfc1, dhf, da, acc, gq, gr, got, gotq, acrq,
-    sb, rb, sbq, rbq, out1, outq, part, mr, xr, sss, srs, gss, grs, lsem, ssem, *rsems,
+    sb, rb, sbq, rbq, out1, outq, part, mr, xr, sss, srs, gss, grs, lsem, ssem, oss, ors, osem, *rsems,
 ):
     col, dp = cfg["col"], cfg["dp"]
     me = Mesh(dp, cfg["tensor"])
     ga = Gather(me, dhf, gss, grs)
     sc = Scatter(me, part, mr, xr, sss, srs)
     half = sc.half
-    own = [ds(sc.own(n), half) for n in range(2)]
     loads = load(
         [
             (w1.at[:, col["qkv"] : col["fc1"]], wqkv),
@@ -1356,7 +1435,7 @@
             (gp_in, gp),
             (o_in, o),
         ]
-        + [(cf.at[rr], dhf.at[rr]) for rr in own],
+        + [(cf.at[ds(sc.own(me.y), half)], dhf.at[ds(sc.own(me.y), half)]), (cy, dhf.at[ds(sc.own(1 - me.y), half)])],
         lsem,
     )
     gr_load = pltpu.make_async_copy(gr1, gr, lsem.at[13])
@@ -1370,6 +1449,7 @@
     red1 = GradReduce(me, 1, gr1, gr, gr, got, sb, rb, out1, rsems[:6])
     redq = GradReduce(me, 1, gq, gq, gotq, acrq, sbq, rbq, outq, rsems[6:])
     st = Stores([(e2, e2_o), (do, do_o), (dhf, dh_o)], half, ssem)
+    ys = OwnedOut(me, y_in, yx, 1, oss, ors, osem.at[0])
     red1.send()
     vgf[...] = jnp.zeros_like(vgf)
     vgd[...] = jnp.zeros_like(vgd)
@@ -1382,6 +1462,8 @@
         qkv_grad(b, dmix, small, half)
         store_low(small, gq)
         redq.send()
+        ys.far().start()
+        ys.start_here()
 
         @pl.when(holds)
         def _():
@@ -1441,11 +1523,12 @@
     sc.finish()
     st.finish()
     gr_out.wait()
+    ys.wait()
     for c in outs:
         c.wait()
 
 
-def layer_back(cfg, dmix, e2, cf, hf, n1, w1, w0, vecs, xf, g, gp, n2, o, gr1):
+def layer_back(cfg, dmix, e2, cf, cy, hf, n1, w1, w0, vecs, xf, g, gp, n2, o, gr1, y):
     seq, model = hf.shape
     ff, dp = cfg["ff"], cfg["dp"]
     rows, nr, nq = model // dp, 2 * ff + HW, 3 * HW
@@ -1461,9 +1544,10 @@
             sds((rows, nr), F32),
             sds((rows, nq), F32),
             sds((model, nr), BF),
+            sds((2,) + y.shape, BF),
         ),
-        in_specs=[ANY] * 7 + [VMEM] + [ANY] * 6,
-        out_specs=(ANY, ANY, ANY, VMEM, VMEM, ANY, ANY, ANY),
+        in_specs=[ANY] * 8 + [VMEM] + [ANY] * 7,
+        out_specs=(ANY, ANY, ANY, VMEM, VMEM, ANY, ANY, ANY, ANY),
         scratch_shapes=[
             pltpu.VMEM((seq, nq), BF), heads, heads, wide, wide, wide, hidden, hidden,
             pltpu.VMEM((model, nq), BF), pltpu.VMEM((model, HW), BF), pltpu.VMEM((model, ff), BF),
@@ -1475,17 +1559,17 @@
             pltpu.VMEM((rows, nr), F32), pltpu.VMEM((rows, nq), F32),
         ]
         + scatter_scratch(seq, model)
-        + [DMA((6,)), DMA((6,)), DMA((16,)), DMA((3, 8))]
+        + [DMA((6,)), DMA((6,)), DMA((16,)), DMA((3, 8)), DMA((2,)), DMA((3,)), DMA((1,))]
         + GradReduce.scratch(dp) * 2,
         compiler_params=params(5),
         cost_estimate=cost(70),
         name="layer_back",
-    )(dmix, e2, cf, hf, n1, w1, w0, vecs, xf, g, gp, n2, o, gr1)
+    )(dmix, e2, cf, cy, hf, n1, w1, w0, vecs, xf, g, gp, n2, o, gr1, y)
 
 
 def last_kernel(
     cfg, q_in, k_in, v_in, o_in, do_in, lse, srow, kcol, tab_in, e2_in, dh_in, xf_in, n1_in, w0, vecs, vf1, vd1, vd0,
-    gr0, out1, outq, hf_in, y_in, so, ig, fq_o, fr_o, vec_o,
+    gr0, out1, outq, dhx, dxx, fq_o, fr_o, vec_o,
     q, k, v, o, do, tab, kt, dk, dv, dmix, dh, dx, xf, n1, e2, wqkv, gq, gotq, acrq, sbq, rbq, gr, got, sb, rb, fq, fr,
     vgf, va, vr, vout, part, mr, xr, sss, srs, lsem, vss, vrs, oss, ors, *rsems,
 ):
@@ -1525,63 +1609,13 @@
     vr_ = VectorReduce(me, va, vr, vss, vrs)
     redr.send()
 
-    def at(dst, h):
-        return dst.at[0, me.y, 0, pl.ds(h * half, half)]
-
-    def full_out(src, dst, i):
-        chunk = 2 * half
-        mine, theirs = ds(me.t * chunk, chunk), ds(me.py * chunk, chunk)
-        return [
-            pltpu.make_async_copy(src.at[mine], dst.at[0, me.y, 0], lsem.at[13]),
-            push(src.at[theirs], dst.at[0, me.y, 0], oss.at[i], ors.at[i], me.across),
-        ]
-
-    def owned_out(src, dst, core, i):
-        here, far = src.at[me.y], src.at[1 - me.y]
-        place = dst.at[0, me.y, 0, ds(me.s * half, half)]
-        across = push(far, place, oss.at[i], ors.at[i + me.s], me.across_core(core))
-        local = pltpu.make_async_copy(here, place, lsem.at[14])
-        mate = push(here, place, oss.at[i + 2], ors.at[i + 2], me.mate)
-        return across, local, mate
-
-    def whole(n):
-        return full_out(hf_in, so, 0) if n == 0 else full_out(dh_in, ig, 0)
-
-    for n in range(2):
-
-        @pl.when(me.s == n)
-        def _(n=n):
-            for c in whole(n):
-                c.start()
-
-    def start_here(src, dst, core, i):
-        across, local, mate = owned_out(src, dst, core, i)
-
-        @pl.when(me.s == core)
-        def _():
-            local.start()
-
-        @pl.when(me.s != core)
-        def _():
-            mate.start()
-
-    def wait_owned(src, dst, core, i):
-        across, local, mate = owned_out(src, dst, core, i)
-        across.wait_send()
-
-        @pl.when(me.s == core)
-        def _():
-            local.wait()
-            mate.wait_recv()
-            for n in range(2):
-                push(src.at[0], at(dst, n), oss.at[i], ors.at[i + n], me.across_core(core)).wait_recv()
-
-        @pl.when(me.s != core)
-        def _():
-            mate.wait_send()
-
-    owned_out(y_in, so, 1, 1)[0].start()
-    start_here(y_in, so, 1, 1)
+    dh_over = push(dh_in.at[ds(me.py * 2 * half, 2 * half)], dhx, oss.at[2], ors.at[3], me.across)
+
+    @pl.when(me.s == 1)
+    def _():
+        dh_over.start()
+
+    xs = OwnedOut(me, dx, dxx, 0, oss, ors, lsem.at[14])
     old = [pltpu.make_async_copy(out1, fr, lsem.at[15]), pltpu.make_async_copy(outq, fq, lsem.at[16])]
 
     @pl.when(me.s == 1)
@@ -1632,44 +1666,46 @@
     for c in loads[6:]:
         c.wait()
 
+    nf = gq.shape[0]
+    accs = [dk.at[0:nf], dk.at[nf : 2 * nf], dv.at[0:nf]]
+    for acc in accs:
+        acc[...] = jnp.zeros_like(acc)
+
+    def body(i, _):
+        rows = ds(i * half, half)
+        n1t = n1[rows, :].T
+        for p, acc in enumerate(accs):
+            acc[...] += dot(n1t, dmix[rows, p * HW : (p + 1) * HW])
+        return 0
+
+    lax.fori_loop(0, 8, body, 0)
+    for p, acc in enumerate(accs):
+        gq[:, p * HW : (p + 1) * HW] = acc[...].astype(BF)
+    redq.send()
+
     def early():
         va[0, 0:8, :] = vgf[...] + vd0[...]
         va[0, 8:16, :] = vf1[...] + vd1[...]
+        redq.step(0)
         vr_.send(0)
-        nf = gq.shape[0]
-        accs = [dk.at[0:nf], dk.at[nf : 2 * nf], dv.at[0:nf]]
-        for acc in accs:
-            acc[...] = jnp.zeros_like(acc)
-
-        def body(i, _):
-            rows = ds(i * half, half)
-            n1t = n1[rows, :].T
-            for p, acc in enumerate(accs):
-                acc[...] += dot(n1t, dmix[rows, p * HW : (p + 1) * HW])
-            return 0
-
-        lax.fori_loop(0, 8, body, 0)
-        for p, acc in enumerate(accs):
-            gq[:, p * HW : (p + 1) * HW] = acc[...].astype(BF)
+        redq.step(1)
         vr_.add(0, va.at[1])
         vr_.send(1)
-        redq.send()
-        vr_.add(1, va.at[2])
-        vr_.send(2)
-        redq.step(0)
 
     sc.run(lambda r0, i: back_tail(r0, half, dmix, xf, e2, wqkv, vecs.at[0], part, vgf), early)
-    for d in range(1, dp - 1):
+    for d in range(2, dp - 1):
         redq.step(d)
+    vr_.add(1, va.at[2])
+    vr_.send(2)
 
     def write(n, i, value):
         dx[sc.side(n), ds(i * SUB, SUB), :] = value
 
     def leave(n):
         if n == 0:
-            owned_out(dx, ig, 0, 4)[0].start()
+            xs.far().start()
         else:
-            start_here(dx, ig, 0, 4)
+            xs.start_here()
 
     grad_out(sc, lambda n, i: dh[sc.side(n), ds(i * SUB, SUB), :], xf, vecs.at[0], write, leave)
     redq.step(dp - 1)
@@ -1690,30 +1726,25 @@
     redq.finish()
     vr_.finish()
     sc.finish()
-    for n in range(2):
-
-        @pl.when(me.s == n)
-        def _(n=n):
-            for c in whole(n):
-                c.wait()
-
-    wait_owned(y_in, so, 1, 1)
-    wait_owned(dx, ig, 0, 4)
+    @pl.when(me.s == 1)
+    def _():
+        dh_over.wait()
+
+    xs.wait()
     for c in ends:
         c.wait()
 
 
-def layer_last(cfg, q, k, v, o, do, lse, sr, kc, tab, e2, dh, xf, n1, w0, vecs, vf1, vd1, vd0, gr0, out1, outq, hf, y):
+def layer_last(cfg, q, k, v, o, do, lse, sr, kc, tab, e2, dh, xf, n1, w0, vecs, vf1, vd1, vd0, gr0, out1, outq):
     seq, model = xf.shape
     dp, tensor, ff = cfg["dp"], cfg["tensor"], cfg["ff"]
     rows, nr, nq = model // dp, 2 * ff + HW, 3 * HW
     nv = dp + tensor - 1
     wide, owned, heads = pltpu.VMEM((seq, model), BF), pltpu.VMEM((2, seq // 8, model), BF), pltpu.VMEM((seq, HW), BF)
-    both = sds((1, 2, 1, seq // 4, model), BF)
     return pl.pallas_call(
         functools.partial(last_kernel, cfg),
-        out_shape=(both, both, sds((rows, nq), F32), sds((rows, nr), F32), sds((8, model), F32)),
-        in_specs=[ANY] * 5 + [VMEM] * 3 + [ANY] * 6 + [VMEM] * 4 + [ANY] * 5,
+        out_shape=(sds((seq // 4, model), BF), sds((2, 2, seq // 8, model), BF), sds((rows, nq), F32), sds((rows, nr), F32), sds((8, model), F32)),
+        in_specs=[ANY] * 5 + [VMEM] * 3 + [ANY] * 6 + [VMEM] * 4 + [ANY] * 3,
         out_specs=(ANY, ANY, ANY, ANY, VMEM),
         scratch_shapes=[
             heads, heads, heads, heads, heads, pltpu.VMEM(tab.shape, F32), pltpu.VMEM((HW, seq), BF),
@@ -1728,21 +1759,49 @@
             pltpu.VMEM((16, model), F32),
         ]
         + scatter_scratch(seq, model)
-        + [DMA((17,)), DMA((nv,)), DMA((nv,)), DMA((7,)), DMA((7,))]
+        + [DMA((17,)), DMA((nv,)), DMA((nv,)), DMA((3,)), DMA((4,))]
         + GradReduce.scratch(dp) * 2,
         compiler_params=params(6),
         cost_estimate=cost(80),
         name="layer_last",
-    )(q, k, v, o, do, lse, sr, kc, tab, e2, dh, xf, n1, w0, vecs, vf1, vd1, vd0, gr0, out1, outq, hf, y)
+    )(q, k, v, o, do, lse, sr, kc, tab, e2, dh, xf, n1, w0, vecs, vf1, vd1, vd0, gr0, out1, outq)
 
 
 def finish_kernel(
-    cfg, so_in, ig_in, fq_in, fr_in, vec, so, ig, bg1, bb1, gqkv, bqkv, gout, bdy, bdy2, bg2, bb2, gfc1, bfc1, gfc2,
-    a, b, fq, fr, lsem, osem,
+    cfg, hf, hx, yx, dhf, dhx, dxx, fq_in, fr_in, vec, so, ig, bg1, bb1, gqkv, bqkv, gout, bdy, bdy2, bg2, bb2, gfc1, bfc1, gfc2,
+    a, b, fq, fr, lsem, msem, osem,
 ):
     heads, ff, own, qw, fw = cfg["heads"], cfg["ff"], cfg["own"], cfg["qw"], cfg["fw"]
     me = Mesh(cfg["dp"], cfg["tensor"])
-    loads = load([(fr_in, fr), (fq_in, fq), (so_in, a), (ig_in, b)], lsem)
+    loads = load([(fr_in, fr), (fq_in, fq)], lsem)
+    half = a.shape[2]
+    mine = [ref.at[pl.ds(pl.multiple_of((2 * me.t + n) * half, half), half)] for ref in (hf, dhf) for n in range(2)]
+
+    def sources(core):
+        if core == 0:
+            first, second = [mine[0:2], [hx.at[pl.ds(n * half, half)] for n in range(2)]], None
+        else:
+            first, second = None, [mine[2:4], [dhx.at[pl.ds(n * half, half)] for n in range(2)]]
+        whole = yx if core else dxx
+        third = [[whole.at[me.y, n] for n in range(2)], [whole.at[1 - me.y, n] for n in range(2)]]
+        return (first or third), (second or third)
+
+    def moves(core):
+        out = []
+        for o, (ref, src) in enumerate(zip((a, b), sources(core))):
+            for m in range(2):
+                for n in range(2):
+                    dst = ref.at[me.y if m == 0 else 1 - me.y, n]
+                    out.append(pltpu.make_async_copy(src[m][n], dst, msem.at[4 * o + 2 * m + n]))
+        return out
+
+    for core in range(2):
+
+        @pl.when(me.s == core)
+        def _(core=core):
+            for c in moves(core):
+                c.start()
+
     model = vec.shape[1]
     short = pltpu.roll(vec[...], (model - (me.z * me.tensor + me.t) * own) % model, 1)
     for row, ref in ((0, bg1), (1, bb1), (2, bdy), (2, bdy2), (3, bg2), (4, bb2)):
@@ -1759,9 +1818,19 @@
     gfc1[0] = fr[:, 0:ff]
     gfc2[...] = fr[:, ff : 2 * ff]
     gout[0] = fr[:, 2 * ff : 2 * ff + HW].T[0 : heads * HD, :]
-    loads[2].wait()
-    loads[3].wait()
-    outs = [pltpu.make_async_copy(a, so, osem.at[0]), pltpu.make_async_copy(b, ig, osem.at[1])]
+    for core in range(2):
+
+        @pl.when(me.s == core)
+        def _(core=core):
+            for c in moves(core):
+                c.wait()
+
+    outs = []
+    for o, (ref, dst) in enumerate(((a, so), (b, ig))):
+        for m in range(2):
+            for n in range(2):
+                place = dst.at[0, m, 0, pl.ds(n * half, half)]
+                outs.append(pltpu.make_async_copy(ref.at[m, n], place, osem.at[4 * o + 2 * m + n]))
     for c in outs:
         c.start()
     loads[1].wait()
@@ -1771,24 +1840,25 @@
         c.wait()
 
 
-def finish(cfg, so, ig, fq, fr, vec):
+def finish(cfg, hf, hx, yx, dhf, dhx, dxx, fq, fr, vec):
     heads, ff, rows = cfg["heads"], cfg["ff"], fq.shape[0]
     line = sds((1, cfg["own"]), F32)
+    both = sds((1, 2, 1) + hx.shape, BF)
     return pl.pallas_call(
         functools.partial(finish_kernel, cfg),
-        out_shape=(sds(so.shape, BF), sds(ig.shape, BF), line, line, sds((1, rows, heads * 3 * HD), F32),
+        out_shape=(both, both, line, line, sds((1, rows, heads * 3 * HD), F32),
                    sds((heads, 1, cfg["qw"]), F32), sds((1, heads * HD, rows), F32), line, line, line, line,
                    sds((1, rows, ff), F32), sds((heads, 1, cfg["fw"]), F32), sds((rows, ff), F32)),
-        in_specs=[ANY] * 4 + [VMEM],
+        in_specs=[ANY] * 8 + [VMEM],
         out_specs=(ANY, ANY) + (VMEM,) * 12,
         scratch_shapes=[
-            pltpu.VMEM(so.shape, BF), pltpu.VMEM(ig.shape, BF), pltpu.VMEM(fq.shape, F32), pltpu.VMEM(fr.shape, F32),
-            DMA((4,)), DMA((2,)),
+            pltpu.VMEM(yx.shape, BF), pltpu.VMEM(yx.shape, BF), pltpu.VMEM(fq.shape, F32), pltpu.VMEM(fr.shape, F32),
+            DMA((2,)), DMA((8,)), DMA((8,)),
         ],
         compiler_params=pltpu.CompilerParams(vmem_limit_bytes=67043328),
         cost_estimate=cost(5),
         name="finish",
-    )(so, ig, fq, fr, vec)
+    )(hf, hx, yx, dhf, dhx, dxx, fq, fr, vec)
 
 
 def by_part(w):
@@ -1821,7 +1891,7 @@
     cfg = {
         "col": col, "ff": ff, "heads": heads, "dp": dp, "tensor": tensor, "own": small.shape[1],
         "qw": qkv_bias.shape[2], "fw": fc1_bias.shape[2],
-        "groups": [(0, col["fc1"]), (col["fc1"], col["fc2"]), (col["fc2"], col["end"])],
+        "groups": [(0, col["fc1"]), (col["fc1"], col["fc2"]), (col["fc2"], col["out"]), (col["out"], col["end"])],
     }
 
     xf, n1a, n2a, ga, gpa, tab, w0, qa, ka, va, cf, vecs, sr, kc = layer_in(
@@ -1829,17 +1899,15 @@
     )
     oa, lsea, hf, n1b, n2b, gb, gpb, w1, qb, kb, vb = layer_mid(cfg, qa, ka, va, sr, kc, ga, xf, w, w0, vecs, tab)
     ob, lseb = attn_fwd(heads, segments, live_blocks, qb, kb, vb, sr, kc)
-    y, dob, e2b, grb, vdb = layer_turn(cfg, ob, gb, hf, cf, w1, vecs, n2b, gpb)
+    y, dob, e2b, grb, hx, cy, vdb = layer_turn(cfg, ob, gb, hf, cf, cotangent, w1, vecs, n2b, gpb)
     dmb = attn_bwd(heads, segments, live_blocks, qb, kb, vb, ob, dob, lseb, sr, kc, tab)
-    dhf, e2a, doa, vfb, vda, out1, outq, gra = layer_back(
-        cfg, dmb, e2b, cf, hf, n1b, w1, w0, vecs, xf, ga, gpa, n2a, oa, grb
+    dhf, e2a, doa, vfb, vda, out1, outq, gra, yx = layer_back(
+        cfg, dmb, e2b, cf, cy, hf, n1b, w1, w0, vecs, xf, ga, gpa, n2a, oa, grb, y
     )
-    last_part = finish(
-        cfg,
-        *layer_last(
-            cfg, qa, ka, va, oa, doa, lsea, sr, kc, tab, e2a, dhf, xf, n1a, w0, vecs, vfb, vdb, vda, gra, out1, outq, hf, y
-        ),
+    dhx, dxx, fq, fr_, gv = layer_last(
+        cfg, qa, ka, va, oa, doa, lsea, sr, kc, tab, e2a, dhf, xf, n1a, w0, vecs, vfb, vdb, vda, gra, out1, outq
     )
+    last_part = finish(cfg, hf, hx, yx, dhf, dhx, dxx, fq, fr_, gv)
     so, ig, bg1, bb1, gqkv, bqkv, gout, bdy, bdy2, bg2, bb2, gfc1, bfc1, gfc2 = last_part
     bqkv, bfc1, gfc2 = bqkv.transpose(1, 0, 2), bfc1.transpose(1, 0, 2), gfc2.T[None]
     return (so, ig, bg1, bb1, gqkv, bqkv, gout, bdy, bg2, bb2, gfc1, bfc1, gfc2, bdy2)

time: 395 us -> 395 us (level)
    pallas_call x1, Pallas kernels: 29 us -> 46.6 us  [layer_turn(): pl.pallas_call(functools.partial(turn_kernel, cfg), out_shape=(sds(owned,...]
    pallas_call x1, Pallas kernels: 78.6 us -> 66.1 us  [layer_in(): pl.pallas_call(functools.partial(in_kernel, cfg), out_shape=(rows, rows,...]
    pallas_call x2, Pallas kernels: 113 us -> 103 us  [the longest x1 97.4 us: layer_last(): pl.pallas_call(functools.partial(last_kernel, cfg), out_shape=(sds((seq /...]
    pallas_call x1, Pallas kernels: 59.1 us -> 65.5 us  [layer_mid(): pl.pallas_call(functools.partial(mid_kernel, cfg), out_shape=(heads, sds(...]
    pallas_call x1, Pallas kernels: 38.4 us -> 33.9 us  [attn_bwd(): pl.pallas_call(functools.partial(attn_bwd_kernel, heads), out_shape=sds((...]
where the time goes in v5:
time: 395 us; the launch traced here: 393 us
  Pallas kernels  387 us (98%)
    pallas_call x1, Pallas kernels, layer_last(): pl.pallas_call(functools.partial(last_kernel, cfg), out_shape=(sds((seq /...  97.4 us
    pallas_call x1, Pallas kernels, layer_in(): pl.pallas_call(functools.partial(in_kernel, cfg), out_shape=(rows, rows,...  66.1 us
    pallas_call x1, Pallas kernels, layer_mid(): pl.pallas_call(functools.partial(mid_kernel, cfg), out_shape=(heads, sds(...  65.5 us
    pallas_call x1, Pallas kernels, layer_back(): pl.pallas_call(functools.partial(back_kernel, cfg), out_shape=(sds((seq,...  53.1 us
    pallas_call x1, Pallas kernels, layer_turn(): pl.pallas_call(functools.partial(turn_kernel, cfg), out_shape=(sds(owned,...  46.6 us
    pallas_call x1, Pallas kernels, attn_bwd(): pl.pallas_call(functools.partial(attn_bwd_kernel, heads), out_shape=sds((...  33.9 us
    pallas_call x1, Pallas kernels, attn_fwd(): pl.pallas_call(functools.partial(attn_fwd_kernel, heads), out_shape=(sds(...  18 us

profile of v5, /device:TPU:0, one launch (start us, length us, event | category | flops | bytes accessed | tf_op | source)
XLA Modules:
  0.0 393.0 jit_solution(4455252725070016236)
XLA Ops:
  0.6 0.0 copy-start
  0.7 0.0 copy-start.1
  0.7 0.8 stack.3
  1.5 0.7 fusion.7
  2.2 0.6 pad_convert_fusion.sv_ref
  2.8 1.0 copy.36
  3.8 1.1 copy.33
  5.0 0.2 copy.37
  5.1 0.0 copy-done
  5.2 0.0 copy-done.1
  5.2 1.0 fusion.1.w_ref
  6.2 66.1 %layer_in.1 = (bf16[2048,768]{1,0:T(8,128)(2,1)}, bf16[2048,768]{1,0:T(8,128)(2,1)}, bf16[2048,768]{1,0:T(8,128)(2,1)}, bf16[2048,768]{1,0:T(8,128)(2,1)}, bf16[...) custom-call(bf16[2,1,512,768]{3,2,1,0:T(8,128)(2,1)} %in_ref.1, ...), custom_call_target="tpu_custom_call" | custom-call | flops 35999997952 | tf_op jit(solution)/shard_map/layer_in/pallas_call | solution.py:1137
  72.3 65.5 %layer_mid.1 = (bf16[2048,256]{1,0:T(8,128)(2,1)}, f32[8,2048]{1,0:T(8,128)}, bf16[2048,768]{1,0:T(8,128)(2,1)}, bf16[2048,768]{1,0:T(8,128)(2,1)}, bf16[2048,76...) custom-call(bf16[2048,256]{1,0:T(8,128)(2,1)} %get-tuple-element.76., ...), custom_call_target="tpu_custom_call" | custom-call | flops 56000000000 | tf_op jit(solution)/shard_map/layer_mid/pallas_call | solution.py:1266
  137.8 18.0 %attn_fwd.1 = (bf16[2048,256]{1,0:T(8,128)(2,1)}, f32[8,2048]{1,0:T(8,128)}) custom-call(s32[2,1,2048]{2,1,0:T(1,128)} %seg.3, s32[1,2]{1,0:T(1,128)} %bitcast.29, bf16[2048,256]{1,0:T(8,128)(2,1)} %get-tuple-element.87.q_in, bf16[2048,256]{1,0:T(8,128)(2,1)} %get-tuple-element.88.k_in, bf16[2048,256]{1,0:T(8,128)(2,1)} %get-tuple-element.89.v_in, ...), custom_call_target="tpu_custom_call" | custom-call | flops 9600000000 | tf_op jit(solution)/shard_map/attn_fwd/pallas_call | solution.py:159
  155.7 46.6 %layer_turn.1 = (bf16[2,256,768]{2,1,0:T(8,128)(2,1)}, bf16[2048,256]{1,0:T(8,128)(2,1)}, bf16[2048,768]{1,0:T(8,128)(2,1)}, bf16[768,1792]{1,0:T(8,128)(2,1)}, ...) custom-call(bf16[2048,256]{1,0:T(8,128)(2,1)} %get-tuple-element.90.o_in, ...), custom_call_target="tpu_custom_call" | custom-call | flops 32000000000 | tf_op jit(solution)/shard_map/layer_turn/pallas_call | solution.py:1386
  202.3 33.9 %attn_bwd.1.dm_in = bf16[2048,768]{1,0:T(8,128)(2,1)} custom-call(s32[2,1,2048]{2,1,0:T(1,128)} %seg.3, s32[1,2]{1,0:T(1,128)} %bitcast.30, bf16[2048,256]{1,0:T(8,128)(2,1)} %get-tuple-element.87.q_in, bf16[2048,256]{1,0:T(8,128)(2,1)} %get-tuple-element.88.k_in, bf16[2048,256]{1,0:T(8,128)(2,1)} %get-tuple-element.89.v_in, ...), custom_call_target="tpu_custom_call" | custom-call | flops 20800000000 | tf_op jit(solution)/shard_map/attn_bwd/pallas_call | solution.py:270
  236.2 53.1 %layer_back.1 = (bf16[2048,768]{1,0:T(8,128)(2,1)}, bf16[2048,768]{1,0:T(8,128)(2,1)}, bf16[2048,256]{1,0:T(8,128)(2,1)}, f32[8,768]{1,0:T(8,128)}, f32[8,768]{1...) custom-call(bf16[2048,768]{1,0:T(8,128)(2,1)} %attn_bwd.1.dm_in, ...), custom_call_target="tpu_custom_call" | custom-call | flops 56000000000 | tf_op jit(solution)/shard_map/layer_back/pallas_call | solution.py:1536
  289.3 97.4 %layer_last.1 = (bf16[512,768]{1,0:T(8,128)(2,1)}, bf16[2,2,256,768]{3,2,1,0:T(8,128)(2,1)}, f32[192,768]{1,0:T(8,128)}, f32[192,1792]{1,0:T(8,128)}, f32[8,768]{1,0:T(8,128)}) custom-call(bf16[2048,256]{1,0:T(8,128)(2,1)} %get-tuple-element.76.q_in, bf16[2048,256]{1,0:T(8,128)(2,1)} %get-tuple-element.77.k_in, bf16[2048,256]{1,0:T(8,128)(2,1)} %get-tuple-element.78.v_in, ...), custom_call_target="tpu_custom_call" | custom-call | flops 64000000000 | tf_op jit(solution)/shard_map/layer_last/pallas_call | solution.py:1744
  386.7 6.1 %finish.1 = (bf16[1,2,1,512,768]{4,3,2,1,0:T(8,128)(2,1)}, bf16[1,2,1,512,768]{4,3,2,1,0:T(8,128)(2,1)}, f32[1,48]{1,0:T(1,128)}, f32[1,48]{1,0:T(1,128)}, f32[1...) custom-call(bf16[2048,768]{1,0:T(8,128)(2,1)} %get-tuple-element.86., ...), custom_call_target="tpu_custom_call" | custom-call | flops 4000000000 | tf_op jit(solution)/shard_map/finish/pallas_call | solution.py:1847
  (2 shorter events, 0.1 us)
Async XLA Ops:
  0.6 4.5 %copy-start = (bf16[1,768,192]{1,2,0:T(8,128)(2,1)S(1)}, bf16[1,768,192]{1,2,0:T(8,128)(2,1)}, u32[]{:S(2)}) copy-start(bf16[1,768,192]{1,2,0:T(8,128)(2,1)} %param.31) | copy-start | bytes 884740
  0.7 4.5 %copy-start.1 = (bf16[1,192,768]{2,1,0:T(8,128)(2,1)S(1)}, bf16[1,192,768]{2,1,0:T(8,128)(2,1)}, u32[]{:S(2)}) copy-start(bf16[1,192,768]{2,1,0:T(8,128)(2,1)} %param.29) | copy-start | bytes 884740

commit v6 on v5

--- a/solution.py
+++ b/solution.py
@@ -1156,10 +1156,10 @@
 
 
 def mid_kernel(
-    cfg, q_in, k_in, v_in, srow, kcol, g_in, x_in, w_ref, w0, vecs, tab_in,
-    o_o, lse, hf_o, n1_o, n2_o, g_o, gp_o, w_o, q_o, k_o, v_o,
+    cfg, q_in, k_in, v_in, srow, kcol, g_in, x_in, cot_ref, w_ref, w0, vecs, tab_in,
+    o_o, lse, hf_o, n1_o, n2_o, g_o, gp_o, w_o, q_o, k_o, v_o, cy,
     wout, wfc2, hf, n1, n2, g, gp, tab, wfull, gat, q, k, v, o, vt, s_scr,
-    part, mr, xr, sss, srs, gss, grs, lsem, ssem, osem, *wsems,
+    part, mr, xr, sss, srs, gss, grs, lsem, ssem, osem, yss, yrs, *wsems,
 ):
     col, heads = cfg["col"], cfg["heads"]
     me = Mesh(cfg["dp"], cfg["tensor"])
@@ -1181,6 +1181,7 @@
     )
     greet([me.mate, me.beside, me.across, me.across_mate] + me.ring)
     wg = WeightGather(me, 1, w_ref, wfull, gat, cfg["groups"], wsems)
+    over = push(cot_ref.at[1 - me.y, 0, ds(me.s * half, half)], cy, yss.at[0], yrs.at[0], me.across)
     wg.send_ring()
     for n in range(4):
         wg.send_own(n)
@@ -1240,6 +1241,7 @@
         @pl.when(i == 7)
         def _():
             wg.forward(3)
+            over.start()
 
     ga.run(work)
 
@@ -1256,18 +1258,20 @@
     sc.finish()
     wg.finish()
     st_o.finish()
+    over.wait()
     w_out.wait()
 
 
-def layer_mid(cfg, q, k, v, srow, kcol, g, xf, w, w0, vecs, tab):
+def layer_mid(cfg, q, k, v, srow, kcol, g, xf, cotangent, w, w0, vecs, tab):
     seq, model, ff = tab.shape[0], xf.shape[1], cfg["ff"]
     rows, hidden, heads = sds((seq, model), BF), sds((seq, ff), BF), sds((seq, HW), BF)
     wide, wide_h, wide_q = pltpu.VMEM((seq, model), BF), pltpu.VMEM((seq, ff), BF), pltpu.VMEM((seq, HW), BF)
     return pl.pallas_call(
         functools.partial(mid_kernel, cfg),
-        out_shape=(heads, sds((8, seq), F32), rows, rows, rows, hidden, hidden, sds(w0.shape, BF), heads, heads, heads),
-        in_specs=[ANY, ANY, ANY, VMEM, VMEM, ANY, ANY, VMEM, ANY, VMEM, ANY],
-        out_specs=(ANY, VMEM) + (ANY,) * 9,
+        out_shape=(heads, sds((8, seq), F32), rows, rows, rows, hidden, hidden, sds(w0.shape, BF), heads, heads, heads,
+                   sds((seq // 8, model), BF)),
+        in_specs=[ANY, ANY, ANY, VMEM, VMEM, ANY, ANY, ANY, VMEM, ANY, VMEM, ANY],
+        out_specs=(ANY, VMEM) + (ANY,) * 10,
         scratch_shapes=[
             pltpu.VMEM((model, HW), BF), pltpu.VMEM((model, ff), BF),
             wide, wide, wide, wide_h, wide_h, pltpu.VMEM((seq, 256), F32),
@@ -1276,16 +1280,16 @@
             pltpu.VMEM((cfg["heads"], DOC_MAX + QB, QB), F32),
         ]
         + scatter_scratch(seq, model)
-        + [DMA((6,)), DMA((6,)), DMA((9,)), DMA((8, 8)), DMA((1, 8))]
+        + [DMA((6,)), DMA((6,)), DMA((9,)), DMA((8, 8)), DMA((1, 8)), DMA((1,)), DMA((1,))]
         + WeightGather.scratch(cfg["dp"], 4),
         compiler_params=params(3),
         cost_estimate=cost(70),
         name="layer_mid",
-    )(q, k, v, srow, kcol, g, xf, w, w0, vecs, tab)
+    )(q, k, v, srow, kcol, g, xf, cotangent, w, w0, vecs, tab)
 
 
 def turn_kernel(
-    cfg, o_in, g_in, hf_in, cf, cot_ref, w1, vecs, n2_in, gp_in, y_o, do_o, e2_o, gr_o, hx, cy, vg,
+    cfg, o_in, g_in, hf_in, cf, cy, w1, vecs, n2_in, gp_in, y_o, do_o, e2_o, gr_o, hx, vg,
     o, g, hf, dyf, n2, gp, e2, do, y, gr, wout, wfc2, wfc1, da, acc,
     part, mr, xr, sss, srs, gss, grs, yss, yrs, lsem, ssem,
 ):
@@ -1297,6 +1301,7 @@
     near = ds(4 * me.y * half, 4 * half)
     loads = load(
         [
+            (cy, dyf.at[ds(gt.own(1 - me.y), half)]),
             (w1.at[:, col["out"] : col["end"]], wout),
             (w1.at[:, col["fc2"] : col["out"]], wfc2),
             (o_in, o),
@@ -1310,18 +1315,15 @@
         lsem,
     )
     greet([me.mate, me.beside, me.across])
-    over = push(
-        cot_ref.at[1 - me.y, 0, ds(me.s * half, half)], dyf.at[ds(gt.own(me.y), half)], yss.at[0], yrs.at[0], me.across
-    )
-    over.start()
-    cy_out = pltpu.make_async_copy(dyf.at[ds(gt.own(1 - me.y), half)], cy, lsem.at[2])
-    h_over = push(hf_in.at[ds(me.py * 2 * half, 2 * half)], hx, yss.at[1], yrs.at[1], me.across)
+    loads[0].wait()
+    gt.start(1)
+    h_over = push(hf_in.at[ds(me.py * 2 * half, 2 * half)], hx, yss.at[0], yrs.at[0], me.across)
 
     @pl.when(me.s == 0)
     def _():
         h_over.start()
 
-    for c in loads[:4]:
+    for c in loads[1:5]:
         c.wait()
     vec = vecs.at[1]
     st = Stores([(e2, e2_o), (do, do_o)], half, ssem)
@@ -1329,11 +1331,8 @@
     def early():
         vg[...] = jnp.zeros_like(vg)
         acc[...] = jnp.zeros_like(acc)
-        for c in loads[4:]:
+        for c in loads[5:]:
             c.wait()
-        over.wait_recv()
-        gt.start(1)
-        cy_out.start()
 
         def head(i, _):
             for n, step in ((5, 3), (6, 6), (7, 7)):
@@ -1365,8 +1364,6 @@
     y_out.start()
     sc.finish()
     st.finish()
-    cy_out.wait()
-    over.wait_send()
     for n in (1, 3, 5):
         gt.plan(n).wait_send()
 
@@ -1378,7 +1375,7 @@
     y_out.wait()
 
 
-def layer_turn(cfg, o, g, hf, cf, cotangent, w1, vecs, n2, gp):
+def layer_turn(cfg, o, g, hf, cf, cy, w1, vecs, n2, gp):
     seq, model = hf.shape
     ff = cfg["ff"]
     wide, hidden, heads = pltpu.VMEM((seq, model), BF), pltpu.VMEM((seq, ff), BF), pltpu.VMEM((seq, HW), BF)
@@ -1391,11 +1388,10 @@
             sds((seq, model), BF),
             sds((model, 2 * ff + HW), BF),
             sds((seq // 4, model), BF),
-            sds((seq // 8, model), BF),
             sds((8, model), F32),
         ),
         in_specs=[ANY] * 6 + [VMEM, ANY, ANY],
-        out_specs=(ANY,) * 6 + (VMEM,),
+        out_specs=(ANY,) * 5 + (VMEM,),
         scratch_shapes=[
             heads, hidden, wide, wide, wide, hidden, wide, heads, pltpu.VMEM(owned, BF),
             pltpu.VMEM((model, 2 * ff + HW), BF),
@@ -1403,11 +1399,11 @@
             pltpu.VMEM((seq // 8, ff), BF), pltpu.VMEM((model, 2 * ff + HW), F32),
         ]
         + scatter_scratch(seq, model)
-        + [DMA((6,)), DMA((6,)), DMA((2,)), DMA((2,)), DMA((9,)), DMA((2, 8))],
+        + [DMA((6,)), DMA((6,)), DMA((1,)), DMA((1,)), DMA((10,)), DMA((2, 8))],
         compiler_params=params(4),
         cost_estimate=cost(40),
         name="layer_turn",
-    )(o, g, hf, cf, cotangent, w1, vecs, n2, gp)
+    )(o, g, hf, cf, cy, w1, vecs, n2, gp)
 
 
 def back_kernel(
@@ -1611,10 +1607,6 @@
 
     dh_over = push(dh_in.at[ds(me.py * 2 * half, 2 * half)], dhx, oss.at[2], ors.at[3], me.across)
 
-    @pl.when(me.s == 1)
-    def _():
-        dh_over.start()
-
     xs = OwnedOut(me, dx, dxx, 0, oss, ors, lsem.at[14])
     old = [pltpu.make_async_copy(out1, fr, lsem.at[15]), pltpu.make_async_copy(outq, fq, lsem.at[16])]
 
@@ -1639,6 +1631,11 @@
 
     def qloop(i, _):
         lo = jnp.maximum(i - DOC_MAX // QB, 0)
+
+        @pl.when((i == n_blocks // 2 + 1) & (me.s == 1))
+        def _():
+            dh_over.start()
+
         attn_bwd_block(i, lo, i, heads, q, k, v, o, do, kt, lse, srow, kcol, tab, dk, dv, dmix)
         for at_block, steps in (
             (n_blocks // 2 - 1, range(0, 1)),
@@ -1666,37 +1663,35 @@
     for c in loads[6:]:
         c.wait()
 
-    nf = gq.shape[0]
-    accs = [dk.at[0:nf], dk.at[nf : 2 * nf], dv.at[0:nf]]
-    for acc in accs:
-        acc[...] = jnp.zeros_like(acc)
-
-    def body(i, _):
-        rows = ds(i * half, half)
-        n1t = n1[rows, :].T
-        for p, acc in enumerate(accs):
-            acc[...] += dot(n1t, dmix[rows, p * HW : (p + 1) * HW])
-        return 0
-
-    lax.fori_loop(0, 8, body, 0)
-    for p, acc in enumerate(accs):
-        gq[:, p * HW : (p + 1) * HW] = acc[...].astype(BF)
-    redq.send()
-
     def early():
         va[0, 0:8, :] = vgf[...] + vd0[...]
         va[0, 8:16, :] = vf1[...] + vd1[...]
-        redq.step(0)
         vr_.send(0)
-        redq.step(1)
+        nf = gq.shape[0]
+        accs = [dk.at[0:nf], dk.at[nf : 2 * nf], dv.at[0:nf]]
+        for acc in accs:
+            acc[...] = jnp.zeros_like(acc)
+
+        def body(i, _):
+            rows = ds(i * half, half)
+            n1t = n1[rows, :].T
+            for p, acc in enumerate(accs):
+                acc[...] += dot(n1t, dmix[rows, p * HW : (p + 1) * HW])
+            return 0
+
+        lax.fori_loop(0, 8, body, 0)
+        for p, acc in enumerate(accs):
+            gq[:, p * HW : (p + 1) * HW] = acc[...].astype(BF)
         vr_.add(0, va.at[1])
         vr_.send(1)
+        redq.send()
+        vr_.add(1, va.at[2])
+        vr_.send(2)
+        redq.step(0)
 
     sc.run(lambda r0, i: back_tail(r0, half, dmix, xf, e2, wqkv, vecs.at[0], part, vgf), early)
-    for d in range(2, dp - 1):
+    for d in range(1, dp - 1):
         redq.step(d)
-    vr_.add(1, va.at[2])
-    vr_.send(2)
 
     def write(n, i, value):
         dx[sc.side(n), ds(i * SUB, SUB), :] = value
@@ -1897,9 +1892,11 @@
     xf, n1a, n2a, ga, gpa, tab, w0, qa, ka, va, cf, vecs, sr, kc = layer_in(
         cfg, inputs, cotangent, segments, live_blocks, w, sv, fr
     )
-    oa, lsea, hf, n1b, n2b, gb, gpb, w1, qb, kb, vb = layer_mid(cfg, qa, ka, va, sr, kc, ga, xf, w, w0, vecs, tab)
+    oa, lsea, hf, n1b, n2b, gb, gpb, w1, qb, kb, vb, cy = layer_mid(
+        cfg, qa, ka, va, sr, kc, ga, xf, cotangent, w, w0, vecs, tab
+    )
     ob, lseb = attn_fwd(heads, segments, live_blocks, qb, kb, vb, sr, kc)
-    y, dob, e2b, grb, hx, cy, vdb = layer_turn(cfg, ob, gb, hf, cf, cotangent, w1, vecs, n2b, gpb)
+    y, dob, e2b, grb, hx, vdb = layer_turn(cfg, ob, gb, hf, cf, cy, w1, vecs, n2b, gpb)
     dmb = attn_bwd(heads, segments, live_blocks, qb, kb, vb, ob, dob, lseb, sr, kc, tab)
     dhf, e2a, doa, vfb, vda, out1, outq, gra, yx = layer_back(
         cfg, dmb, e2b, cf, cy, hf, n1b, w1, w0, vecs, xf, ga, gpa, n2a, oa, grb, y

time: 395 us -> 398 us (level)
  Pallas kernels: 387 us -> 391 us
    pallas_call x1, Pallas kernels: 46.6 us -> 37 us  [layer_turn(): pl.pallas_call(functools.partial(turn_kernel, cfg), out_shape=(sds(owned,...]
    pallas_call x1, Pallas kernels: 65.5 us -> 71.7 us  [layer_mid(): pl.pallas_call(functools.partial(mid_kernel, cfg), out_shape=(heads, sds(...]
    pallas_call x1, Pallas kernels: 53.1 us -> 58.9 us  [layer_back(): pl.pallas_call(functools.partial(back_kernel, cfg), out_shape=(sds((seq,...]
    pallas_call x1, Pallas kernels: 97.4 us -> 103 us  [layer_last(): pl.pallas_call(functools.partial(last_kernel, cfg), out_shape=(sds((seq /...]
where the time goes in v6:
time: 398 us
  Pallas kernels  391 us (98%)
    pallas_call x1, Pallas kernels, layer_last(): pl.pallas_call(functools.partial(last_kernel, cfg), out_shape=(sds((seq /...  103 us
    pallas_call x1, Pallas kernels, layer_mid(): pl.pallas_call(functools.partial(mid_kernel, cfg), out_shape=(heads, sds(...  71.7 us
    pallas_call x1, Pallas kernels, layer_in(): pl.pallas_call(functools.partial(in_kernel, cfg), out_shape=(rows, rows,...  66.1 us
    pallas_call x1, Pallas kernels, layer_back(): pl.pallas_call(functools.partial(back_kernel, cfg), out_shape=(sds((seq,...  58.9 us
    pallas_call x1, Pallas kernels, layer_turn(): pl.pallas_call(functools.partial(turn_kernel, cfg), out_shape=(sds(owned,...  37 us
    pallas_call x1, Pallas kernels, attn_bwd(): pl.pallas_call(functools.partial(attn_bwd_kernel, heads), out_shape=sds((...  31.6 us
    pallas_call x1, Pallas kernels, attn_fwd(): pl.pallas_call(functools.partial(attn_fwd_kernel, heads), out_shape=(sds(...  16.8 us

profile of v6, /device:TPU:0, one launch (start us, length us, event | category | flops | bytes accessed | tf_op | source)
XLA Modules:
  0.0 397.5 jit_solution(13555104724759263354)
XLA Ops:
  0.6 0.0 copy-start
  0.7 0.0 copy-start.1
  0.7 0.8 stack.3
  1.5 0.7 fusion.7
  2.2 0.6 pad_convert_fusion.sv_ref
  2.8 1.0 copy.36
  3.8 1.1 copy.33
  5.0 0.2 copy.37
  5.1 0.0 copy-done
  5.2 0.0 copy-done.1
  5.2 1.0 fusion.1.w_ref
  6.2 66.1 %layer_in.1 = (bf16[2048,768]{1,0:T(8,128)(2,1)}, bf16[2048,768]{1,0:T(8,128)(2,1)}, bf16[2048,768]{1,0:T(8,128)(2,1)}, bf16[2048,768]{1,0:T(8,128)(2,1)}, bf16[...) custom-call(bf16[2,1,512,768]{3,2,1,0:T(8,128)(2,1)} %in_ref.1, ...), custom_call_target="tpu_custom_call" | custom-call | flops 35999997952 | tf_op jit(solution)/shard_map/layer_in/pallas_call | solution.py:1137
  72.3 71.7 %layer_mid.1 = (bf16[2048,256]{1,0:T(8,128)(2,1)}, f32[8,2048]{1,0:T(8,128)}, bf16[2048,768]{1,0:T(8,128)(2,1)}, bf16[2048,768]{1,0:T(8,128)(2,1)}, bf16[2048,76...) custom-call(bf16[2048,256]{1,0:T(8,128)(2,1)} %get-tuple-element.76., ...), custom_call_target="tpu_custom_call" | custom-call | flops 56000000000 | tf_op jit(solution)/shard_map/layer_mid/pallas_call | solution.py:1269
  143.9 16.8 %attn_fwd.1 = (bf16[2048,256]{1,0:T(8,128)(2,1)}, f32[8,2048]{1,0:T(8,128)}) custom-call(s32[2,1,2048]{2,1,0:T(1,128)} %seg.3, s32[1,2]{1,0:T(1,128)} %bitcast.29, bf16[2048,256]{1,0:T(8,128)(2,1)} %get-tuple-element.87.q_in, bf16[2048,256]{1,0:T(8,128)(2,1)} %get-tuple-element.88.k_in, bf16[2048,256]{1,0:T(8,128)(2,1)} %get-tuple-element.89.v_in, ...), custom_call_target="tpu_custom_call" | custom-call | flops 9600000000 | tf_op jit(solution)/shard_map/attn_fwd/pallas_call | solution.py:159
  160.8 37.0 %layer_turn.1 = (bf16[2,256,768]{2,1,0:T(8,128)(2,1)}, bf16[2048,256]{1,0:T(8,128)(2,1)}, bf16[2048,768]{1,0:T(8,128)(2,1)}, bf16[768,1792]{1,0:T(8,128)(2,1)}, ...) custom-call(bf16[2048,256]{1,0:T(8,128)(2,1)} %get-tuple-element.90.o_in, bf16[2048,768]{1,0:T(8,128)(2,1)} %get-tuple-element.91.g_in, ...), custom_call_target="tpu_custom_call" | custom-call | flops 32000000000 | tf_op jit(solution)/shard_map/layer_turn/pallas_call | solution.py:1383
  197.8 31.6 %attn_bwd.1.dm_in = bf16[2048,768]{1,0:T(8,128)(2,1)} custom-call(s32[2,1,2048]{2,1,0:T(1,128)} %seg.3, s32[1,2]{1,0:T(1,128)} %bitcast.30, bf16[2048,256]{1,0:T(8,128)(2,1)} %get-tuple-element.87.q_in, bf16[2048,256]{1,0:T(8,128)(2,1)} %get-tuple-element.88.k_in, bf16[2048,256]{1,0:T(8,128)(2,1)} %get-tuple-element.89.v_in, ...), custom_call_target="tpu_custom_call" | custom-call | flops 20800000000 | tf_op jit(solution)/shard_map/attn_bwd/pallas_call | solution.py:270
  229.4 58.9 %layer_back.1 = (bf16[2048,768]{1,0:T(8,128)(2,1)}, bf16[2048,768]{1,0:T(8,128)(2,1)}, bf16[2048,256]{1,0:T(8,128)(2,1)}, f32[8,768]{1,0:T(8,128)}, f32[8,768]{1...) custom-call(bf16[2048,768]{1,0:T(8,128)(2,1)} %attn_bwd.1.dm_in, ...), custom_call_target="tpu_custom_call" | custom-call | flops 56000000000 | tf_op jit(solution)/shard_map/layer_back/pallas_call | solution.py:1532
  288.3 103.0 %layer_last.1 = (bf16[512,768]{1,0:T(8,128)(2,1)}, bf16[2,2,256,768]{3,2,1,0:T(8,128)(2,1)}, f32[192,768]{1,0:T(8,128)}, f32[192,1792]{1,0:T(8,128)}, f32[8,768]{1,0:T(8,128)}) custom-call(bf16[2048,256]{1,0:T(8,128)(2,1)} %get-tuple-element.76.q_in, bf16[2048,256]{1,0:T(8,128)(2,1)} %get-tuple-element.77.k_in, bf16[2048,256]{1,0:T(8,128)(2,1)} %get-tuple-element.78.v_in, ...), custom_call_target="tpu_custom_call" | custom-call | flops 64000000000 | tf_op jit(solution)/shard_map/layer_last/pallas_call | solution.py:1739
  391.3 6.1 %finish.1 = (bf16[1,2,1,512,768]{4,3,2,1,0:T(8,128)(2,1)}, bf16[1,2,1,512,768]{4,3,2,1,0:T(8,128)(2,1)}, f32[1,48]{1,0:T(1,128)}, f32[1,48]{1,0:T(1,128)}, f32[1...) custom-call(bf16[2048,768]{1,0:T(8,128)(2,1)} %get-tuple-element.86., ...), custom_call_target="tpu_custom_call" | custom-call | flops 4000000000 | tf_op jit(solution)/shard_map/finish/pallas_call | solution.py:1842
  (2 shorter events, 0.1 us)
Async XLA Ops:
  0.6 4.5 %copy-start = (bf16[1,768,192]{1,2,0:T(8,128)(2,1)S(1)}, bf16[1,768,192]{1,2,0:T(8,128)(2,1)}, u32[]{:S(2)}) copy-start(bf16[1,768,192]{1,2,0:T(8,128)(2,1)} %param.31) | copy-start | bytes 884740
  0.7 4.5 %copy-start.1 = (bf16[1,192,768]{2,1,0:T(8,128)(2,1)S(1)}, bf16[1,192,768]{2,1,0:T(8,128)(2,1)}, u32[]{:S(2)}) copy-start(bf16[1,192,768]{2,1,0:T(8,128)(2,1)} %param.29) | copy-start | bytes 884740

commit v7 on v6

--- a/solution.py
+++ b/solution.py
@@ -1040,7 +1040,10 @@
     up = pltpu.make_async_copy(cot_ref.at[me.y, 0, part], cot, lsem.at[4])
     up.start()
     greet([me.mate, me.across_mate] + me.ring + me.group)
-    over = push(in_ref.at[1 - me.y, 0, part], hf.at[ds(ga.own(me.y), half)], yss.at[0], yrs.at[0], me.across)
+    over = [
+        push(ref.at[1 - me.y, 0, part], full.at[ds(ga.own(me.y), half)], yss.at[n], yrs.at[n], me.across)
+        for n, (ref, full) in enumerate(((in_ref, hf), (cot_ref, cf_o)))
+    ]
     wg = WeightGather(me, 0, w_ref, wfull, gat, cfg["groups"], wsems)
     vg = VectorGather(me, sv_ref, vb, vss, vrs, lsem.at[1])
     st = Stores([(hf, hf_o), (n1, n1_o), (n2, n2_o), (g, g_o), (gp, gp_o), (q, q_o), (k, k_o), (v, v_o)], half, ssem)
@@ -1051,7 +1054,7 @@
     vg.wait(0)
     vg.send(1)
     ga.start(0)
-    over.start()
+    over[0].start()
     wg.send_own(0)
     tab_out = pltpu.make_async_copy(tab, tab_o, lsem.at[2])
     tab_out.start()
@@ -1070,7 +1073,7 @@
 
         @pl.when(i == 0)
         def _():
-            over.wait_recv()
+            over[0].wait_recv()
             ga.start(1)
 
         @pl.when(i == 1)
@@ -1080,8 +1083,7 @@
 
     ga.run(norm)
     cot_out.wait()
-    gc.plan(0).start()
-    gc.plan(2).start()
+    gc.start(0)
     wg.ready(0)
 
     def qkv(i, _):
@@ -1105,6 +1107,7 @@
         @pl.when(i == 5)
         def _():
             wg.forward(3)
+            over[1].start()
 
         return 0
 
@@ -1118,11 +1121,15 @@
     wg.ready(3)
     w_out = pltpu.make_async_copy(wfull, w_o, lsem.at[3])
     w_out.start()
+    over[1].wait_recv()
+    gc.start(1)
+    for n in (3, 6, 7):
+        gc.step(n)
     wg.finish()
     vg.finish()
-    for n in (0, 2, 4):
-        gc.plan(n).wait_send()
-    over.wait_send()
+    gc.finish()
+    for c in over:
+        c.wait_send()
     w_out.wait()
 
 
@@ -1145,7 +1152,7 @@
             wide, wide, wide, wide_h, wide_h, pltpu.VMEM((seq, 256), F32), wide_q, wide_q, wide_q,
             weights, weights, pltpu.VMEM((2, tensor, dp) + sv.shape, F32),
             pltpu.VMEM((seq // 8, model), BF),
-            DMA((6,)), DMA((6,)), DMA((6,)), DMA((6,)), DMA((1,)), DMA((1,)), DMA((6,)), DMA((8, 8)),
+            DMA((6,)), DMA((6,)), DMA((6,)), DMA((6,)), DMA((2,)), DMA((2,)), DMA((6,)), DMA((8, 8)),
             DMA((nv,)), DMA((nv,)),
         ]
         + WeightGather.scratch(dp, 4),
@@ -1156,10 +1163,10 @@
 
 
 def mid_kernel(
-    cfg, q_in, k_in, v_in, srow, kcol, g_in, x_in, cot_ref, w_ref, w0, vecs, tab_in,
-    o_o, lse, hf_o, n1_o, n2_o, g_o, gp_o, w_o, q_o, k_o, v_o, cy,
+    cfg, q_in, k_in, v_in, srow, kcol, g_in, x_in, w_ref, w0, vecs, tab_in,
+    o_o, lse, hf_o, n1_o, n2_o, g_o, gp_o, w_o, q_o, k_o, v_o,
     wout, wfc2, hf, n1, n2, g, gp, tab, wfull, gat, q, k, v, o, vt, s_scr,
-    part, mr, xr, sss, srs, gss, grs, lsem, ssem, osem, yss, yrs, *wsems,
+    part, mr, xr, sss, srs, gss, grs, lsem, ssem, osem, *wsems,
 ):
     col, heads = cfg["col"], cfg["heads"]
     me = Mesh(cfg["dp"], cfg["tensor"])
@@ -1181,7 +1188,6 @@
     )
     greet([me.mate, me.beside, me.across, me.across_mate] + me.ring)
     wg = WeightGather(me, 1, w_ref, wfull, gat, cfg["groups"], wsems)
-    over = push(cot_ref.at[1 - me.y, 0, ds(me.s * half, half)], cy, yss.at[0], yrs.at[0], me.across)
     wg.send_ring()
     for n in range(4):
         wg.send_own(n)
@@ -1241,7 +1247,6 @@
         @pl.when(i == 7)
         def _():
             wg.forward(3)
-            over.start()
 
     ga.run(work)
 
@@ -1258,20 +1263,18 @@
     sc.finish()
     wg.finish()
     st_o.finish()
-    over.wait()
     w_out.wait()
 
 
-def layer_mid(cfg, q, k, v, srow, kcol, g, xf, cotangent, w, w0, vecs, tab):
+def layer_mid(cfg, q, k, v, srow, kcol, g, xf, w, w0, vecs, tab):
     seq, model, ff = tab.shape[0], xf.shape[1], cfg["ff"]
     rows, hidden, heads = sds((seq, model), BF), sds((seq, ff), BF), sds((seq, HW), BF)
     wide, wide_h, wide_q = pltpu.VMEM((seq, model), BF), pltpu.VMEM((seq, ff), BF), pltpu.VMEM((seq, HW), BF)
     return pl.pallas_call(
         functools.partial(mid_kernel, cfg),
-        out_shape=(heads, sds((8, seq), F32), rows, rows, rows, hidden, hidden, sds(w0.shape, BF), heads, heads, heads,
-                   sds((seq // 8, model), BF)),
-        in_specs=[ANY, ANY, ANY, VMEM, VMEM, ANY, ANY, ANY, VMEM, ANY, VMEM, ANY],
-        out_specs=(ANY, VMEM) + (ANY,) * 10,
+        out_shape=(heads, sds((8, seq), F32), rows, rows, rows, hidden, hidden, sds(w0.shape, BF), heads, heads, heads),
+        in_specs=[ANY, ANY, ANY, VMEM, VMEM, ANY, ANY, VMEM, ANY, VMEM, ANY],
+        out_specs=(ANY, VMEM) + (ANY,) * 9,
         scratch_shapes=[
             pltpu.VMEM((model, HW), BF), pltpu.VMEM((model, ff), BF),
             wide, wide, wide, wide_h, wide_h, pltpu.VMEM((seq, 256), F32),
@@ -1280,34 +1283,31 @@
             pltpu.VMEM((cfg["heads"], DOC_MAX + QB, QB), F32),
         ]
         + scatter_scratch(seq, model)
-        + [DMA((6,)), DMA((6,)), DMA((9,)), DMA((8, 8)), DMA((1, 8)), DMA((1,)), DMA((1,))]
+        + [DMA((6,)), DMA((6,)), DMA((9,)), DMA((8, 8)), DMA((1, 8))]
         + WeightGather.scratch(cfg["dp"], 4),
         compiler_params=params(3),
         cost_estimate=cost(70),
         name="layer_mid",
-    )(q, k, v, srow, kcol, g, xf, cotangent, w, w0, vecs, tab)
+    )(q, k, v, srow, kcol, g, xf, w, w0, vecs, tab)
 
 
 def turn_kernel(
-    cfg, o_in, g_in, hf_in, cf, cy, w1, vecs, n2_in, gp_in, y_o, do_o, e2_o, gr_o, hx, vg,
+    cfg, o_in, g_in, hf_in, cf, w1, vecs, n2_in, gp_in, y_o, do_o, e2_o, gr_o, hx, vg,
     o, g, hf, dyf, n2, gp, e2, do, y, gr, wout, wfc2, wfc1, da, acc,
-    part, mr, xr, sss, srs, gss, grs, yss, yrs, lsem, ssem,
+    part, mr, xr, sss, srs, yss, yrs, lsem, ssem,
 ):
     col = cfg["col"]
     me = Mesh(cfg["dp"], cfg["tensor"])
     sc = Scatter(me, part, mr, xr, sss, srs)
     half = sc.half
-    gt = Gather(me, dyf, gss, grs, me.y)
-    near = ds(4 * me.y * half, 4 * half)
     loads = load(
         [
-            (cy, dyf.at[ds(gt.own(1 - me.y), half)]),
             (w1.at[:, col["out"] : col["end"]], wout),
             (w1.at[:, col["fc2"] : col["out"]], wfc2),
             (o_in, o),
             (g_in, g),
             (w1.at[:, col["fc1"] : col["fc2"]], wfc1),
-            (cf.at[near], dyf.at[near]),
+            (cf, dyf),
             (gp_in, gp),
             (hf_in, hf),
             (n2_in, n2),
@@ -1315,15 +1315,13 @@
         lsem,
     )
     greet([me.mate, me.beside, me.across])
-    loads[0].wait()
-    gt.start(1)
     h_over = push(hf_in.at[ds(me.py * 2 * half, 2 * half)], hx, yss.at[0], yrs.at[0], me.across)
 
     @pl.when(me.s == 0)
     def _():
         h_over.start()
 
-    for c in loads[1:5]:
+    for c in loads[:4]:
         c.wait()
     vec = vecs.at[1]
     st = Stores([(e2, e2_o), (do, do_o)], half, ssem)
@@ -1331,19 +1329,11 @@
     def early():
         vg[...] = jnp.zeros_like(vg)
         acc[...] = jnp.zeros_like(acc)
-        for c in loads[5:]:
+        for c in loads[4:]:
             c.wait()
 
         def head(i, _):
-            for n, step in ((5, 3), (6, 6), (7, 7)):
-
-                @pl.when(i == n)
-                def _(step=step):
-                    gt.step(step)
-
-            far_b = jnp.where(i < 6, me.x, 1 - me.x)
-            far_h = jnp.where(i % 2 == 0, me.s, 1 - me.s)
-            r0 = jnp.where(i < 4, (4 * me.y + i) * half, gt.start_of(1 - me.y, far_b, far_h))
+            r0 = i * half
             back_head(r0, half, dyf, hf, g, gp, n2, o, wfc1, wfc2, wout, vec, do, e2, da, acc, vg)
             st.start((0, 1), r0, i)
             return 0
@@ -1364,8 +1354,6 @@
     y_out.start()
     sc.finish()
     st.finish()
-    for n in (1, 3, 5):
-        gt.plan(n).wait_send()
 
     @pl.when(me.s == 0)
     def _():
@@ -1375,7 +1363,7 @@
     y_out.wait()
 
 
-def layer_turn(cfg, o, g, hf, cf, cy, w1, vecs, n2, gp):
+def layer_turn(cfg, o, g, hf, cf, w1, vecs, n2, gp):
     seq, model = hf.shape
     ff = cfg["ff"]
     wide, hidden, heads = pltpu.VMEM((seq, model), BF), pltpu.VMEM((seq, ff), BF), pltpu.VMEM((seq, HW), BF)
@@ -1390,7 +1378,7 @@
             sds((seq // 4, model), BF),
             sds((8, model), F32),
         ),
-        in_specs=[ANY] * 6 + [VMEM, ANY, ANY],
+        in_specs=[ANY] * 5 + [VMEM, ANY, ANY],
         out_specs=(ANY,) * 5 + (VMEM,),
         scratch_shapes=[
             heads, hidden, wide, wide, wide, hidden, wide, heads, pltpu.VMEM(owned, BF),
@@ -1399,15 +1387,15 @@
             pltpu.VMEM((seq // 8, ff), BF), pltpu.VMEM((model, 2 * ff + HW), F32),
         ]
         + scatter_scratch(seq, model)
-        + [DMA((6,)), DMA((6,)), DMA((1,)), DMA((1,)), DMA((10,)), DMA((2, 8))],
+        + [DMA((1,)), DMA((1,)), DMA((9,)), DMA((2, 8))],
         compiler_params=params(4),
         cost_estimate=cost(40),
         name="layer_turn",
-    )(o, g, hf, cf, cy, w1, vecs, n2, gp)
+    )(o, g, hf, cf, w1, vecs, n2, gp)
 
 
 def back_kernel(
-    cfg, dm_in, e2_in, cf, cy, hf_in, n1_in, w1, w0, vecs, xf_in, g_in, gp_in, n2_in, o_in, gr1, y_in,
+    cfg, dm_in, e2_in, cf, hf_in, n1_in, w1, w0, vecs, xf_in, g_in, gp_in, n2_in, o_in, gr1, y_in,
     dh_o, e2_o, do_o, vgf, vgd, out1_o, outq_o, gr_o, yx,
     dmix, o, do, a, b, e2, g, gp, wqkv, wout, wfc2, wfc1, dhf, da, acc, gq, gr, got, gotq, acrq,
     sb, rb, sbq, rbq, out1, outq, part, mr, xr, sss, srs, gss, grs, lsem, ssem, oss, ors, osem, *rsems,
@@ -1431,7 +1419,7 @@
             (gp_in, gp),
             (o_in, o),
         ]
-        + [(cf.at[ds(sc.own(me.y), half)], dhf.at[ds(sc.own(me.y), half)]), (cy, dhf.at[ds(sc.own(1 - me.y), half)])],
+        + [(cf.at[ds(sc.own(n), half)], dhf.at[ds(sc.own(n), half)]) for n in range(2)],
         lsem,
     )
     gr_load = pltpu.make_async_copy(gr1, gr, lsem.at[13])
@@ -1524,7 +1512,7 @@
         c.wait()
 
 
-def layer_back(cfg, dmix, e2, cf, cy, hf, n1, w1, w0, vecs, xf, g, gp, n2, o, gr1, y):
+def layer_back(cfg, dmix, e2, cf, hf, n1, w1, w0, vecs, xf, g, gp, n2, o, gr1, y):
     seq, model = hf.shape
     ff, dp = cfg["ff"], cfg["dp"]
     rows, nr, nq = model // dp, 2 * ff + HW, 3 * HW
@@ -1542,7 +1530,7 @@
             sds((model, nr), BF),
             sds((2,) + y.shape, BF),
         ),
-        in_specs=[ANY] * 8 + [VMEM] + [ANY] * 7,
+        in_specs=[ANY] * 7 + [VMEM] + [ANY] * 7,
         out_specs=(ANY, ANY, ANY, VMEM, VMEM, ANY, ANY, ANY, ANY),
         scratch_shapes=[
             pltpu.VMEM((seq, nq), BF), heads, heads, wide, wide, wide, hidden, hidden,
@@ -1560,7 +1548,7 @@
         compiler_params=params(5),
         cost_estimate=cost(70),
         name="layer_back",
-    )(dmix, e2, cf, cy, hf, n1, w1, w0, vecs, xf, g, gp, n2, o, gr1, y)
+    )(dmix, e2, cf, hf, n1, w1, w0, vecs, xf, g, gp, n2, o, gr1, y)
 
 
 def last_kernel(
@@ -1892,14 +1880,12 @@
     xf, n1a, n2a, ga, gpa, tab, w0, qa, ka, va, cf, vecs, sr, kc = layer_in(
         cfg, inputs, cotangent, segments, live_blocks, w, sv, fr
     )
-    oa, lsea, hf, n1b, n2b, gb, gpb, w1, qb, kb, vb, cy = layer_mid(
-        cfg, qa, ka, va, sr, kc, ga, xf, cotangent, w, w0, vecs, tab
-    )
+    oa, lsea, hf, n1b, n2b, gb, gpb, w1, qb, kb, vb = layer_mid(cfg, qa, ka, va, sr, kc, ga, xf, w, w0, vecs, tab)
     ob, lseb = attn_fwd(heads, segments, live_blocks, qb, kb, vb, sr, kc)
-    y, dob, e2b, grb, hx, vdb = layer_turn(cfg, ob, gb, hf, cf, cy, w1, vecs, n2b, gpb)
+    y, dob, e2b, grb, hx, vdb = layer_turn(cfg, ob, gb, hf, cf, w1, vecs, n2b, gpb)
     dmb = attn_bwd(heads, segments, live_blocks, qb, kb, vb, ob, dob, lseb, sr, kc, tab)
     dhf, e2a, doa, vfb, vda, out1, outq, gra, yx = layer_back(
-        cfg, dmb, e2b, cf, cy, hf, n1b, w1, w0, vecs, xf, ga, gpa, n2a, oa, grb, y
+        cfg, dmb, e2b, cf, hf, n1b, w1, w0, vecs, xf, ga, gpa, n2a, oa, grb, y
     )
     dhx, dxx, fq, fr_, gv = layer_last(
         cfg, qa, ka, va, oa, doa, lsea, sr, kc, tab, e2a, dhf, xf, n1a, w0, vecs, vfb, vdb, vda, gra, out1, outq

time: 398 us -> 401 us (level)
    pallas_call x1, Pallas kernels: 66.1 us -> 87.8 us  [layer_in(): pl.pallas_call(functools.partial(in_kernel, cfg), out_shape=(rows, rows,...]
    pallas_call x1, Pallas kernels: 71.7 us -> 60.8 us  [layer_mid(): pl.pallas_call(functools.partial(mid_kernel, cfg), out_shape=(heads, sds(...]
    pallas_call x1, Pallas kernels: 58.9 us -> 52.3 us  [layer_back(): pl.pallas_call(functools.partial(back_kernel, cfg), out_shape=(sds((seq,...]
where the time goes in v7:
time: 401 us; the launch traced here: 400 us
  Pallas kernels  394 us (98%)
    pallas_call x1, Pallas kernels, layer_last(): pl.pallas_call(functools.partial(last_kernel, cfg), out_shape=(sds((seq /...  102 us
    pallas_call x1, Pallas kernels, layer_in(): pl.pallas_call(functools.partial(in_kernel, cfg), out_shape=(rows, rows,...  87.8 us
    pallas_call x1, Pallas kernels, layer_mid(): pl.pallas_call(functools.partial(mid_kernel, cfg), out_shape=(heads, sds(...  60.8 us
    pallas_call x1, Pallas kernels, layer_back(): pl.pallas_call(functools.partial(back_kernel, cfg), out_shape=(sds((seq,...  52.3 us
    pallas_call x1, Pallas kernels, attn_bwd(): pl.pallas_call(functools.partial(attn_bwd_kernel, heads), out_shape=sds((...  33.9 us
    pallas_call x1, Pallas kernels, layer_turn(): pl.pallas_call(functools.partial(turn_kernel, cfg), out_shape=(sds(owned,...  33.3 us
    pallas_call x1, Pallas kernels, attn_fwd(): pl.pallas_call(functools.partial(attn_fwd_kernel, heads), out_shape=(sds(...  17.9 us

profile of v7, /device:TPU:0, one launch (start us, length us, event | category | flops | bytes accessed | tf_op | source)
XLA Modules:
  0.0 400.2 jit_solution(13320896047412910841)
XLA Ops:
  0.6 0.0 copy-start
  0.7 0.0 copy-start.1
  0.7 0.8 stack.3
  1.5 0.7 fusion.7
  2.2 0.6 pad_convert_fusion.sv_ref
  2.8 1.0 copy.36
  3.8 1.1 copy.33
  5.0 0.2 copy.37
  5.1 0.0 copy-done
  5.2 0.0 copy-done.1
  5.2 1.0 fusion.1.w_ref
  6.2 87.8 %layer_in.1 = (bf16[2048,768]{1,0:T(8,128)(2,1)}, bf16[2048,768]{1,0:T(8,128)(2,1)}, bf16[2048,768]{1,0:T(8,128)(2,1)}, bf16[2048,768]{1,0:T(8,128)(2,1)}, bf16[...) custom-call(bf16[2,1,512,768]{3,2,1,0:T(8,128)(2,1)} %in_ref.1, ...), custom_call_target="tpu_custom_call" | custom-call | flops 35999997952 | tf_op jit(solution)/shard_map/layer_in/pallas_call | solution.py:1144
  94.0 60.8 %layer_mid.1 = (bf16[2048,256]{1,0:T(8,128)(2,1)}, f32[8,2048]{1,0:T(8,128)}, bf16[2048,768]{1,0:T(8,128)(2,1)}, bf16[2048,768]{1,0:T(8,128)(2,1)}, bf16[2048,76...) custom-call(bf16[2048,256]{1,0:T(8,128)(2,1)} %get-tuple-element.75., ...), custom_call_target="tpu_custom_call" | custom-call | flops 56000000000 | tf_op jit(solution)/shard_map/layer_mid/pallas_call | solution.py:1273
  154.8 17.9 %attn_fwd.1 = (bf16[2048,256]{1,0:T(8,128)(2,1)}, f32[8,2048]{1,0:T(8,128)}) custom-call(s32[2,1,2048]{2,1,0:T(1,128)} %seg.3, s32[1,2]{1,0:T(1,128)} %bitcast.29, bf16[2048,256]{1,0:T(8,128)(2,1)} %get-tuple-element.86.q_in, bf16[2048,256]{1,0:T(8,128)(2,1)} %get-tuple-element.87.k_in, bf16[2048,256]{1,0:T(8,128)(2,1)} %get-tuple-element.88.v_in, ...), custom_call_target="tpu_custom_call" | custom-call | flops 9600000000 | tf_op jit(solution)/shard_map/attn_fwd/pallas_call | solution.py:159
  172.7 33.3 %layer_turn.1 = (bf16[2,256,768]{2,1,0:T(8,128)(2,1)}, bf16[2048,256]{1,0:T(8,128)(2,1)}, bf16[2048,768]{1,0:T(8,128)(2,1)}, bf16[768,1792]{1,0:T(8,128)(2,1)}, ...) custom-call(bf16[2048,256]{1,0:T(8,128)(2,1)} %get-tuple-element.89.o_in, bf16[2048,768]{1,0:T(8,128)(2,1)} %get-tuple-element.90.g_in, ...), custom_call_target="tpu_custom_call" | custom-call | flops 32000000000 | tf_op jit(solution)/shard_map/layer_turn/pallas_call | solution.py:1371
  206.0 33.9 %attn_bwd.1.dm_in = bf16[2048,768]{1,0:T(8,128)(2,1)} custom-call(s32[2,1,2048]{2,1,0:T(1,128)} %seg.3, s32[1,2]{1,0:T(1,128)} %bitcast.30, bf16[2048,256]{1,0:T(8,128)(2,1)} %get-tuple-element.86.q_in, bf16[2048,256]{1,0:T(8,128)(2,1)} %get-tuple-element.87.k_in, bf16[2048,256]{1,0:T(8,128)(2,1)} %get-tuple-element.88.v_in, ...), custom_call_target="tpu_custom_call" | custom-call | flops 20800000000 | tf_op jit(solution)/shard_map/attn_bwd/pallas_call | solution.py:270
  239.9 52.3 %layer_back.1 = (bf16[2048,768]{1,0:T(8,128)(2,1)}, bf16[2048,768]{1,0:T(8,128)(2,1)}, bf16[2048,256]{1,0:T(8,128)(2,1)}, f32[8,768]{1,0:T(8,128)}, f32[8,768]{1...) custom-call(bf16[2048,768]{1,0:T(8,128)(2,1)} %attn_bwd.1.dm_in, ...), custom_call_target="tpu_custom_call" | custom-call | flops 56000000000 | tf_op jit(solution)/shard_map/layer_back/pallas_call | solution.py:1520
  292.2 101.7 %layer_last.1 = (bf16[512,768]{1,0:T(8,128)(2,1)}, bf16[2,2,256,768]{3,2,1,0:T(8,128)(2,1)}, f32[192,768]{1,0:T(8,128)}, f32[192,1792]{1,0:T(8,128)}, f32[8,768]{1,0:T(8,128)}) custom-call(bf16[2048,256]{1,0:T(8,128)(2,1)} %get-tuple-element.75.q_in, bf16[2048,256]{1,0:T(8,128)(2,1)} %get-tuple-element.76.k_in, bf16[2048,256]{1,0:T(8,128)(2,1)} %get-tuple-element.77.v_in, ...), custom_call_target="tpu_custom_call" | custom-call | flops 64000000000 | tf_op jit(solution)/shard_map/layer_last/pallas_call | solution.py:1727
  393.9 6.1 %finish.1 = (bf16[1,2,1,512,768]{4,3,2,1,0:T(8,128)(2,1)}, bf16[1,2,1,512,768]{4,3,2,1,0:T(8,128)(2,1)}, f32[1,48]{1,0:T(1,128)}, f32[1,48]{1,0:T(1,128)}, f32[1...) custom-call(bf16[2048,768]{1,0:T(8,128)(2,1)} %get-tuple-element.85., ...), custom_call_target="tpu_custom_call" | custom-call | flops 4000000000 | tf_op jit(solution)/shard_map/finish/pallas_call | solution.py:1830
  (2 shorter events, 0.1 us)
Async XLA Ops:
  0.6 4.5 %copy-start = (bf16[1,768,192]{1,2,0:T(8,128)(2,1)S(1)}, bf16[1,768,192]{1,2,0:T(8,128)(2,1)}, u32[]{:S(2)}) copy-start(bf16[1,768,192]{1,2,0:T(8,128)(2,1)} %param.31) | copy-start | bytes 884740
  0.7 4.5 %copy-start.1 = (bf16[1,192,768]{2,1,0:T(8,128)(2,1)S(1)}, bf16[1,192,768]{2,1,0:T(8,128)(2,1)}, u32[]{:S(2)}) copy-start(bf16[1,192,768]{2,1,0:T(8,128)(2,1)} %param.29) | copy-start | bytes 884740

commit v8 on v4

--- a/solution.py
+++ b/solution.py
@@ -1547,13 +1547,6 @@
     def whole(n):
         return full_out(hf_in, so, 0) if n == 0 else full_out(dh_in, ig, 0)
 
-    for n in range(2):
-
-        @pl.when(me.s == n)
-        def _(n=n):
-            for c in whole(n):
-                c.start()
-
     def start_here(src, dst, core, i):
         across, local, mate = owned_out(src, dst, core, i)
 
@@ -1580,8 +1573,6 @@
         def _():
             mate.wait_send()
 
-    owned_out(y_in, so, 1, 1)[0].start()
-    start_here(y_in, so, 1, 1)
     old = [pltpu.make_async_copy(out1, fr, lsem.at[15]), pltpu.make_async_copy(outq, fq, lsem.at[16])]
 
     @pl.when(me.s == 1)
@@ -1605,6 +1596,19 @@
 
     def qloop(i, _):
         lo = jnp.maximum(i - DOC_MAX // QB, 0)
+
+        @pl.when(i == n_blocks - 2)
+        def _():
+            for n in range(2):
+
+                @pl.when(me.s == n)
+                def _(n=n):
+                    for c in whole(n):
+                        c.start()
+
+            owned_out(y_in, so, 1, 1)[0].start()
+            start_here(y_in, so, 1, 1)
+
         attn_bwd_block(i, lo, i, heads, q, k, v, o, do, kt, lse, srow, kcol, tab, dk, dv, dmix)
         for at_block, steps in (
             (n_blocks // 2 - 1, range(0, 1)),

time: 395 us -> 390 us (0.987); the launches traced: 396 us -> 386 us
  Pallas kernels: 390 us -> 379 us
    pallas_call x1, Pallas kernels: 107 us -> 102 us  [layer_last(): pl.pallas_call(functools.partial(last_kernel, cfg), out_shape=(both, both...]
    pallas_call x1, Pallas kernels: 38.4 us -> 33.9 us  [attn_bwd(): pl.pallas_call(functools.partial(attn_bwd_kernel, heads), out_shape=sds((...]
where the time goes in v8:
time: 390 us; the launch traced here: 386 us
  Pallas kernels  379 us (97%)
    pallas_call x1, Pallas kernels, layer_last(): pl.pallas_call(functools.partial(last_kernel, cfg), out_shape=(both, both...  102 us
    pallas_call x1, Pallas kernels, layer_in(): pl.pallas_call(functools.partial(in_kernel, cfg), out_shape=(rows, rows,...  78.6 us
    pallas_call x1, Pallas kernels, layer_mid(): pl.pallas_call(functools.partial(mid_kernel, cfg), out_shape=(heads, sds(...  59.1 us
    pallas_call x1, Pallas kernels, layer_back(): pl.pallas_call(functools.partial(back_kernel, cfg), out_shape=(sds((seq,...  52.7 us
    pallas_call x1, Pallas kernels, attn_bwd(): pl.pallas_call(functools.partial(attn_bwd_kernel, heads), out_shape=sds((...  33.9 us
    pallas_call x1, Pallas kernels, layer_turn(): pl.pallas_call(functools.partial(turn_kernel, cfg), out_shape=(sds(owned,...  29 us
    pallas_call x1, Pallas kernels, attn_fwd(): pl.pallas_call(functools.partial(attn_fwd_kernel, heads), out_shape=(sds(...  18 us

profile of v8, /device:TPU:0, one launch (start us, length us, event | category | flops | bytes accessed | tf_op | source)
XLA Modules:
  0.0 385.6 jit_solution(18071512189981488199)
XLA Ops:
  0.6 0.0 copy-start
  0.7 0.0 copy-start.1
  0.7 0.8 stack.3
  1.5 0.7 fusion.7
  2.2 0.6 pad_convert_fusion.sv_ref
  2.8 1.0 copy.36
  3.8 1.1 copy.33
  5.0 0.2 copy.37
  5.1 0.0 copy-done
  5.2 0.0 copy-done.1
  5.2 1.0 fusion.1.w_ref
  6.2 78.6 %layer_in.1 = (bf16[2048,768]{1,0:T(8,128)(2,1)}, bf16[2048,768]{1,0:T(8,128)(2,1)}, bf16[2048,768]{1,0:T(8,128)(2,1)}, bf16[2048,768]{1,0:T(8,128)(2,1)}, bf16[...) custom-call(bf16[2,1,512,768]{3,2,1,0:T(8,128)(2,1)} %in_ref.1, ...), custom_call_target="tpu_custom_call" | custom-call | flops 35999997952 | tf_op jit(solution)/shard_map/layer_in/pallas_call | solution.py:1097
  84.8 59.1 %layer_mid.1 = (bf16[2048,256]{1,0:T(8,128)(2,1)}, f32[8,2048]{1,0:T(8,128)}, bf16[2048,768]{1,0:T(8,128)(2,1)}, bf16[2048,768]{1,0:T(8,128)(2,1)}, bf16[2048,76...) custom-call(bf16[2048,256]{1,0:T(8,128)(2,1)} %get-tuple-element.73., ...), custom_call_target="tpu_custom_call" | custom-call | flops 56000000000 | tf_op jit(solution)/shard_map/layer_mid/pallas_call | solution.py:1221
  143.9 18.0 %attn_fwd.1 = (bf16[2048,256]{1,0:T(8,128)(2,1)}, f32[8,2048]{1,0:T(8,128)}) custom-call(s32[2,1,2048]{2,1,0:T(1,128)} %seg.3, s32[1,2]{1,0:T(1,128)} %bitcast.29, bf16[2048,256]{1,0:T(8,128)(2,1)} %get-tuple-element.84.q_in, bf16[2048,256]{1,0:T(8,128)(2,1)} %get-tuple-element.85.k_in, bf16[2048,256]{1,0:T(8,128)(2,1)} %get-tuple-element.86.v_in, ...), custom_call_target="tpu_custom_call" | custom-call | flops 9600000000 | tf_op jit(solution)/shard_map/attn_fwd/pallas_call | solution.py:159
  161.9 29.0 %layer_turn.1 = (bf16[2,256,768]{2,1,0:T(8,128)(2,1)}, bf16[2048,256]{1,0:T(8,128)(2,1)}, bf16[2048,768]{1,0:T(8,128)(2,1)}, bf16[768,1792]{1,0:T(8,128)(2,1)}, f32[8,768]{1,0:T(8,128)}) custom-call(bf16[2048,256]{1,0:T(8,128)(2,1)} %get-tuple-element.87.o_in, bf16[2048,768]{1,0:T(8,128)(2,1)} %get-tuple-element.88.g_in, ...), custom_call_target="tpu_custom_call" | custom-call | flops 32000000000 | tf_op jit(solution)/shard_map/layer_turn/pallas_call | solution.py:1308
  190.9 33.9 %attn_bwd.1.dm_in = bf16[2048,768]{1,0:T(8,128)(2,1)} custom-call(s32[2,1,2048]{2,1,0:T(1,128)} %seg.3, s32[1,2]{1,0:T(1,128)} %bitcast.30, bf16[2048,256]{1,0:T(8,128)(2,1)} %get-tuple-element.84.q_in, bf16[2048,256]{1,0:T(8,128)(2,1)} %get-tuple-element.85.k_in, bf16[2048,256]{1,0:T(8,128)(2,1)} %get-tuple-element.86.v_in, ...), custom_call_target="tpu_custom_call" | custom-call | flops 20800000000 | tf_op jit(solution)/shard_map/attn_bwd/pallas_call | solution.py:270
  224.7 52.7 %layer_back.1 = (bf16[2048,768]{1,0:T(8,128)(2,1)}, bf16[2048,768]{1,0:T(8,128)(2,1)}, bf16[2048,256]{1,0:T(8,128)(2,1)}, f32[8,768]{1,0:T(8,128)}, f32[8,768]{1...) custom-call(bf16[2048,768]{1,0:T(8,128)(2,1)} %attn_bwd.1.dm_in, ...), custom_call_target="tpu_custom_call" | custom-call | flops 56000000000 | tf_op jit(solution)/shard_map/layer_back/pallas_call | solution.py:1453
  277.5 101.8 %layer_last.1 = (bf16[1,2,1,512,768]{4,3,2,1,0:T(8,128)(2,1)}, bf16[1,2,1,512,768]{4,3,2,1,0:T(8,128)(2,1)}, f32[192,768]{1,0:T(8,128)}, f32[192,1792]{1,0:T(8,128)}, f32[8,768]{1,0:T(8,128)}) custom-call(bf16[2048,256]{1,0:T(8,128)(2,1)} %get-tuple-element.73.q_in, bf16[2048,256]{1,0:T(8,128)(2,1)} %get-tuple-element.74.k_in, ...), custom_call_target="tpu_custom_call" | custom-call | flops 64000000000 | tf_op jit(solution)/shard_map/layer_last/pallas_call | solution.py:1717
  379.2 6.2 %finish.1 = (bf16[1,2,1,512,768]{4,3,2,1,0:T(8,128)(2,1)}, bf16[1,2,1,512,768]{4,3,2,1,0:T(8,128)(2,1)}, f32[1,48]{1,0:T(1,128)}, f32[1,48]{1,0:T(1,128)}, f32[1...) custom-call(bf16[1,2,1,512,768]{4,3,2,1,0:T(8,128)(2,1)} %get-tuple-, ...), custom_call_target="tpu_custom_call" | custom-call | flops 4000000000 | tf_op jit(solution)/shard_map/finish/pallas_call | solution.py:1781
  (2 shorter events, 0.1 us)
Async XLA Ops:
  0.6 4.5 %copy-start = (bf16[1,768,192]{1,2,0:T(8,128)(2,1)S(1)}, bf16[1,768,192]{1,2,0:T(8,128)(2,1)}, u32[]{:S(2)}) copy-start(bf16[1,768,192]{1,2,0:T(8,128)(2,1)} %param.31) | copy-start | bytes 884740
  0.7 4.5 %copy-start.1 = (bf16[1,192,768]{2,1,0:T(8,128)(2,1)S(1)}, bf16[1,192,768]{2,1,0:T(8,128)(2,1)}, u32[]{:S(2)}) copy-start(bf16[1,192,768]{2,1,0:T(8,128)(2,1)} %param.29) | copy-start | bytes 884740

commit v9 on v8

--- a/solution.py
+++ b/solution.py
@@ -1157,7 +1157,7 @@
         st_o.start((0,), r0, i)
         branch_out(r0, half, o, g, wout, wfc2, part)
 
-        @pl.when(i == 6)
+        @pl.when(i == 5)
         def _():
             wg.forward(0)
 
@@ -1746,7 +1746,7 @@
 ):
     heads, ff, own, qw, fw = cfg["heads"], cfg["ff"], cfg["own"], cfg["qw"], cfg["fw"]
     me = Mesh(cfg["dp"], cfg["tensor"])
-    loads = load([(fr_in, fr), (fq_in, fq), (so_in, a), (ig_in, b)], lsem)
+    loads = load([(so_in, a), (ig_in, b), (fr_in, fr), (fq_in, fq)], lsem)
     model = vec.shape[1]
     short = pltpu.roll(vec[...], (model - (me.z * me.tensor + me.t) * own) % model, 1)
     for row, ref in ((0, bg1), (1, bb1), (2, bdy), (2, bdy2), (3, bg2), (4, bb2)):
@@ -1760,15 +1760,15 @@
         one = jnp.broadcast_to(vec[7:8, h * wide : (h + 1) * wide], (8, wide))
         bfc1[h] = pltpu.roll(one, (wide - me.z * fw) % wide, 1)[0:1, 0:fw]
     loads[0].wait()
+    loads[1].wait()
+    outs = [pltpu.make_async_copy(a, so, osem.at[0]), pltpu.make_async_copy(b, ig, osem.at[1])]
+    for c in outs:
+        c.start()
+    loads[2].wait()
     gfc1[0] = fr[:, 0:ff]
     gfc2[...] = fr[:, ff : 2 * ff]
     gout[0] = fr[:, 2 * ff : 2 * ff + HW].T[0 : heads * HD, :]
-    loads[2].wait()
     loads[3].wait()
-    outs = [pltpu.make_async_copy(a, so, osem.at[0]), pltpu.make_async_copy(b, ig, osem.at[1])]
-    for c in outs:
-        c.start()
-    loads[1].wait()
     pieces = [fq[:, p * HW + h * HD : p * HW + (h + 1) * HD] for h in range(heads) for p in range(3)]
     gqkv[0] = jnp.concatenate(pieces, axis=1)
     for c in outs:

time: 390 us -> 389 us (level); the launches traced: 386 us -> 390 us
  Pallas kernels: 379 us -> 383 us
    pallas_call x1, Pallas kernels: 52.7 us -> 61.9 us  [layer_back(): pl.pallas_call(functools.partial(back_kernel, cfg), out_shape=(sds((seq,...]
where the time goes in v9:
time: 389 us; the launch traced here: 390 us
  Pallas kernels  383 us (98%)
    pallas_call x1, Pallas kernels, layer_last(): pl.pallas_call(functools.partial(last_kernel, cfg), out_shape=(both, both...  102 us
    pallas_call x1, Pallas kernels, layer_in(): pl.pallas_call(functools.partial(in_kernel, cfg), out_shape=(rows, rows,...  78.6 us
    pallas_call x1, Pallas kernels, layer_back(): pl.pallas_call(functools.partial(back_kernel, cfg), out_shape=(sds((seq,...  61.9 us
    pallas_call x1, Pallas kernels, layer_mid(): pl.pallas_call(functools.partial(mid_kernel, cfg), out_shape=(heads, sds(...  59.1 us
    pallas_call x1, Pallas kernels, attn_bwd(): pl.pallas_call(functools.partial(attn_bwd_kernel, heads), out_shape=sds((...  31.6 us
    pallas_call x1, Pallas kernels, layer_turn(): pl.pallas_call(functools.partial(turn_kernel, cfg), out_shape=(sds(owned,...  27.8 us
    pallas_call x1, Pallas kernels, attn_fwd(): pl.pallas_call(functools.partial(attn_fwd_kernel, heads), out_shape=(sds(...  16.8 us

profile of v9, /device:TPU:0, one launch (start us, length us, event | category | flops | bytes accessed | tf_op | source)
XLA Modules:
  0.0 389.8 jit_solution(8285078449310868913)
XLA Ops:
  0.6 0.0 copy-start
  0.7 0.0 copy-start.1
  0.7 0.8 stack.3
  1.5 0.7 fusion.7
  2.2 0.6 pad_convert_fusion.sv_ref
  2.8 1.0 copy.36
  3.8 1.1 copy.33
  5.0 0.2 copy.37
  5.1 0.0 copy-done
  5.2 0.0 copy-done.1
  5.2 1.0 fusion.1.w_ref
  6.2 78.6 %layer_in.1 = (bf16[2048,768]{1,0:T(8,128)(2,1)}, bf16[2048,768]{1,0:T(8,128)(2,1)}, bf16[2048,768]{1,0:T(8,128)(2,1)}, bf16[2048,768]{1,0:T(8,128)(2,1)}, bf16[...) custom-call(bf16[2,1,512,768]{3,2,1,0:T(8,128)(2,1)} %in_ref.1, ...), custom_call_target="tpu_custom_call" | custom-call | flops 35999997952 | tf_op jit(solution)/shard_map/layer_in/pallas_call | solution.py:1097
  84.8 59.1 %layer_mid.1 = (bf16[2048,256]{1,0:T(8,128)(2,1)}, f32[8,2048]{1,0:T(8,128)}, bf16[2048,768]{1,0:T(8,128)(2,1)}, bf16[2048,768]{1,0:T(8,128)(2,1)}, bf16[2048,76...) custom-call(bf16[2048,256]{1,0:T(8,128)(2,1)} %get-tuple-element.73., ...), custom_call_target="tpu_custom_call" | custom-call | flops 56000000000 | tf_op jit(solution)/shard_map/layer_mid/pallas_call | solution.py:1221
  143.9 16.8 %attn_fwd.1 = (bf16[2048,256]{1,0:T(8,128)(2,1)}, f32[8,2048]{1,0:T(8,128)}) custom-call(s32[2,1,2048]{2,1,0:T(1,128)} %seg.3, s32[1,2]{1,0:T(1,128)} %bitcast.29, bf16[2048,256]{1,0:T(8,128)(2,1)} %get-tuple-element.84.q_in, bf16[2048,256]{1,0:T(8,128)(2,1)} %get-tuple-element.85.k_in, bf16[2048,256]{1,0:T(8,128)(2,1)} %get-tuple-element.86.v_in, ...), custom_call_target="tpu_custom_call" | custom-call | flops 9600000000 | tf_op jit(solution)/shard_map/attn_fwd/pallas_call | solution.py:159
  160.8 27.8 %layer_turn.1 = (bf16[2,256,768]{2,1,0:T(8,128)(2,1)}, bf16[2048,256]{1,0:T(8,128)(2,1)}, bf16[2048,768]{1,0:T(8,128)(2,1)}, bf16[768,1792]{1,0:T(8,128)(2,1)}, f32[8,768]{1,0:T(8,128)}) custom-call(bf16[2048,256]{1,0:T(8,128)(2,1)} %get-tuple-element.87.o_in, bf16[2048,768]{1,0:T(8,128)(2,1)} %get-tuple-element.88.g_in, ...), custom_call_target="tpu_custom_call" | custom-call | flops 32000000000 | tf_op jit(solution)/shard_map/layer_turn/pallas_call | solution.py:1308
  188.5 31.6 %attn_bwd.1.dm_in = bf16[2048,768]{1,0:T(8,128)(2,1)} custom-call(s32[2,1,2048]{2,1,0:T(1,128)} %seg.3, s32[1,2]{1,0:T(1,128)} %bitcast.30, bf16[2048,256]{1,0:T(8,128)(2,1)} %get-tuple-element.84.q_in, bf16[2048,256]{1,0:T(8,128)(2,1)} %get-tuple-element.85.k_in, bf16[2048,256]{1,0:T(8,128)(2,1)} %get-tuple-element.86.v_in, ...), custom_call_target="tpu_custom_call" | custom-call | flops 20800000000 | tf_op jit(solution)/shard_map/attn_bwd/pallas_call | solution.py:270
  220.1 61.9 %layer_back.1 = (bf16[2048,768]{1,0:T(8,128)(2,1)}, bf16[2048,768]{1,0:T(8,128)(2,1)}, bf16[2048,256]{1,0:T(8,128)(2,1)}, f32[8,768]{1,0:T(8,128)}, f32[8,768]{1...) custom-call(bf16[2048,768]{1,0:T(8,128)(2,1)} %attn_bwd.1.dm_in, ...), custom_call_target="tpu_custom_call" | custom-call | flops 56000000000 | tf_op jit(solution)/shard_map/layer_back/pallas_call | solution.py:1453
  282.0 102.0 %layer_last.1 = (bf16[1,2,1,512,768]{4,3,2,1,0:T(8,128)(2,1)}, bf16[1,2,1,512,768]{4,3,2,1,0:T(8,128)(2,1)}, f32[192,768]{1,0:T(8,128)}, f32[192,1792]{1,0:T(8,128)}, f32[8,768]{1,0:T(8,128)}) custom-call(bf16[2048,256]{1,0:T(8,128)(2,1)} %get-tuple-element.73.q_in, bf16[2048,256]{1,0:T(8,128)(2,1)} %get-tuple-element.74.k_in, ...), custom_call_target="tpu_custom_call" | custom-call | flops 64000000000 | tf_op jit(solution)/shard_map/layer_last/pallas_call | solution.py:1717
  384.0 5.6 %finish.1 = (bf16[1,2,1,512,768]{4,3,2,1,0:T(8,128)(2,1)}, bf16[1,2,1,512,768]{4,3,2,1,0:T(8,128)(2,1)}, f32[1,48]{1,0:T(1,128)}, f32[1,48]{1,0:T(1,128)}, f32[1...) custom-call(bf16[1,2,1,512,768]{4,3,2,1,0:T(8,128)(2,1)} %get-tuple-, ...), custom_call_target="tpu_custom_call" | custom-call | flops 4000000000 | tf_op jit(solution)/shard_map/finish/pallas_call | solution.py:1781
  (2 shorter events, 0.1 us)
Async XLA Ops:
  0.6 4.5 %copy-start = (bf16[1,768,192]{1,2,0:T(8,128)(2,1)S(1)}, bf16[1,768,192]{1,2,0:T(8,128)(2,1)}, u32[]{:S(2)}) copy-start(bf16[1,768,192]{1,2,0:T(8,128)(2,1)} %param.31) | copy-start | bytes 884740
  0.7 4.5 %copy-start.1 = (bf16[1,192,768]{2,1,0:T(8,128)(2,1)S(1)}, bf16[1,192,768]{2,1,0:T(8,128)(2,1)}, u32[]{:S(2)}) copy-start(bf16[1,192,768]{2,1,0:T(8,128)(2,1)} %param.29) | copy-start | bytes 884740
